TPU v7x, 32 devices: a whole 2x2x4 slice. The times are simulated.
32 devices in a mesh: fsdp: 32 (over z, y, x, core).
Axes of the slice: x: 2, y: 2, z: 4, core: 2. Of those that a mesh axis runs over, the one named last changes fastest.
Arguments:
- x_in: bfloat16 [32, 1024, 1536], P('fsdp')
- ln1_w: float32 [1536], P('fsdp')
- w_qkv: bfloat16 [1536, 3, 12, 128], P('fsdp')
- w_out: bfloat16 [1536, 1536], P('fsdp')
- ln2_w: float32 [1536], P('fsdp')
- w_up: bfloat16 [1536, 6144], P('fsdp')
- w_down: bfloat16 [6144, 1536], P('fsdp')
- dy_out: bfloat16 [32, 1024, 1536], P('fsdp')
Outputs:
- output 1: bfloat16 [32, 1024, 1536], P('fsdp')
- output 2: bfloat16 [32, 1024, 1536], P('fsdp')
- output 3: float32 [1536], P('fsdp')
- output 4: float32 [1536, 3, 12, 128], P('fsdp')
- output 5: float32 [1536, 1536], P('fsdp')
- output 6: float32 [1536], P('fsdp')
- output 7: float32 [1536, 6144], P('fsdp')
- output 8: float32 [6144, 1536], P('fsdp')
All inputs are finite; a program needn't handle non-finite values.
Results may differ from a plain program's by a relative error of at most 0.018174.
Values are sent between devices in bfloat16 or wider.
A program may use at most 1 GiB of HBM per device.

v0:
```python
import math
import jax
import jax.numpy as jnp
from jax import lax
from jax.sharding import PartitionSpec as P

EPS = 1e-5


def alibi_slopes(n_heads):
    padded = 2 ** math.ceil(math.log2(n_heads))
    base_list = [2.0 ** (-8.0 * (k + 1) / padded) for k in range(padded)]
    ordered = base_list if padded == n_heads else base_list[1::2] + base_list[0::2]
    return jnp.array(ordered[:n_heads], dtype=jnp.float32)


def layer_norm(x_rows, ln_gain):
    row_mean = jnp.mean(x_rows, axis=-1, keepdims=True)
    centered = x_rows - row_mean
    row_var = jnp.mean(centered * centered, axis=-1, keepdims=True)
    return centered * lax.rsqrt(row_var + EPS) * ln_gain


def gelu_exact(pre_act):
    return jax.nn.gelu(pre_act, approximate=False)


def matmul(form, left, right):
    return jnp.einsum(form, left, right, preferred_element_type=jnp.float32)


def assemble(shards):
    return tuple(lax.all_gather(shard, 'fsdp', axis=0, tiled=True) for shard in shards)


def sum_rows(grad_full):
    return lax.psum_scatter(grad_full, 'fsdp', scatter_dimension=0, tiled=True)


def sum_rows_bf(grad_full):
    return lax.psum_scatter(grad_full.astype(jnp.bfloat16), 'fsdp', scatter_dimension=0, tiled=True).astype(jnp.float32)


def reduce_grads(grads):
    g_ln1, g_qkv, g_out, g_ln2, g_up, g_down = grads
    return (sum_rows(g_ln1), sum_rows_bf(g_qkv), sum_rows_bf(g_out), sum_rows(g_ln2), sum_rows_bf(g_up), sum_rows_bf(g_down))


def forward_local(x_in, full_params):
    ln1_w, w_qkv, w_out, ln2_w, w_up, w_down = full_params
    n_batch, seq_len, d_model = x_in.shape
    n_heads, head_dim = w_qkv.shape[2], w_qkv.shape[3]
    x_f = x_in.astype(jnp.float32)
    h_one = layer_norm(x_f, ln1_w).astype(jnp.bfloat16)
    qkv_rows = matmul('bsd,dthe->bsthe', h_one, w_qkv).astype(jnp.bfloat16)
    q_rows, k_rows, v_rows = qkv_rows[:, :, 0], qkv_rows[:, :, 1], qkv_rows[:, :, 2]
    scores = matmul('bqhe,bkhe->bhqk', q_rows, k_rows) / math.sqrt(head_dim)
    positions = jnp.arange(seq_len)
    rel_pos = (positions[:, None] - positions[None, :]).astype(jnp.float32)
    scores = jnp.where(rel_pos >= 0, scores - alibi_slopes(n_heads)[:, None, None] * rel_pos, -jnp.inf)
    attn_probs = jax.nn.softmax(scores, axis=-1)
    probs_bf = attn_probs.astype(jnp.bfloat16)
    attn_out = matmul('bhqk,bkhe->bqhe', probs_bf, v_rows).astype(jnp.bfloat16).reshape(n_batch, seq_len, d_model)
    x_mid_f = (x_f + matmul('bsf,fd->bsd', attn_out, w_out)).astype(jnp.bfloat16).astype(jnp.float32)
    h_two = layer_norm(x_mid_f, ln2_w).astype(jnp.bfloat16)
    up_pre = matmul('bsd,df->bsf', h_two, w_up)
    gelu_out = gelu_exact(up_pre).astype(jnp.bfloat16)
    y_out = (x_mid_f + matmul('bsf,fd->bsd', gelu_out, w_down)).astype(jnp.bfloat16)
    saved = (x_f, h_one, q_rows, k_rows, v_rows, attn_probs, probs_bf, attn_out, x_mid_f, h_two, up_pre, gelu_out)
    return y_out, saved


def backward_local(dy_out, full_params, saved):
    ln1_w, w_qkv, w_out, ln2_w, w_up, w_down = full_params
    x_f, h_one, q_rows, k_rows, v_rows, attn_probs, probs_bf, attn_out, x_mid_f, h_two, up_pre, gelu_out = saved
    n_batch, seq_len, n_heads, head_dim = q_rows.shape
    score_scale = 1.0 / math.sqrt(head_dim)
    g_down = matmul('bsf,bsd->fd', gelu_out, dy_out)
    d_gelu = matmul('bsd,fd->bsf', dy_out, w_down)
    _, gelu_pull = jax.vjp(gelu_exact, up_pre)
    d_up = gelu_pull(d_gelu)[0].astype(jnp.bfloat16)
    g_up = matmul('bsd,bsf->df', h_two, d_up)
    d_htwo = matmul('bsf,df->bsd', d_up, w_up)
    _, norm_pull_two = jax.vjp(layer_norm, x_mid_f, ln2_w)
    d_mid_ln, g_ln2 = norm_pull_two(d_htwo)
    d_mid = dy_out.astype(jnp.float32) + d_mid_ln
    d_mid_bf = d_mid.astype(jnp.bfloat16)
    g_out = matmul('bsf,bsd->fd', attn_out, d_mid_bf)
    d_attn = matmul('bsd,fd->bsf', d_mid_bf, w_out).astype(jnp.bfloat16).reshape(n_batch, seq_len, n_heads, head_dim)
    d_probs = matmul('bqhe,bkhe->bhqk', d_attn, v_rows)
    d_value = matmul('bhqk,bqhe->bkhe', probs_bf, d_attn)
    d_scores = attn_probs * (d_probs - jnp.sum(d_probs * attn_probs, axis=-1, keepdims=True))
    d_scores_bf = (d_scores * score_scale).astype(jnp.bfloat16)
    d_query = matmul('bhqk,bkhe->bqhe', d_scores_bf, k_rows)
    d_key = matmul('bhqk,bqhe->bkhe', d_scores_bf, q_rows)
    d_qkv = jnp.stack([d_query, d_key, d_value], axis=2).astype(jnp.bfloat16)
    g_qkv = matmul('bsd,bsthe->dthe', h_one, d_qkv)
    d_hone = matmul('bsthe,dthe->bsd', d_qkv, w_qkv)
    _, norm_pull_one = jax.vjp(layer_norm, x_f, ln1_w)
    d_x_ln, g_ln1 = norm_pull_one(d_hone)
    dx_in = (d_mid + d_x_ln).astype(jnp.bfloat16)
    return dx_in, (g_ln1, g_qkv, g_out, g_ln2, g_up, g_down)


def solution(mesh):
    row_spec = P('fsdp')

    def local_step(x_in, ln1_w, w_qkv, w_out, ln2_w, w_up, w_down, dy_out):
        shards = (ln1_w, w_qkv, w_out, ln2_w, w_up, w_down)
        y_out, saved = forward_local(x_in, assemble(shards))
        shards_again, _ = lax.optimization_barrier((shards, y_out))
        dx_in, grads = backward_local(dy_out, assemble(shards_again), saved)
        return (y_out, dx_in) + reduce_grads(grads)

    return jax.shard_map(local_step, mesh=mesh, in_specs=(row_spec,) * 8, out_specs=(row_spec,) * 8, check_vma=False)
```

profile of v0, /device:TPU:0, one launch (start us, length us, event | category | flops | bytes accessed | tf_op | source)
XLA Modules:
  0.0 1600.2 jit_solution(17772873417606270368)
XLA Ops:
  19.1 43.3 %all-reduce.8 = (f32[1536]{0:T(1024)S(1)}, f32[1536]{0:T(1024)S(1)}) all-reduce(f32[1536]{0:T(1024)S(1)} %dynamic-update-slice, f32[1536]{0:T(1024)S(1)} %dynamic-update-slice.1), channel_id=1, replica_groups=mesh['fsdp'=32] {'fsdp'}, use_global_device_ids=true, to_apply=%add | all-reduce | flops 3072 | bytes 24576
  62.5 57.5 %all-gather.9.cloned.1.call-done = bf16[1536,3,12,128]{3,0,2,1:T(8,128)(2,1)} async-done(((bf16[48,3,12,128]{3,0,2,1:T(8,128)(2,1)}), bf16[1536,3,12,128]{3,0,2,1:T(8,128)(2,1)}) %all-gather.9.cloned.1.call-update) | async-done | bytes 14155792 | tf_op jit(solution)/shard_map/all_gather | solution.py:33
  120.0 19.3 %convert_bitcast_fusion = bf16[1,1024,3,12,128]{4,1,3,2,0:T(8,128)(2,1)} fusion(bf16[1536,3,12,128]{3,0,2,1:T(8,128)(2,1)} %all-gather.9.cloned.1.call-done, bf16[1,1024,1536]{2,1,0:T(8,128)(2,1)S(1)} %copy-done.1, f32[1536]{0:T(1024)S(1)} %get-tuple-element.28, f32[1024]{0:T(1024)S(1)} %fusion.81, f32[1024]{0:T(1024)S(1)} %broadcast_multiply_fusion.1), kind=kOutput, calls=%fused_computation.69 | convolution fusion | flops 14508097536 | bytes 26753024 | tf_op jit(solution)/shard_map/bsd,dthe->bsthe/dot_general | solution.py:29
  139.3 27.7 %fusion.95 = (f32[12,1024]{1,0:T(8,128)S(1)}, f32[12,1024,1024]{1,2,0:T(8,128)}) fusion(f32[1024,1024]{0,1:T(8,128)} %subtract_convert_fusion, f32[12]{0:T(128)S(1)} %copy-done.30, pred[1024,1024]{0,1:T(8,128)(4,1)} %broadcast_compare_fusion, bf16[1,1024,3,12,128]{4,1,3,2,0:T(8,128)(2,1)} %convert_bitcast_fusion), kind=kOutput, calls=%fused_computation.126 | convolution fusion | flops 3296723968 | bytes 61915184 | tf_op jit(solution)/shard_map/sub | solution.py:61
  167.1 19.7 %fusion.70 = bf16[12,128,1024]{2,1,0:T(8,128)(2,1)} fusion(bf16[1,1024,3,12,128]{4,1,3,2,0:T(8,128)(2,1)} %convert_bitcast_fusion, f32[12,1024,1024]{1,2,0:T(8,128)} %get-tuple-element.35, f32[12,1024]{1,0:T(8,128)S(1)} %get-tuple-element.34), kind=kOutput, calls=%fused_computation.105 | convolution fusion | flops 3247964160 | bytes 56672256 | tf_op jit(solution)/shard_map/bhqk,bkhe->bqhe/dot_general | solution.py:29
  186.8 8.7 convert_reduce_fusion
  198.7 111.9 %all-gather.13.cloned.1.call-done = bf16[1536,6144]{1,0:T(8,128)(2,1)} async-done(((bf16[48,6144]{1,0:T(8,128)(2,1)}), bf16[1536,6144]{1,0:T(8,128)(2,1)}) %all-gather.13.cloned.1.call-update) | async-done | bytes 18874384 | tf_op jit(solution)/shard_map/all_gather | solution.py:33
  310.7 80.1 %multiply_convert_fusion.1 = (bf16[1024,6144]{1,0:T(8,128)(2,1)}, f32[1024,6144]{1,0:T(8,128)}, f32[1024,6144]{1,0:T(8,128)}) fusion(bf16[1536,6144]{1,0:T(8,128)(2,1)} %all-gather.13.cloned.1.call-done, bf16[1,1024,1536]{2,1,0:T(8,128)(2,1)} %copy-done.4, f32[1536]{0:T(1024)S(1)} %get-tuple-element.29, f32[1024]{0:T(1024)S(1)} %fusion.82, ...), kind=kOutput, calls=%fused_computation.21 | convolution fusion | flops 19744161792 | bytes 84948992 | tf_op jit(solution)/shard_map/bsd,df->bsf/dot_general | solution.py:29
  390.7 44.8 %all-gather.15.cloned.1.call-done = bf16[6144,1536]{1,0:T(8,128)(2,1)} async-done(((bf16[192,1536]{1,0:T(8,128)(2,1)}), bf16[6144,1536]{1,0:T(8,128)(2,1)}) %all-gather.15.cloned.1.call-update) | async-done | bytes 18874384 | tf_op jit(solution)/shard_map/all_gather | solution.py:33
  435.5 28.0 %fusion.59 = bf16[1,1024,1536]{2,1,0:T(8,128)(2,1)} fusion(bf16[1,1024,1536]{2,1,0:T(8,128)(2,1)} %copy-done.4, bf16[1024,6144]{1,0:T(8,128)(2,1)} %get-tuple-element.32, bf16[6144,1536]{1,0:T(8,128)(2,1)} %all-gather.15.cloned.1.call-done), kind=kOutput, calls=%fused_computation.84 | convolution fusion | flops 19332071424 | bytes 37748736 | tf_op jit(solution)/shard_map/bsf,fd->bsd/dot_general | solution.py:29
  465.0 28.5 %convolution_convert_fusion = bf16[6144,1536]{1,0:T(8,128)(2,1)} fusion(bf16[1024,6144]{1,0:T(8,128)(2,1)} %get-tuple-element.32, bf16[1,1024,1536]{2,1,0:T(8,128)(2,1)S(1)} %copy-done.3), kind=kOutput, calls=%fused_computation.43 | convolution fusion | flops 19336790016 | bytes 34603008 | tf_op jit(solution)/shard_map/bsf,bsd->fd/dot_general | solution.py:29
  496.0 40.3 %all-reduce.7 = (f32[1536]{0:T(1024)S(1)}, f32[1536]{0:T(1024)}) all-reduce(f32[1536]{0:T(1024)S(1)} %dynamic-update-slice.2, f32[1536]{0:T(1024)S(1)} %dynamic-update-slice.3), channel_id=1, replica_groups=mesh['fsdp'=32] {'fsdp'}, use_global_device_ids=true, to_apply=%add.2 | all-reduce | flops 3072 | bytes 24576
  536.3 51.5 %all-gather.17.cloned.1.call-done = bf16[6144,1536]{1,0:T(8,128)(2,1)} async-done(((bf16[192,1536]{1,0:T(8,128)(2,1)}), bf16[6144,1536]{1,0:T(8,128)(2,1)}) %all-gather.17.cloned.1.call-update) | async-done | bytes 18874384 | tf_op jit(solution)/shard_map/all_gather | solution.py:33
  587.9 36.0 %fusion.18 = bf16[1024,6144]{1,0:T(8,128)(2,1)} fusion(f32[1024,6144]{1,0:T(8,128)} %get-tuple-element.33, f32[1024,6144]{1,0:T(8,128)} %get-tuple-element.38, bf16[6144,1536]{1,0:T(8,128)(2,1)} %all-gather.17.cloned.1.call-done, bf16[1,1024,1536]{2,1,0:T(8,128)(2,1)S(1)} %copy-done.3), kind=kOutput, calls=%fused_computation.19 | convolution fusion | flops 19415433216 | bytes 84934656 | tf_op jit(solution)/shard_map/bsd,fd->bsf/dot_general | solution.py:29
  623.8 88.9 %all-gather.19.cloned.1.call-done = bf16[1536,6144]{1,0:T(8,128)(2,1)} async-done(((bf16[48,6144]{1,0:T(8,128)(2,1)}), bf16[1536,6144]{1,0:T(8,128)(2,1)}) %all-gather.19.cloned.1.call-update) | async-done | bytes 18874384 | tf_op jit(solution)/shard_map/all_gather | solution.py:33
  712.7 29.8 %fusion.51 = (f32[1536]{0:T(1024)}, f32[1024]{0:T(1024)S(1)}, f32[1024,1536]{1,0:T(8,128)}) fusion(bf16[1,1024,1536]{2,1,0:T(8,128)(2,1)} %copy-done.4, f32[1024]{0:T(1024)S(1)} %fusion.82, f32[1024]{0:T(1024)S(1)} %broadcast_multiply_fusion, f32[1536]{0:T(1024)S(1)} %get-tuple-element.26, bf16[1024,6144]{1,0:T(8,128)(2,1)} %fusion.18, ...), kind=kOutput, calls=%fused_computation.76 | convolution fusion | flops 19339931648 | bytes 40919040 | tf_op jit(solution)/shard_map/bsf,df->bsd/dot_general | solution.py:29
  752.2 25.3 %all-gather.21.cloned.1.call-done = bf16[1536,1536]{1,0:T(8,128)(2,1)} async-done(((bf16[48,1536]{1,0:T(8,128)(2,1)}), bf16[1536,1536]{1,0:T(8,128)(2,1)}) %all-gather.21.cloned.1.call-update) | async-done | bytes 4718608 | tf_op jit(solution)/shard_map/all_gather | solution.py:33
  777.6 9.2 convolution_convert_fusion.4
  790.0 9.2 convolution_convert_fusion.3
  799.2 19.9 %convert_bitcast_fusion.1 = bf16[1024,1,12,128]{0,3,2,1:T(8,128)(2,1)} fusion(bf16[1024,12,128]{0,2,1:T(8,128)(2,1)S(1)} %bitcast.163, f32[12,1024,1024]{1,2,0:T(8,128)} %get-tuple-element.35, f32[12,1024]{1,0:T(8,128)S(1)} %copy-done.32), kind=kOutput, calls=%fused_computation.100 | convolution fusion | flops 3247964160 | bytes 56672256 | tf_op jit(solution)/shard_map/bhqk,bqhe->bkhe/dot_general | solution.py:29
  819.1 21.4 %fusion.68 = f32[12,1024,1024]{1,2,0:T(8,128)} fusion(bf16[1024,12,128]{0,2,1:T(8,128)(2,1)S(1)} %bitcast.164, bf16[1,1024,3,12,128]{4,1,3,2,0:T(8,128)(2,1)} %convert_bitcast_fusion), kind=kOutput, calls=%fused_computation.103 | convolution fusion | flops 3221225472 | bytes 56623104 | tf_op jit(solution)/shard_map/bqhe,bkhe->bhqk/dot_general | solution.py:29
  840.5 63.8 %convert_bitcast_fusion.3 = bf16[1024,1,12,128]{0,3,2,1:T(8,128)(2,1)} fusion(f32[12,1024,1024]{1,2,0:T(8,128)} %fusion.68, bf16[1,1024,3,12,128]{4,1,3,2,0:T(8,128)(2,1)} %convert_bitcast_fusion, f32[12,1024,1024]{1,2,0:T(8,128)} %get-tuple-element.35, f32[12,1024]{1,0:T(8,128)S(1)} %copy-done.32), kind=kOutput, calls=%fused_computation.102 | convolution fusion | flops 3310892032 | bytes 207749120 | tf_op jit(solution)/shard_map/bhqk,bkhe->bqhe/dot_general | solution.py:29
  904.3 64.5 %convert_bitcast_fusion.2 = bf16[1024,1,12,128]{0,3,2,1:T(8,128)(2,1)} fusion(f32[12,1024,1024]{1,2,0:T(8,128)} %fusion.68, bf16[1,1024,3,12,128]{4,1,3,2,0:T(8,128)(2,1)} %convert_bitcast_fusion, f32[12,1024,1024]{1,2,0:T(8,128)} %get-tuple-element.35, f32[12,1024]{1,0:T(8,128)S(1)} %copy-done.32), kind=kOutput, calls=%fused_computation.101 | convolution fusion | flops 3310892032 | bytes 207749120 | tf_op jit(solution)/shard_map/bhqk,bqhe->bkhe/dot_general | solution.py:29
  968.8 21.8 %convolution_convert_fusion.2 = bf16[1536,3,12,128]{3,0,2,1:T(8,128)(2,1)} fusion(bf16[1,1024,1536]{2,1,0:T(8,128)(2,1)S(1)} %copy-done.2, f32[1536]{0:T(1024)S(1)} %copy-done.25, f32[1024]{0:T(1024)S(1)} %copy-done.9, f32[1024]{0:T(1024)S(1)} %copy-done.7, bf16[1024,1,12,128]{0,3,2,1:T(8,128)(2,1)} %convert_bitcast_fusion.1, ...), kind=kOutput, calls=%fused_computation.45 | convolution fusion | flops 14538768384 | bytes 26753024 | tf_op jit(solution)/shard_map/bsd,bsthe->dthe/dot_general | solution.py:29
  991.4 28.6 %convolution_convert_fusion.1 = bf16[1536,6144]{1,0:T(8,128)(2,1)} fusion(bf16[1024,6144]{1,0:T(8,128)(2,1)} %fusion.18, bf16[1,1024,1536]{2,1,0:T(8,128)(2,1)} %copy-done.4, f32[1536]{0:T(1024)S(1)} %copy-done.23, f32[1024]{0:T(1024)S(1)} %copy-done.20, f32[1024]{0:T(1024)S(1)} %copy-done.17), kind=kOutput, calls=%fused_computation.44 | convolution fusion | flops 19344654336 | bytes 34617344 | tf_op jit(solution)/shard_map/bsd,bsf->df/dot_general | solution.py:29
  1022.2 76.2 %all-gather.23.cloned.1.call-done = bf16[1536,3,12,128]{3,0,1,2:T(8,128)(2,1)} async-done(((bf16[48,3,12,128]{3,0,1,2:T(8,128)(2,1)}), bf16[1536,3,12,128]{3,0,1,2:T(8,128)(2,1)}) %all-gather.23.cloned.1.call-update) | async-done | bytes 14155792 | tf_op jit(solution)/shard_map/all_gather | solution.py:33
  1098.5 23.7 %fusion.55 = (f32[1024]{0:T(1024)S(1)}, f32[1024,1536,1,1]{1,0,3,2:T(8,128)}) fusion(bf16[1,1024,1536]{2,1,0:T(8,128)(2,1)S(1)} %copy-done.2, f32[1536]{0:T(1024)S(1)} %copy-done.18, f32[1024]{0:T(1024)S(1)} %copy-done.7, bf16[1536,3,12,128]{3,0,1,2:T(8,128)(2,1)} %all-gather.23.cloned.1.call-done, bf16[1024,1,12,128]{0,3,2,1:T(8,128)(2,1)} %convert_bitcast_fusion.1, ...), kind=kOutput, calls=%fused_computation.80 | convolution fusion | flops 14512815104 | bytes 33044480 | tf_op jit(solution)/shard_map/bsthe,dthe->bsd/dot_general | solution.py:29
  1127.4 39.6 %all-reduce.6 = (f32[1536]{0:T(1024)S(1)}, f32[1536]{0:T(1024)S(1)}) all-reduce(f32[1536]{0:T(1024)S(1)} %get-tuple-element.20, f32[1536]{0:T(1024)S(1)} %copy-done.21), channel_id=2, replica_groups=mesh['fsdp'=32] {'fsdp'}, use_global_device_ids=true, to_apply=%region_12.13.clone | all-reduce | flops 3072 | bytes 24576
  1168.1 8.1 add_convert_fusion
  1176.3 34.1 %reduce-scatter.7.cloned.1.call-done = bf16[48,1536]{1,0:T(8,128)(2,1)} async-done(((bf16[1536,1536]{1,0:T(8,128)(2,1)}), bf16[48,1536]{1,0:T(8,128)(2,1)}) %reduce-scatter.7.cloned.1.call-update) | async-done | bytes 147472 | tf_op jit(solution)/shard_map/reduce_scatter | solution.py:41
  1212.0 166.2 %reduce-scatter.5.cloned.1.call-done = bf16[48,3,12,128]{3,0,2,1:T(8,128)(2,1)} async-done(((bf16[1536,3,12,128]{3,0,2,1:T(8,128)(2,1)}), bf16[48,3,12,128]{3,0,2,1:T(8,128)(2,1)}) %reduce-scatter.5.cloned.1.call-update) | async-done | bytes 442384 | tf_op jit(solution)/shard_map/reduce_scatter | solution.py:41
  1380.2 210.5 %reduce-scatter.9.cloned.1.call-done = bf16[48,6144]{1,0:T(8,128)(2,1)} async-done(((bf16[1536,6144]{1,0:T(8,128)(2,1)}), bf16[48,6144]{1,0:T(8,128)(2,1)}) %reduce-scatter.9.cloned.1.call-update) | async-done | bytes 589840 | tf_op jit(solution)/shard_map/reduce_scatter | solution.py:41
  (124 shorter events, 46.9 us)
Async XLA Ops:
  7.2 11.4 copy-start.26
  7.2 11.7 copy-start.28
  7.2 112.8 %all-gather.9.cloned.1.call-start = ((), (), s32[]{:S(2)}) async-start(), calls=%async_computation.4 | async-start | bytes 14598144 | tf_op jit(solution)/shard_map/all_gather | solution.py:33
  7.9 178.9 %all-gather.11.cloned.1.call-start = ((), (), s32[]{:S(2)}) async-start(), calls=%async_computation.5 | async-start | bytes 4866048 | tf_op jit(solution)/shard_map/all_gather | solution.py:33
  8.7 302.0 %all-gather.13.cloned.1.call-start = ((), (), s32[]{:S(2)}) async-start(), calls=%async_computation.6 | async-start | bytes 19464192 | tf_op jit(solution)/shard_map/all_gather | solution.py:33
  9.4 426.1 %all-gather.15.cloned.1.call-start = ((), (), s32[]{:S(2)}) async-start(), calls=%async_computation.7 | async-start | bytes 19464192 | tf_op jit(solution)/shard_map/all_gather | solution.py:33
  10.0 577.9 %all-gather.17.cloned.1.call-start = ((), (), s32[]{:S(2)}) async-start(), calls=%async_computation.8 | async-start | bytes 19464192 | tf_op jit(solution)/shard_map/all_gather | solution.py:33
  17.0 122.3 %copy-start.6 = (f32[1024]{0:T(1024)}, f32[1024]{0:T(1024)S(1)}, u32[]{:S(2)}) copy-start(f32[1024]{0:T(1024)S(1)} %broadcast_multiply_fusion.1) | copy-start | bytes 12292
  18.6 120.8 %copy-start.8 = (f32[1024]{0:T(1024)}, f32[1024]{0:T(1024)S(1)}, u32[]{:S(2)}) copy-start(f32[1024]{0:T(1024)S(1)} %fusion.81) | copy-start | bytes 12292
  62.5 76.9 %copy-start.24 = (f32[1536]{0:T(1024)}, f32[1536]{0:T(1024)S(1)}, u32[]{:S(2)}) copy-start(f32[1536]{0:T(1024)S(1)} %get-tuple-element.28) | copy-start | bytes 18436
  62.5 248.2 %copy-start.22 = (f32[1536]{0:T(1024)}, f32[1536]{0:T(1024)S(1)}, u32[]{:S(2)}) copy-start(f32[1536]{0:T(1024)S(1)} %get-tuple-element.29) | copy-start | bytes 18436
  120.0 19.3 %copy-start.30 = (f32[12]{0:T(128)S(1)}, f32[12]{0:T(128)}, u32[]{:S(2)}) copy-start(f32[12]{0:T(128)} %constant.87.clone) | copy-start | bytes 148
  167.1 19.7 %copy-start.31 = (f32[12,1024]{1,0:T(8,128)}, f32[12,1024]{1,0:T(8,128)S(1)}, u32[]{:S(2)}) copy-start(f32[12,1024]{1,0:T(8,128)S(1)} %get-tuple-element.34) | copy-start | bytes 147460
  195.6 547.0 %copy-start.16 = (f32[1024]{0:T(1024)}, f32[1024]{0:T(1024)S(1)}, u32[]{:S(2)}) copy-start(f32[1024]{0:T(1024)S(1)} %broadcast_multiply_fusion) | copy-start | bytes 12292
  198.7 543.8 %copy-start.19 = (f32[1024]{0:T(1024)}, f32[1024]{0:T(1024)S(1)}, u32[]{:S(2)}) copy-start(f32[1024]{0:T(1024)S(1)} %fusion.82) | copy-start | bytes 12292
  435.5 29.4 %copy-start.3 = (bf16[1,1024,1536]{2,1,0:T(8,128)(2,1)S(1)}, bf16[1,1024,1536]{2,1,0:T(8,128)(2,1)}, u32[]{:S(2)}) copy-start(bf16[1,1024,1536]{2,1,0:T(8,128)(2,1)} %param.16) | copy-start | bytes 9437188
  463.6 249.2 %all-gather.19.cloned.1.call-start = ((), (), s32[]{:S(2)}) async-start(), calls=%async_computation.9 | async-start | bytes 19464192 | tf_op jit(solution)/shard_map/all_gather | solution.py:33
  464.1 313.4 %all-gather.21.cloned.1.call-start = ((), (), s32[]{:S(2)}) async-start(), calls=%async_computation.10 | async-start | bytes 4866048 | tf_op jit(solution)/shard_map/all_gather | solution.py:33
  464.9 555.1 %reduce-scatter.11.cloned.1.call-start = ((), (), s32[]{:S(2)}) async-start(), calls=%async_computation.15 | async-start | bytes 19464192 | tf_op jit(solution)/shard_map/reduce_scatter | solution.py:41
  493.5 605.0 %all-gather.23.cloned.1.call-start = ((), (), s32[]{:S(2)}) async-start(), calls=%async_computation.11 | async-start | bytes 14598144 | tf_op jit(solution)/shard_map/all_gather | solution.py:33
  495.4 715.0 %reduce-scatter.7.cloned.1.call-start = ((), (), s32[]{:S(2)}) async-start(), calls=%async_computation.13 | async-start | bytes 4866048 | tf_op jit(solution)/shard_map/reduce_scatter | solution.py:41
  712.7 29.8 %copy-start.15 = (f32[1024]{0:T(1024)S(1)}, f32[1024]{0:T(1024)}, u32[]{:S(2)}) copy-start(f32[1024]{0:T(1024)} %copy-done.14) | copy-start | bytes 12292
  712.7 29.8 %copy-start.5 = (bf16[1,1024,1536]{2,1,0:T(8,128)(2,1)S(1)}, bf16[1,1024,1536]{2,1,0:T(8,128)(2,1)}, u32[]{:S(2)}) copy-start(bf16[1,1024,1536]{2,1,0:T(8,128)(2,1)} %copy-done.4) | copy-start | bytes 9437188
  819.0 559.2 %reduce-scatter.5.cloned.1.call-start = ((), (), s32[]{:S(2)}) async-start(), calls=%async_computation.12 | async-start | bytes 14598144 | tf_op jit(solution)/shard_map/reduce_scatter | solution.py:41
  904.3 64.5 %copy-start.2 = (bf16[1,1024,1536]{2,1,0:T(8,128)(2,1)S(1)}, bf16[1,1024,1536]{2,1,0:T(8,128)(2,1)}, u32[]{:S(2)}) copy-start(bf16[1,1024,1536]{2,1,0:T(8,128)(2,1)} %param.9) | copy-start | bytes 9437188
  904.3 64.5 %copy-start.7 = (f32[1024]{0:T(1024)S(1)}, f32[1024]{0:T(1024)}, u32[]{:S(2)}) copy-start(f32[1024]{0:T(1024)} %copy-done.6) | copy-start | bytes 12292
  904.3 64.5 %copy-start.9 = (f32[1024]{0:T(1024)S(1)}, f32[1024]{0:T(1024)}, u32[]{:S(2)}) copy-start(f32[1024]{0:T(1024)} %copy-done.8) | copy-start | bytes 12292
  904.3 64.5 %copy-start.25 = (f32[1536]{0:T(1024)S(1)}, f32[1536]{0:T(1024)}, u32[]{:S(2)}) copy-start(f32[1536]{0:T(1024)} %copy-done.24) | copy-start | bytes 18436
  990.7 600.0 %reduce-scatter.9.cloned.1.call-start = ((), (), s32[]{:S(2)}) async-start(), calls=%async_computation.14 | async-start | bytes 19464192 | tf_op jit(solution)/shard_map/reduce_scatter | solution.py:41
  1020.0 78.5 %copy-start.18 = (f32[1536]{0:T(1024)S(1)}, f32[1536]{0:T(1024)}, u32[]{:S(2)}) copy-start(f32[1536]{0:T(1024)} %get-tuple-element.27) | copy-start | bytes 18436
  1098.5 23.7 %copy-start.13 = (f32[1024]{0:T(1024)S(1)}, f32[1024]{0:T(1024)}, u32[]{:S(2)}) copy-start(f32[1024]{0:T(1024)} %copy-done.12) | copy-start | bytes 12292
  1122.2 46.0 %copy-start.11 = (f32[1024]{0:T(1024)S(1)}, f32[1024]{0:T(1024)}, u32[]{:S(2)}) copy-start(f32[1024]{0:T(1024)} %copy-done.10) | copy-start | bytes 12292
  (13 other events, 38.7 us)
Sparse Core Ops, SparseCore 0:
  10.8 109.1 all-gather.8
  122.9 62.4 all-gather.10
  188.3 122.3 all-gather.12
  313.4 122.0 all-gather.14
  463.7 124.1 all-gather.16
  590.6 122.0 all-gather.18
  715.6 61.9 all-gather.20
  784.0 205.2 reduce-scatter.10
  992.7 105.7 all-gather.22
  1103.8 106.5 reduce-scatter.6
  1216.4 161.7 reduce-scatter.4
  1384.5 206.1 reduce-scatter.8
where the time goes:
time: 1600 us
  waiting for transfers between devices  871 us (54%)
  matrix products  540 us (34%)
  blocking collectives  123 us (8%)
  other arithmetic  37.2 us (2%)
    dot_general x17, matrix products, matmul(): return jnp.einsum(form, left, right, preferred_element_type=jnp.float32)  512 us
    all_gather x8, waiting for transfers between devices, assemble(): lax.all_gather(shard, 'fsdp', axis=0, tiled=True)  456 us
    reduce_scatter x4, waiting for transfers between devices, sum_rows_bf(): lax.psum_scatter(grad_full.astype(jnp.bfloat16), 'fsdp', scatter_dimensio...  411 us
    unnamed x3, blocking collectives  123 us
  transfers between devices with their start and end apart: 12, of which 10 were waited for; matrix products, arithmetic and copies ran while one was open for 35% of the time, Pallas kernels for 0%

commit v1 on v0

v1 whole, which is shorter than its diff:
```python
import functools
import math

import jax
import jax.numpy as jnp
from jax import lax
from jax.experimental import pallas as pl
from jax.experimental.pallas import tpu as pltpu
from jax.sharding import PartitionSpec as P

EPS = 1e-5
SUB = 768
HALF = SUB // 2
RB = 48
F32, BF16 = jnp.float32, jnp.bfloat16
VMEM_LIMIT = 62 * 1024 * 1024
MESH = pl.DeviceIdType.MESH
HBM = pltpu.MemorySpace.HBM


def sds(shape, dtype):
    return jax.ShapeDtypeStruct(shape, dtype)


def dot(a, b, ca=1, cb=0):
    return lax.dot_general(a, b, (((ca,), (cb,)), ((), ())), preferred_element_type=F32)


def clip(t, n):
    return jnp.minimum(jnp.maximum(t, 0), n - 1)


class Phase:
    def __init__(self, n, ins, outs, body, start=None):
        self.n, self.ins, self.outs, self.body, self.start = n, ins, outs, body, start


def coords():
    me = lax.axis_index('fsdp')
    return me, me // 8, (me // 4) % 2, (me // 2) % 2, me % 2


def peers():
    me, z, y, x, c = coords()
    zs = [lax.rem(me + 8 * d, 32) for d in (1, 2, 3)]
    return zs, me + 4 - 8 * y, me + 2 - 4 * x, me + 1 - 2 * c


def remote(src, dst, ssem, rsem, dev):
    return pltpu.make_async_remote_copy(src_ref=src, dst_ref=dst, send_sem=ssem, recv_sem=rsem, device_id=(dev,), device_id_type=MESH)


class Unit:
    def __init__(self, rows, cols):
        self.nc, self.nr = cols // SUB, rows // RB
        self.count = self.nc * self.nr

    def at(self, u, half=None):
        col = pl.multiple_of((u % self.nc) * SUB, HALF)
        width = SUB
        if half is not None:
            col, width = pl.multiple_of(col + half * HALF, HALF), HALF
        rows = slice(None) if self.nr == 1 else pl.ds(pl.multiple_of((u // self.nc) * RB, 16), RB)
        return rows, pl.ds(col, width)


class Gather:
    def __init__(self, shard, off=0):
        rows, cols = shard.shape
        self.unit, self.off = Unit(rows, cols), off
        self.s = self.unit.count
        self.k = off + self.s + 3
        self.ins = [(shard, pl.BlockSpec(memory_space=pltpu.VMEM))]
        self.outs = [(sds((4, 2, 2, 2, rows, cols), BF16), pl.BlockSpec(memory_space=HBM))]
        self.scratch = [pltpu.SemaphoreType.DMA((self.s, 8)), pltpu.SemaphoreType.DMA((self.s, 8)), pltpu.SemaphoreType.DMA]

    def copies(self, stage, u, refs):
        shard, full, ss, rs, _ = refs
        me, z, y, x, c = coords()
        zs, yp, xp, cp = peers()
        at = self.unit.at
        if stage == 0:
            r, q = at(u)
            return [remote(shard.at[r, q], full.at[z, y, x, c, r, q], ss.at[u, d], rs.at[u, d], zs[d]) for d in range(3)]
        if stage == 3:
            r, q = at(u)
            v = full.at[:, :, :, c, r, q]
            return [remote(v, v, ss.at[u, 7], rs.at[u, 7], cp)]
        (ra, qa), (rb, qb) = at(u, 0), at(u, 1)
        if stage == 1:
            va, vb = full.at[:, y, x, c, ra, qa], full.at[:, y, x, c, rb, qb]
            return [remote(va, va, ss.at[u, 3], rs.at[u, 3], yp), remote(vb, vb, ss.at[u, 4], rs.at[u, 4], xp)]
        va, vb = full.at[:, :, x, c, ra, qa], full.at[:, y, :, c, rb, qb]
        return [remote(va, va, ss.at[u, 5], rs.at[u, 5], xp), remote(vb, vb, ss.at[u, 6], rs.at[u, 6], yp)]

    def step(self, k, fire, refs):
        shard, full, ss, rs, ls = refs
        me, z, y, x, c = coords()
        s = self.s

        @pl.when(fire & (k == 0))
        def _():
            own = pltpu.make_async_copy(shard, full.at[z, y, x, c], ls)
            own.start()

            @pl.loop(0, s)
            def _(u):
                for cp in self.copies(0, u, refs):
                    cp.start()

            own.wait()

        for stage in (1, 2, 3):
            u = k - self.off - (stage - 1)

            @pl.when(fire & (u >= 0) & (u < s))
            def _(stage=stage, u=u):
                for cp in self.copies(stage - 1, u, refs):
                    cp.wait_recv()
                for cp in self.copies(stage, u, refs):
                    cp.start()

        @pl.when(fire & (k == self.off + s + 2))
        def _():
            @pl.loop(0, s)
            def _(u):
                for cp in self.copies(3, u, refs):
                    cp.wait_recv()
                for stage in range(4):
                    for cp in self.copies(stage, u, refs):
                        cp.wait_send()


class GatherSmall:
    def __init__(self, tile):
        self.k = 5
        self.ins = [(tile, pl.BlockSpec(memory_space=pltpu.VMEM))]
        self.outs = [(sds((4, 2, 2, 2) + tile.shape, F32), pl.BlockSpec(memory_space=HBM))]
        self.scratch = [pltpu.SemaphoreType.DMA((6,)), pltpu.SemaphoreType.DMA((6,)), pltpu.SemaphoreType.DMA]

    def copies(self, stage, refs):
        tile, full, ss, rs, _ = refs
        me, z, y, x, c = coords()
        zs, yp, xp, cp = peers()
        if stage == 0:
            return [remote(tile, full.at[z, y, x, c], ss.at[d], rs.at[d], zs[d]) for d in range(3)]
        v, dev = ((full.at[:, y, x, c], yp), (full.at[:, :, x, c], xp), (full.at[:, :, :, c], cp))[stage - 1]
        return [remote(v, v, ss.at[2 + stage], rs.at[2 + stage], dev)]

    def step(self, k, fire, refs):
        tile, full, ss, rs, ls = refs
        me, z, y, x, c = coords()
        for stage in range(5):
            @pl.when(fire & (k == stage))
            def _(stage=stage):
                if stage == 0:
                    own = pltpu.make_async_copy(tile, full.at[z, y, x, c], ls)
                    own.start()
                else:
                    for cp in self.copies(stage - 1, refs):
                        cp.wait_recv()
                if stage < 4:
                    for cp in self.copies(stage, refs):
                        cp.start()
                else:
                    for st in range(4):
                        for cp in self.copies(st, refs):
                            cp.wait_send()
                if stage == 0:
                    own.wait()


class Scatter:
    def __init__(self, grad, u0, s, off=0):
        rows, cols = grad.shape[-2:]
        self.unit, self.u0, self.s, self.off = Unit(rows, cols), u0, s, off
        self.k = off + s + 3
        nc = self.unit.nc
        self.ins = [(grad, pl.BlockSpec(memory_space=HBM))]
        nblk = s // nc if self.unit.nr > 1 else 1
        ncol = nc if self.unit.nr > 1 else s
        self.out_shape = sds((nblk * RB, ncol * SUB), F32)
        self.ncol = ncol
        self.scratch = [
            pltpu.VMEM((s, 4, 2, 2, RB, SUB), BF16),
            pltpu.VMEM((2, 4, 2, 2, RB, SUB), BF16),
            pltpu.VMEM((2, s, 4, 2, RB, HALF), BF16),
            pltpu.VMEM((s, 4, RB, SUB), BF16),
            pltpu.VMEM((s, 3, RB, SUB), BF16),
            pltpu.SemaphoreType.DMA((s, 8)), pltpu.SemaphoreType.DMA((s, 8)), pltpu.SemaphoreType.DMA((2,))]

    def out_spec(self, kmap):
        ncol = self.ncol

        def index(t):
            u = clip(kmap(t) - self.off - 3, self.s)
            return u // ncol, u % ncol

        self.outs = [(self.out_shape, pl.BlockSpec((RB, SUB), index))]

    def local(self, u, refs):
        grad, _, _, own, _, _, _, _, _, ls = refs
        me, z, y, x, c = coords()
        r, q = self.unit.at(self.u0 + u)
        slot = u % 2
        return pltpu.make_async_copy(grad.at[:, :, :, c, r, q], own.at[slot], ls.at[slot])

    def copies(self, stage, u, refs):
        grad, _, got, own, two, three, four, ss, rs, ls = refs
        me, z, y, x, c = coords()
        zs, yp, xp, cp = peers()
        a, b = pl.ds(0, HALF), pl.ds(HALF, HALF)
        if stage == 0:
            r, q = self.unit.at(self.u0 + u)
            return [remote(grad.at[:, :, :, 1 - c, r, q], got.at[u], ss.at[u, 0], rs.at[u, 0], cp)]
        if stage == 1:
            return [remote(got.at[u, :, 1 - y, :, :, a], two.at[0, u], ss.at[u, 1], rs.at[u, 1], yp),
                    remote(got.at[u, :, :, 1 - x, :, b], two.at[1, u], ss.at[u, 2], rs.at[u, 2], xp)]
        if stage == 2:
            return [remote(two.at[0, u, :, 1 - x], three.at[u, :, :, a], ss.at[u, 3], rs.at[u, 3], xp),
                    remote(two.at[1, u, :, 1 - y], three.at[u, :, :, b], ss.at[u, 4], rs.at[u, 4], yp)]
        return [remote(three.at[u, lax.rem(z + d + 1, 4)], four.at[u, d], ss.at[u, 5 + d], rs.at[u, 5 + d], zs[d]) for d in range(3)]

    def add(self, stage, u, refs):
        grad, out, got, own, two, three, four, ss, rs, ls = refs
        me, z, y, x, c = coords()
        a, b = pl.ds(0, HALF), pl.ds(HALF, HALF)
        if stage == 1:
            slot = u % 2
            for zz in range(4):
                for yy in range(2):
                    for xx in range(2):
                        got[u, zz, yy, xx] = got[u, zz, yy, xx] + own[slot, zz, yy, xx]
        elif stage == 2:
            for zz in range(4):
                for i in range(2):
                    two[0, u, zz, i] = two[0, u, zz, i] + got[u, zz, y, i, :, a]
                    two[1, u, zz, i] = two[1, u, zz, i] + got[u, zz, i, x, :, b]
        elif stage == 3:
            for zz in range(4):
                three[u, zz, :, a] = three[u, zz, :, a] + two[0, u, zz, x]
                three[u, zz, :, b] = three[u, zz, :, b] + two[1, u, zz, y]
        else:
            total = three[u, z].astype(F32)
            for d in range(3):
                total = total + four[u, d].astype(F32)
            out[...] = total

    def step(self, k, fire, refs):
        s = self.s

        @pl.when(fire & (k == 0))
        def _():
            @pl.loop(0, s)
            def _(u):
                for cp in self.copies(0, u, refs):
                    cp.start()

            for u in range(min(2, s)):
                self.local(u, refs).start()

        for stage in (1, 2, 3, 4):
            u = k - self.off - (stage - 1)

            @pl.when(fire & (u >= 0) & (u < s))
            def _(stage=stage, u=u):
                for cp in self.copies(stage - 1, u, refs):
                    cp.wait_recv()
                if stage == 1:
                    self.local(u, refs).wait()
                self.add(stage, u, refs)
                if stage < 4:
                    for cp in self.copies(stage, u, refs):
                        cp.start()
                if stage == 1:
                    @pl.when(u + 2 < s)
                    def _():
                        self.local(u + 2, refs).start()

        @pl.when(fire & (k == self.off + s + 2))
        def _():
            @pl.loop(0, s)
            def _(u):
                for stage in range(4):
                    for cp in self.copies(stage, u, refs):
                        cp.wait_send()


def host(name, cid, phases, comms=(), shared=(), steps=None, cost=None):
    k_all = max([c.k for c in comms], default=1)
    at = 0
    for p in phases:
        p.at = at if p.start is None else p.start
        at = p.at + p.n
    total = max(at, k_all, steps or 0)
    kmap = (lambda t: t) if total == k_all else (lambda t: (t * k_all) // total)
    ins, in_specs, outs, out_specs, scratch = [], [], [], [], []
    for p in phases:
        for arr, block, index in p.ins:
            ins.append(arr)
            if block == 'smem':
                in_specs.append(pl.BlockSpec(memory_space=pltpu.SMEM))
            elif index is None:
                in_specs.append(pl.BlockSpec(block, functools.partial(lambda n, t: (0,) * n, len(block)), pipeline_mode=pl.Buffered(1)))
            else:
                in_specs.append(pl.BlockSpec(block, functools.partial(lambda p, f, t: f(clip(t - p.at, p.n)), p, index)))
        for shape, block, index in p.outs:
            outs.append(shape)
            out_specs.append(pl.BlockSpec(block, functools.partial(lambda p, f, t: f(clip(t - p.at, p.n)), p, index)))
    for c in comms:
        if isinstance(c, Scatter):
            c.out_spec(kmap)
        for arr, spec in c.ins:
            ins.append(arr)
            in_specs.append(spec)
        for shape, spec in c.outs:
            outs.append(shape)
            out_specs.append(spec)
        scratch += c.scratch
    scratch += list(shared)

    def kernel(*refs):
        refs = list(refs)
        rin, rout, rscr = refs[:len(ins)], refs[len(ins):len(ins) + len(outs)], refs[len(ins) + len(outs):]
        t = pl.program_id(0)
        if comms:
            @pl.when(t == 0)
            def _():
                zs, yp, xp, cp = peers()
                bar = pltpu.get_barrier_semaphore()
                for dev in (*zs, yp, xp, cp):
                    pl.semaphore_signal(bar, inc=1, device_id=(dev,), device_id_type=MESH)
                pl.semaphore_wait(bar, 6)
        i, o, s = sum(len(p.ins) for p in phases), sum(len(p.outs) for p in phases), 0
        k = kmap(t)
        fire = (t == 0) | (k != kmap(jnp.maximum(t - 1, 0)))
        for c in comms:
            ni, no, ns = len(c.ins), len(c.outs), len(c.scratch)
            c.step(k, fire, rin[i:i + ni] + rout[o:o + no] + rscr[s:s + ns])
            i, o, s = i + ni, o + no, s + ns
        extra = rscr[s:]
        i = o = 0
        for p in phases:
            pi, po = rin[i:i + len(p.ins)], rout[o:o + len(p.outs)]
            i, o = i + len(p.ins), o + len(p.outs)

            @pl.when((t >= p.at) & (t < p.at + p.n))
            def _(p=p, pi=pi, po=po):
                p.body(t - p.at, pi, po, extra)

    params = dict(dimension_semantics=("arbitrary",), vmem_limit_bytes=VMEM_LIMIT)
    if comms:
        params.update(collective_id=cid, has_side_effects=True)
    got = pl.pallas_call(kernel, grid=(total,), in_specs=in_specs, out_specs=out_specs, out_shape=outs, scratch_shapes=scratch,
                         compiler_params=pltpu.CompilerParams(**params), name=name,
                         cost_estimate=pl.CostEstimate(flops=int(cost or 2e10), bytes_accessed=int(3e7), transcendentals=0))(*ins)
    return list(got)


def norm_parts(t):
    mean = jnp.mean(t, axis=-1, keepdims=True)
    cen = t - mean
    rstd = lax.rsqrt(jnp.mean(cen * cen, axis=-1, keepdims=True) + EPS)
    return cen * rstd, rstd


def norm_back(d, t, w):
    xhat, rstd = norm_parts(t)
    dh = d * w
    m1 = jnp.mean(dh, axis=-1, keepdims=True)
    m2 = jnp.mean(dh * xhat, axis=-1, keepdims=True)
    return rstd * (dh - m1 - xhat * m2), jnp.sum(d * xhat, axis=0, keepdims=True)


def alibi_slopes(n_heads):
    padded = 2 ** math.ceil(math.log2(n_heads))
    base = [2.0 ** (-8.0 * (k + 1) / padded) for k in range(padded)]
    ordered = base if padded == n_heads else base[1::2] + base[0::2]
    return jnp.array(ordered[:n_heads], dtype=F32)


def causal(i, tq, slope):
    row = lax.broadcasted_iota(jnp.int32, (tq, tq), 0)
    col = lax.broadcasted_iota(jnp.int32, (tq, tq), 1)
    rel = (row - col).astype(F32)
    diag = slope * rel
    past = None
    if i:
        r = lax.broadcasted_iota(jnp.int32, (tq, i * tq), 0) + i * tq
        q = lax.broadcasted_iota(jnp.int32, (tq, i * tq), 1)
        past = slope * (r - q).astype(F32)
    return past, diag, row >= col


def attn_fwd(q_ref, k_ref, v_ref, o_ref, l_ref, slope, scale, tq):
    n = q_ref.shape[0] // tq
    for i in range(n):
        q = q_ref[i * tq:(i + 1) * tq, :]
        past, diag, keep = causal(i, tq, slope)
        sd = jnp.where(keep, dot(q, k_ref[i * tq:(i + 1) * tq, :], 1, 1) * scale - diag, -jnp.inf)
        m = jnp.max(sd, axis=-1, keepdims=True)
        if i:
            sp = dot(q, k_ref[:i * tq, :], 1, 1) * scale - past
            m = jnp.maximum(m, jnp.max(sp, axis=-1, keepdims=True))
            ep = jnp.exp(sp - m)
        ed = jnp.exp(sd - m)
        l = jnp.sum(ed, axis=-1, keepdims=True)
        if i:
            l = l + jnp.sum(ep, axis=-1, keepdims=True)
        inv = 1.0 / l
        o = dot((ed * inv).astype(BF16), v_ref[i * tq:(i + 1) * tq, :])
        if i:
            o = o + dot((ep * inv).astype(BF16), v_ref[:i * tq, :])
        o_ref[i * tq:(i + 1) * tq, :] = o.astype(BF16)
        l_ref[i * tq:(i + 1) * tq, :] = m + jnp.log(l)


def attn_bwd(q_ref, k_ref, v_ref, a_ref, da_ref, l_ref, dq_ref, dk_ref, dv_ref, dk_s, dv_s, slope, scale, tq):
    n = q_ref.shape[0] // tq
    dk_s[...] = jnp.zeros_like(dk_s)
    dv_s[...] = jnp.zeros_like(dv_s)
    for i in range(n):
        rows = slice(i * tq, (i + 1) * tq)
        q, da = q_ref[rows, :], da_ref[rows, :]
        lse = l_ref[rows, :]
        delta = jnp.sum(da.astype(F32) * a_ref[rows, :].astype(F32), axis=-1, keepdims=True)
        past, diag, keep = causal(i, tq, slope)
        dq = None
        for own in ((True,) if i == 0 else (True, False)):
            keys = rows if own else slice(0, i * tq)
            kk, vv = k_ref[keys, :], v_ref[keys, :]
            s = dot(q, kk, 1, 1) * scale - (diag if own else past)
            p = jnp.exp(s - lse)
            if own:
                p = jnp.where(keep, p, 0.0)
            ds = (p * (dot(da, vv, 1, 1) - delta) * scale).astype(BF16)
            dv_s[keys, :] += dot(p.astype(BF16), da, 0, 0)
            dk_s[keys, :] += dot(ds, q, 0, 0)
            part = dot(ds, kk)
            dq = part if dq is None else dq + part
        dq_ref[rows, :] = dq.astype(BF16)
    dk_ref[...] = dk_s[...].astype(BF16)
    dv_ref[...] = dv_s[...].astype(BF16)


def small_sum(cid, vec):
    shape = vec.shape

    def kernel(v_ref, o_ref, acc, got, ss, rs):
        zs, yp, xp, cp = peers()
        bar = pltpu.get_barrier_semaphore()
        for dev in (*zs, yp, xp, cp):
            pl.semaphore_signal(bar, inc=1, device_id=(dev,), device_id_type=MESH)
        pl.semaphore_wait(bar, 6)
        sends = []
        for i, dev in enumerate((cp, xp, yp)):
            cur = v_ref if i == 0 else acc.at[i - 1]
            sends.append(remote(cur, got.at[i], ss.at[i], rs.at[i], dev))
            sends[-1].start()
            sends[-1].wait_recv()
            acc[i] = cur[...] + got[i]
        last = [remote(acc.at[2], got.at[3 + d], ss.at[3 + d], rs.at[3 + d], zs[d]) for d in range(3)]
        for s in last:
            s.start()
        total = acc[2]
        for d, s in enumerate(last):
            s.wait_recv()
            total = total + got[3 + d]
        o_ref[...] = total
        for s in sends + last:
            s.wait_send()

    vm = pl.BlockSpec(memory_space=pltpu.VMEM)
    return pl.pallas_call(kernel, in_specs=[vm], out_specs=vm, out_shape=sds(shape, F32),
                          scratch_shapes=[pltpu.VMEM((3,) + shape, F32), pltpu.VMEM((6,) + shape, F32),
                                          pltpu.SemaphoreType.DMA((6,)), pltpu.SemaphoreType.DMA((6,))],
                          compiler_params=pltpu.CompilerParams(collective_id=cid, has_side_effects=True), name='small_sum')(vec)


def row_map(i):
    return i, 0


def col_map(i):
    return 0, i


def rows_of(a, n):
    return a, (n, a.shape[1]), row_map


def cols_of(a, n):
    return a, (a.shape[0], n), col_map


def heads_of(a, n, off=0):
    return a, (n,) + a.shape[1:], lambda i: (i + off, 0, 0)


def whole(a):
    return a, a.shape, None


def put(ref, i, part):
    @pl.when(i == 0)
    def _():
        ref[...] = part

    @pl.when(i > 0)
    def _():
        ref[...] += part


def side_by_side(ref, n):
    return jnp.concatenate([ref[j] for j in range(n)], axis=1)


def local_step(x, ln1, wq, wo, ln2, wu, wd, dy, comm=True):
    seq, d = x.shape
    heads, hd, ft = 12, 128, 512
    ff, nq, per = wu.shape[1], 3 * d, SUB // hd
    scale = 1 / math.sqrt(hd)
    tm = tq = min(256, seq)
    nm, nf = seq // tm, ff // ft
    slopes = (alibi_slopes(heads), 'smem', None)
    b16 = lambda *shape: sds(shape, BF16)
    f32 = lambda *shape: sds(shape, F32)
    vm16 = lambda *shape: pltpu.VMEM(shape, BF16)
    vm32 = lambda *shape: pltpu.VMEM(shape, F32)
    act, wide, vec = b16(seq, d), b16(seq, ff), f32(1, d)
    one_vec = (vec, vec.shape, lambda i: (0, 0))
    band = lambda i: pl.ds(pl.multiple_of(i * tm, tm), tm)
    G = (lambda *w: [Gather(s, off) for s, off in w]) if comm else (lambda *w: [])
    flat = lambda full: full.reshape(-1, full.shape[-1])

    def S(*parts):
        if not comm:
            return []
        return [Scatter(a.reshape(4, 2, 2, 2, -1, a.shape[-1]), u0, n, off) for a, u0, n, off in parts]

    if comm:
        tile = jnp.pad(jnp.stack([ln1, ln2]), ((0, 6), (0, 128 - ln1.shape[0])))
        fq, lns = host('ag_qkv', 1, [], G((wq, 0)) + [GatherSmall(tile)])
        fq = flat(fq)
        w1, w2 = lns.reshape(-1, 8, 128)[:, :2, :ln1.shape[0]].transpose(1, 0, 2).reshape(2, 1, d)
    else:
        fq, w1, w2 = wq, ln1.reshape(1, d), ln2.reshape(1, d)

    def ln1_body(i, ins, outs, ext):
        (xr, lw), (ht,), (_, h1) = ins, outs, ext
        xhat, _ = norm_parts(xr[...].astype(F32))
        h = (xhat * lw[...]).astype(BF16)
        h1[band(i), :] = h
        ht[...] = h.T

    def qkv_body(i, ins, outs, ext):
        (w,), (o,), (qkv, h1) = ins, outs, ext
        r = dot(h1[...], w[...]).astype(BF16)
        for j in range(per):
            qkv[i * per + j] = r[:, j * hd:(j + 1) * hd]
            o[j] = r[:, j * hd:(j + 1) * hd]

    def attn_body(i, ins, outs, ext):
        (sl,), (o, l), (qkv, _) = ins, outs, ext
        attn_fwd(qkv.at[i], qkv.at[heads + i], qkv.at[2 * heads + i], o, l.at[0], sl[i], scale, tq)

    pb = [Phase(nm, [rows_of(x, tm), whole(w1)], [cols_of(b16(d, seq), tm)], ln1_body),
          Phase(nq // SUB, [cols_of(fq, SUB)], [heads_of(b16(3 * heads, seq, hd), per)], qkv_body),
          Phase(heads, [slopes], [cols_of(act, hd), heads_of(f32(heads, seq, 1), 1)], attn_body)]
    h1t, qkv, attn, lse, *full = host('attn_fwd', 2, pb, G((wo, 0), (wu, 2)), shared=[vm16(3 * heads, seq, hd), vm16(seq, d)])
    fo, fu = map(flat, full) if comm else (wo, wu)

    def out_body(i, ins, outs, ext):
        (xs, a, w, lw), (o, ht), (h2,) = ins, outs, ext
        x1 = (xs[...].astype(F32) + dot(a[...], w[...])).astype(BF16)
        o[...] = x1
        xhat, _ = norm_parts(x1.astype(F32))
        h = (xhat * lw[...]).astype(BF16)
        h2[band(i), :] = h
        ht[...] = h.T

    def up_body(i, ins, outs, ext):
        (w, dyr), (go, gpo, gd), (h2,) = ins, outs, ext
        u = dot(h2[...], w[...])
        cdf = 0.5 * (1.0 + lax.erf(u * math.sqrt(0.5)))
        g = (u * cdf).astype(BF16)
        go[...] = g
        gpo[...] = cdf + u * (jnp.exp(-0.5 * u * u) * math.sqrt(0.5 / math.pi))
        gd[...] = dot(g, dyr[...], 0, 0).astype(BF16)

    pc = [Phase(nm, [rows_of(x, tm), rows_of(attn, tm), whole(fo), whole(w2)], [rows_of(act, tm), cols_of(b16(d, seq), tm)], out_body),
          Phase(nf, [cols_of(fu, ft), whole(dy)], [cols_of(wide, ft), cols_of(f32(seq, ff), ft), rows_of(b16(ff, d), ft)], up_body)]
    x1, h2t, g, gp, g_down, *full = host('up', 3, pc, G((wd, 0)), shared=[vm16(seq, d)])
    fd, = map(flat, full) if comm else (wd,)

    def dup_body(i, ins, outs, ext):
        (dyr, w, gr, gpr, ht), (duo, gu), (acc,) = ins, outs, ext
        du = (dot(dyr[...], w[...], 1, 1) * gpr[...]).astype(BF16)
        duo[...] = du
        gu[...] = dot(ht[...], du).astype(BF16)
        put(acc, i, dot(gr[...], w[...]))

    def y_body(i, ins, outs, ext):
        (xr,), (o,), (acc,) = ins, outs, ext
        o[...] = (xr[...].astype(F32) + acc[band(i), :]).astype(BF16)

    pd = [Phase(nf, [whole(dy), rows_of(fd, ft), cols_of(g, ft), cols_of(gp, ft), whole(h2t)], [cols_of(wide, ft), cols_of(b16(d, ff), ft)], dup_body),
          Phase(nm, [rows_of(x1, tm)], [rows_of(act, tm)], y_body)]
    d_up, g_up, y, *r_down = host('dup', 4, pd, S((g_down, 0, 8, 0)), shared=[vm32(seq, d)])

    def dh2_body(i, ins, outs, ext):
        (du, w), (acc, _) = ins, ext
        put(acc, i, dot(du[...], w[...], 1, 1))

    def ln2b_body(i, ins, outs, ext):
        (xr, dyr, lw), (dmo, gwo), (acc, dmb) = ins, outs, ext
        dx, gw = norm_back(acc[band(i), :], xr[...].astype(F32), lw[...])
        dm = dyr[...].astype(F32) + dx
        dmo[...] = dm
        dmb[band(i), :] = dm.astype(BF16)
        put(gwo, i, gw)

    def dattn_body(i, ins, outs, ext):
        (w, a), (da, go), (_, dmb) = ins, outs, ext
        da[...] = dot(dmb[...], w[...], 1, 1).astype(BF16)
        go[...] = dot(a[...], dmb[...], 0, 0).astype(BF16)

    pe = [Phase(nf, [cols_of(d_up, ft), cols_of(fu, ft)], [], dh2_body),
          Phase(nm, [rows_of(x1, tm), rows_of(dy, tm), whole(w2)], [rows_of(f32(seq, d), tm), one_vec], ln2b_body),
          Phase(d // ft, [rows_of(fo, ft), cols_of(attn, ft)], [cols_of(act, ft), rows_of(b16(d, d), ft)], dattn_body)]
    d_mid, g_ln2, d_attn, g_out, *r_up0 = host('dh2', 5, pe, S((g_up, 0, 4, 0)), shared=[vm32(seq, d), vm16(seq, d)])

    def battn_body(i, ins, outs, ext):
        (q, k, v, a, da, l, sl), (o,), (dk, dv) = ins, outs, ext
        attn_bwd(q.at[0], k.at[0], v.at[0], a, da, l.at[0], *(o.at[j, 0] for j in range(3)), dk, dv, sl[i], scale, tq)

    pf = [Phase(heads, [*(heads_of(qkv, 1, j * heads) for j in range(3)), cols_of(attn, hd), cols_of(d_attn, hd), heads_of(lse, 1), slopes],
                [(b16(3, heads, seq, hd), (3, 1, seq, hd), lambda i: (0, i, 0, 0))], battn_body)]
    d_qkv, *r_up1 = host('attn_bwd', 6, pf, S((g_up, 4, 4, 0)), shared=[vm32(seq, hd), vm32(seq, hd)])
    d_qkv = d_qkv.reshape(3 * heads, seq, hd)

    def gqkv_body(i, ins, outs, ext):
        (ht, dq), (o,) = ins, outs
        o[...] = dot(ht[...], side_by_side(dq, per)).astype(BF16)

    g_qkv, = host('gqkv', 0, [Phase(nq // SUB, [whole(h1t), heads_of(d_qkv, per)], [cols_of(b16(d, nq), SUB)], gqkv_body)])

    def dh1_body(i, ins, outs, ext):
        (dq, w), (acc,) = ins, ext
        put(acc, i, dot(side_by_side(dq, per // 2), w[...], 1, 1))

    def ln1b_body(i, ins, outs, ext):
        (xr, dm, lw), (o, gwo), (acc,) = ins, outs, ext
        dx, gw = norm_back(acc[band(i), :], xr[...].astype(F32), lw[...])
        o[...] = (dm[...] + dx).astype(BF16)
        put(gwo, i, gw)

    ph = [Phase(nq // HALF, [heads_of(d_qkv, per // 2), cols_of(fq, HALF)], [], dh1_body),
          Phase(nm, [rows_of(x, tm), rows_of(d_mid, tm), whole(w1)], [rows_of(act, tm), one_vec], ln1b_body)]
    dx, g_ln1, *r_last = host('dh1', 7, ph, S((g_out, 0, 2, 0), (g_qkv, 0, 6, 2)), shared=[vm32(seq, d)])
    if comm:
        (g_down,), (g_out, g_qkv), g_up = r_down, r_last, jnp.concatenate(r_up0 + r_up1, axis=1)
    return y, dx, g_ln1, g_qkv, g_out, g_ln2, g_up, g_down


def solution(mesh):
    row_spec = P('fsdp')

    def step(x_in, ln1_w, w_qkv, w_out, ln2_w, w_up, w_down, dy_out):
        rows, _, heads, hd = w_qkv.shape
        d = x_in.shape[-1]
        y, dx, g_ln1, g_qkv, g_out, g_ln2, g_up, g_down = local_step(
            x_in[0], ln1_w, w_qkv.reshape(rows, -1), w_out, ln2_w, w_up, w_down, dy_out[0])
        sums = small_sum(8, jnp.concatenate([g_ln1, g_ln2, jnp.zeros((6, d), F32)], axis=0))
        mine = lax.dynamic_slice_in_dim(sums, lax.axis_index('fsdp') * rows, rows, axis=1)
        return (y[None], dx[None], mine[0], g_qkv.reshape(rows, 3, heads, hd), g_out, mine[1], g_up, g_down)

    return jax.shard_map(step, mesh=mesh, in_specs=(row_spec,) * 8, out_specs=(row_spec,) * 8, check_vma=False)
```

time: 1600 us -> 749 us (0.47)
  waiting for transfers between devices: 871 us -> 0 us
  Pallas kernels: 0 us -> 727 us
  matrix products: 540 us -> 0 us
  blocking collectives: 123 us -> 0 us
  other arithmetic: 37.2 us -> 4.81 us
    pallas_call x0 -> x9, Pallas kernels: none -> 727 us  [the longest x8 709 us: host(): pl.pallas_call(kernel, grid=(total,), in_specs=in_specs, out_specs=out_sp...]
    dot_general x17 -> x0, matrix products: 512 us -> none  [matmul(): return jnp.einsum(form, left, right, preferred_element_type=jnp.float32)]
    all_gather x8 -> x0, waiting for transfers between devices: 456 us -> none  [assemble(): lax.all_gather(shard, 'fsdp', axis=0, tiled=True)]
    reduce_scatter x4 -> x0, waiting for transfers between devices: 411 us -> none  [sum_rows_bf(): lax.psum_scatter(grad_full.astype(jnp.bfloat16), 'fsdp', scatter_dimensio...]
    unnamed x3 -> x0, blocking collectives: 123 us -> none
    sub x1 -> x0, matrix products: 27.7 us -> none  [forward_local(): attn_probs = jax.nn.softmax(scores, axis=-1)]
    convert_element_type x6 -> x0, other arithmetic: 18.7 us -> none  [the longest x1 8.11 us: backward_local(): dx_in = (d_mid + d_x_ln).astype(jnp.bfloat16)]
  transfers between devices with their start and end apart: 12 -> 0, of which waited for: 10 -> 0; matrix products, arithmetic and copies ran while one was open for 35% -> 0% of each run, Pallas kernels for 0% -> 0%
where the time goes in v1:
time: 749 us
  Pallas kernels  727 us (97%)
  local copies, waits for them, and re-layouts  15.8 us (2%)
    pallas_call x8, Pallas kernels, host(): pl.pallas_call(kernel, grid=(total,), in_specs=in_specs, out_specs=out_sp...  709 us
    pallas_call x1, Pallas kernels, small_sum(): pl.pallas_call(kernel, in_specs=[vm], out_specs=vm, out_shape=sds(shape,...  18.1 us

profile of v1, /device:TPU:0, one launch (start us, length us, event | category | flops | bytes accessed | tf_op | source)
XLA Modules:
  0.0 748.5 jit_solution(16112849189269204157)
XLA Ops:
  0.6 1.2 copy.20
  1.8 1.1 reshape.58.refs_0_
  2.9 1.3 select_maximum_fusion.refs_1_
  4.1 95.0 %ag_qkv.1 = (bf16[4,2,2,2,48,4608]{5,4,3,2,1,0:T(8,128)(2,1)}, f32[4,2,2,2,8,128]{5,4,3,2,1,0:T(8,128)}) custom-call(bf16[48,4608]{1,0:T(8,128)(2,1)} %reshape.58.refs_0_, f32[8,128]{1,0:T(8,128)} %select_maximum_fusion.refs_1_), custom_call_target="tpu_custom_call" | custom-call | flops 20000000000 | bytes 30000000 | tf_op jit(solution)/shard_map/ag_qkv/pallas_call | solution.py:354
  99.1 0.9 slice.14
  100.1 0.7 unstack.13.refs_1_.refs_4_
  100.7 123.5 %attn_fwd.1 = (bf16[1536,1024]{1,0:T(8,128)(2,1)}, bf16[36,1024,128]{2,1,0:T(8,128)(2,1)}, bf16[1024,1536]{1,0:T(8,128)(2,1)}, f32[12,1024,1]{2,1,0:T(8,128)}, b...) custom-call(bf16[1024,1536]{1,0:T(8,128)(2,1)} %bitcast.36, ...), custom_call_target="tpu_custom_call" | custom-call | flops 20000000000 | bytes 30000000 | tf_op jit(solution)/shard_map/attn_fwd/pallas_call | solution.py:354
  224.2 0.7 unstack.15.refs_3_.refs_4_
  224.9 115.3 %up.1 = (bf16[1024,1536]{1,0:T(8,128)(2,1)}, bf16[1536,1024]{1,0:T(8,128)(2,1)}, bf16[1024,6144]{1,0:T(8,128)(2,1)}, f32[1024,6144]{1,0:T(8,128)}, bf16[6144,153...) custom-call(bf16[1024,1536]{1,0:T(8,128)(2,1)} %bitcast.37, ...), custom_call_target="tpu_custom_call" | custom-call | flops 20000000000 | bytes 30000000 | tf_op jit(solution)/shard_map/up/pallas_call | solution.py:354
  340.2 121.2 %dup.1 = (bf16[1024,6144]{1,0:T(8,128)(2,1)}, bf16[1536,6144]{1,0:T(8,128)(2,1)}, bf16[1024,1536]{1,0:T(8,128)(2,1)}, f32[192,1536]{1,0:T(8,128)}) custom-call(bf16[1024,1536]{1,0:T(8,128)(2,1)} %bitcast.28, bf16[6144,1536]{1,0:T(8,128)(2,1)} %bitcast.24, bf16[1024,6144]{1,0:T(8,128)(2,1)} %get-tuple-element.43.refs_2_, ...), custom_call_target="tpu_custom_call" | custom-call | flops 20000000000 | bytes 30000000 | tf_op jit(solution)/shard_map/dup/pallas_call | solution.py:354
  461.4 72.3 %dh2.1 = (f32[1024,1536]{1,0:T(8,128)}, f32[1,1536]{1,0:T(1,128)}, bf16[1024,1536]{1,0:T(8,128)(2,1)}, bf16[1536,1536]{1,0:T(8,128)(2,1)}, f32[48,3072]{1,0:T(8,128)}) custom-call(bf16[1024,6144]{1,0:T(8,128)(2,1)} %get-tuple-element.50.refs_0_, bf16[1536,6144]{1,0:T(8,128)(2,1)} %bitcast.40, bf16[1024,1536]{1,0:T(8,128)(2,1)} %get-tuple-element.46.refs_5_.refs_2_, ...), custom_call_target="tpu_custom_call" | custom-call | flops 20000000000 | bytes 30000000 | tf_op jit(solution)/shard_map/dh2/pallas_call | solution.py:354
  533.7 0.0 copy-start.2
  533.7 62.1 %attn_bwd.1 = (bf16[3,12,1024,128]{3,2,1,0:T(8,128)(2,1)}, f32[48,3072]{1,0:T(8,128)}) custom-call(bf16[36,1024,128]{2,1,0:T(8,128)(2,1)} %get-tuple-element.49.refs_0_.refs_1_.refs_2_, bf16[36,1024,128]{2,1,0:T(8,128)(2,1)} %get-tuple-element.49.refs_0_.refs_1_.refs_2_, bf16[36,1024,128]{2,1,0:T(8,128)(2,1)} %get-tuple-element.49.refs_0_.refs_1_.refs_2_, ...), custom_call_target="tpu_custom_call" | custom-call | flops 20000000000 | bytes 30000000 | tf_op jit(solution)/shard_map/attn_bwd/pallas_call | solution.py:354
  595.8 0.0 copy-done.2
  595.8 2.2 pad_maximum_fusion
  598.0 19.7 %gqkv.1 = bf16[1536,4608]{1,0:T(8,128)(2,1)} custom-call(bf16[1536,1024]{1,0:T(8,128)(2,1)} %get-tuple-element.57.refs_0_, bf16[36,1024,128]{2,1,0:T(8,128)(2,1)} %bitcast.44), custom_call_target="tpu_custom_call" | custom-call | flops 20000000000 | bytes 30000000 | tf_op jit(solution)/shard_map/gqkv/pallas_call | solution.py:354
  617.7 100.0 %dh1.1 = (bf16[1024,1536]{1,0:T(8,128)(2,1)}, f32[1,1536]{1,0:T(1,128)}, f32[48,1536]{1,0:T(8,128)}, f32[48,4608]{1,0:T(8,128)}) custom-call(bf16[36,1024,128]{2,1,0:T(8,128)(2,1)} %bitcast.45, bf16[1536,4608]{1,0:T(8,128)(2,1)} %bitcast.42, bf16[1024,1536]{1,0:T(8,128)(2,1)} %bitcast.38, f32[1024,1536]{1,0:T(8,128)} %get-tuple-element.55.refs_3_, ...), custom_call_target="tpu_custom_call" | custom-call | flops 20000000000 | bytes 30000000 | tf_op jit(solution)/shard_map/dh1/pallas_call | solution.py:354
  717.7 0.1 pad.9.clone
  717.8 0.0 copy-done.4
  717.8 1.4 maximum_maximum_fusion.v_ref
  719.2 18.1 %small_sum.1 = f32[8,1536]{1,0:T(8,128)} custom-call(f32[8,1536]{1,0:T(8,128)} %maximum_maximum_fusion.v_ref), custom_call_target="tpu_custom_call" | custom-call | tf_op jit(solution)/shard_map/small_sum/pallas_call | solution.py:474
  737.4 0.8 constant_dynamic-slice_fusion
  738.1 0.5 slice_bitcast_fusion
  738.7 1.3 reshape.69
  740.0 1.2 copy.22
  741.2 3.9 copy.30
  745.1 0.0 copy-done
  745.1 1.7 copy.31
  746.8 0.0 copy-done.3
  746.8 0.7 copy.32
  747.5 0.1 copy-done.1
  747.5 1.0 copy.33
  (7 shorter events, 0.0 us)
Async XLA Ops:
  533.7 62.1 %copy-start.2 = (f32[48,3072]{1,0:T(8,128)S(1)}, f32[48,3072]{1,0:T(8,128)}, u32[]{:S(2)}) copy-start(f32[48,3072]{1,0:T(8,128)} %get-tuple-element.63) | copy-start | bytes 1769476
  617.7 100.1 %copy-start.4 = (f32[1,1536]{1,0:T(1,128)S(1)}, f32[1,1536]{1,0:T(1,128)}, u32[]{:S(2)}) copy-start(f32[1,1536]{1,0:T(1,128)} %get-tuple-element.60) | copy-start | bytes 18436
  741.2 3.9 copy-start
  745.1 1.7 copy-start.3
  745.1 2.4 copy-start.1

commit v2 on v1

v2 whole, which is shorter than its diff:
```python
import functools
import math

import jax
import jax.numpy as jnp
from jax import lax
from jax.experimental import pallas as pl
from jax.experimental.pallas import tpu as pltpu
from jax.sharding import PartitionSpec as P

EPS = 1e-5
SUB = 512
HALF = SUB // 2
LEAD = 3
RB = 48
F32, BF16 = jnp.float32, jnp.bfloat16
VMEM_LIMIT = 62 * 1024 * 1024
MESH = pl.DeviceIdType.MESH
HBM = pltpu.MemorySpace.HBM
CHIPS = (4, 2, 2)


def sds(shape, dtype):
    return jax.ShapeDtypeStruct(shape, dtype)


def dot(a, b, ca=1, cb=0):
    return lax.dot_general(a, b, (((ca,), (cb,)), ((), ())), preferred_element_type=F32)


def dot_t(a, b):
    return dot(a, b, 1, 1)


def t_dot(a, b):
    return dot(a, b, 0, 0)


def over_rows(f):
    return functools.partial(f, axis=-1, keepdims=True)


row_sum, row_max, row_mean = map(over_rows, (jnp.sum, jnp.max, jnp.mean))


def clip(t, n):
    return jnp.minimum(jnp.maximum(t, 0), n - 1)


class Phase:
    def __init__(self, n, ins, outs, body):
        self.n, self.ins, self.outs, self.body = n, ins, outs, body


def quot(a, b):
    return a // b if isinstance(a, int) else lax.div(a, b)


def rest(a, b):
    return a % b if isinstance(a, int) else lax.rem(a, b)


HERE = {}


def locate():
    me = lax.axis_index('fsdp')
    z, y, x, c = quot(me, 8), rest(quot(me, 4), 2), rest(quot(me, 2), 2), rest(me, 2)
    HERE.update(coords=(me, z, y, x, c), peers=([rest(me + 8 * d, 32) for d in (1, 2, 3)], me + 4 - 8 * y, me + 2 - 4 * x, me + 1 - 2 * c),
                zs=[rest(z + d, 4) for d in (1, 2, 3)])


def coords():
    return HERE['coords']


def peers():
    return HERE['peers']


def remote(src, dst, ssem, rsem, dev):
    return pltpu.make_async_remote_copy(src_ref=src, dst_ref=dst, send_sem=ssem, recv_sem=rsem, device_id=(dev,), device_id_type=MESH)


class Unit:
    def __init__(self, rows, cols):
        self.nc, self.nr = cols // SUB, rows // RB
        self.count = self.nc * self.nr

    def at(self, u, half=None):
        col = pl.multiple_of(rest(u, self.nc) * SUB, HALF)
        width = SUB
        if half is not None:
            col, width = pl.multiple_of(col + half * HALF, HALF), HALF
        rows = slice(None) if self.nr == 1 else pl.ds(pl.multiple_of(quot(u, self.nc) * RB, 16), RB)
        return rows, pl.ds(col, width)


class Gather:
    def __init__(self, weights, k0, k1):
        self.k0, self.k1 = k0, k1
        self.k = k1 - k0 + 1
        self.z0 = k0 + LEAD if k0 else 0
        self.z1 = k1 + LEAD
        self.w, self.ins, self.outs, self.alias = [], [], [], []
        for shard, full, first in weights:
            unit = Unit(*shard.shape)
            self.w.append((len(self.ins), unit, first, first + unit.count, full is None))
            self.ins.append((shard, pl.BlockSpec(memory_space=pltpu.VMEM)))
            if full is not None:
                self.alias.append((len(self.ins), len(self.outs)))
                self.ins.append((full, pl.BlockSpec(memory_space=HBM)))
            self.outs.append((sds(CHIPS + (2,) + shard.shape, BF16), pl.BlockSpec(memory_space=HBM)))
        self.base = max(k0 - 2, 0)
        n = self.z1 - self.base
        self.scratch = [pltpu.SemaphoreType.DMA((n, 8)), pltpu.SemaphoreType.DMA((n, 8)), pltpu.SemaphoreType.DMA((len(weights),))]

    def copies(self, stage, w, u, refs):
        i, unit, first, _, _ = self.w[w]
        shard, full = refs[i], refs[len(self.ins) + w]
        sems = lambda i: (refs[-3].at[u - self.base, i], refs[-2].at[u - self.base, i])
        me, z, y, x, c = coords()
        zs, yp, xp, cp = peers()
        r, q = unit.at(u - first)
        if stage == 0:
            return [remote(shard.at[r, q], full.at[z, y, x, c, r, q], *sems(d), zs[d]) for d in range(3)]
        if stage == 3:
            v = full.at[:, :, :, c, r, q]
            return [remote(v, v, *sems(7), cp)]
        out = []
        for half in range(2):
            r, q = unit.at(u - first, half)
            j = 2 * stage + 1 + half
            if stage == 1:
                v = full.at[:, y, x, c, r, q]
            else:
                v = full.at[:, y, :, c, r, q] if half else full.at[:, :, x, c, r, q]
            out.append(remote(v, v, *sems(j), xp if half == stage % 2 else yp))
        return out

    def each(self, lo, hi, u, fn):
        for w, (_, _, first, last, _) in enumerate(self.w):
            a, b = max(lo, first), min(hi, last)
            if a < b:
                if u is None:
                    pl.loop(a, b)(functools.partial(fn, w))
                else:
                    pl.when((u >= a) & (u < b))(functools.partial(fn, w, u))

    def go(self, stage, w, u, refs):
        for cp in self.copies(stage, w, u, refs):
            cp.start()

    def arrive(self, stage, w, u, refs):
        for cp in self.copies(stage, w, u, refs):
            cp.wait_recv()

    def left(self, stage, w, u, refs):
        for cp in self.copies(stage, w, u, refs):
            cp.wait_send()

    def step(self, k, fire, refs):
        me, z, y, x, c = coords()
        k0, k1, k = self.k0, self.k1, k + self.k0
        span = [(self.z0, self.z1), (k0, k1), (max(k0 - 1, 0), k1 - 1), (max(k0 - 2, 0), k1 - 2)]

        @pl.when(fire & (k == k0))
        def _():
            own = [pltpu.make_async_copy(refs[i], refs[len(self.ins) + w].at[z, y, x, c], refs[-1].at[w])
                   for w, (i, _, _, _, fresh) in enumerate(self.w) if fresh]
            for cp in own:
                cp.start()
            if k0 == 0:
                self.each(0, LEAD, None, lambda w, u: self.go(0, w, u, refs))
            for cp in own:
                cp.wait()

        @pl.when(fire & (k < k1))
        def _():
            self.each(*span[0], k + LEAD, lambda w, u: self.go(0, w, u, refs))
            for stage in (1, 2, 3):
                u = k + 1 - stage
                lo, hi = span[stage - 1]
                self.each(lo, hi, u, lambda w, u: self.arrive(stage - 1, w, u, refs))
                self.each(*span[stage], u, lambda w, u: self.go(stage, w, u, refs))

        @pl.when(fire & (k == k1))
        def _():
            for stage in range(4):
                lo, hi = span[stage]
                self.each(max(lo, k1 - stage) if stage < 3 else lo, hi, None, lambda w, u: self.arrive(stage, w, u, refs))
                self.each(lo, hi, None, lambda w, u: self.left(stage, w, u, refs))


class GatherSmall:
    def __init__(self, tile):
        self.k, self.alias = 5, []
        self.ins = [(tile, pl.BlockSpec(memory_space=pltpu.VMEM))]
        self.outs = [(sds(CHIPS + (2,) + tile.shape, F32), pl.BlockSpec(memory_space=HBM))]
        self.scratch = [pltpu.SemaphoreType.DMA((6,)), pltpu.SemaphoreType.DMA((6,)), pltpu.SemaphoreType.DMA]

    def copies(self, stage, refs):
        tile, full, ss, rs, _ = refs
        me, z, y, x, c = coords()
        zs, yp, xp, cp = peers()
        if stage == 0:
            return [remote(tile, full.at[z, y, x, c], ss.at[d], rs.at[d], zs[d]) for d in range(3)]
        v, dev = ((full.at[:, y, x, c], yp), (full.at[:, :, x, c], xp), (full.at[:, :, :, c], cp))[stage - 1]
        return [remote(v, v, ss.at[2 + stage], rs.at[2 + stage], dev)]

    def step(self, k, fire, refs):
        tile, full, ss, rs, ls = refs
        me, z, y, x, c = coords()
        for stage in range(5):
            @pl.when(fire & (k == stage))
            def _(stage=stage):
                if stage == 0:
                    own = pltpu.make_async_copy(tile, full.at[z, y, x, c], ls)
                    own.start()
                else:
                    for cp in self.copies(stage - 1, refs):
                        cp.wait_recv()
                if stage < 4:
                    for cp in self.copies(stage, refs):
                        cp.start()
                else:
                    for st in range(4):
                        for cp in self.copies(st, refs):
                            cp.wait_send()
                if stage == 0:
                    own.wait()


class Scatter:
    def __init__(self, grads, carry=None, last=False):
        self.last, self.carried = last, carry is not None
        self.parts, self.ins, n = [], [], 0
        for g, u0, m in grads:
            self.parts.append((n, n + m, u0, Unit(*g.shape[-2:])))
            self.ins.append((g, pl.BlockSpec(memory_space=HBM)))
            n += m
        self.n = n
        self.first = 0 if self.carried else 2
        self.done = n + (2 if last else 0)
        self.k = n + (3 if last else 1)
        self.two_shape, self.three_shape = (2, 4, 2, RB, HALF), (4, RB, SUB)
        if self.carried:
            self.ins += [(a, pl.BlockSpec(memory_space=pltpu.VMEM)) for a in carry]
        self.scratch = [
            pltpu.VMEM((n, *CHIPS, RB, SUB), BF16),
            pltpu.VMEM((2, *CHIPS, RB, SUB), BF16),
            pltpu.VMEM((n + 2,) + self.two_shape, BF16),
            pltpu.VMEM((n + 2,) + self.three_shape, BF16),
            pltpu.VMEM((n + 2, 3, RB, SUB), BF16),
            pltpu.SemaphoreType.DMA((n + 2, 8)), pltpu.SemaphoreType.DMA((n + 2, 8)), pltpu.SemaphoreType.DMA((2,))]
        self.alias = []

    def out_spec(self, kmap):
        lo, count = self.first, self.done - self.first
        self.outs = [(sds((count, RB, SUB), F32), pl.BlockSpec((1, RB, SUB), lambda t: (clip(kmap(t) - 1 - lo, count), 0, 0)))]
        if not self.last:
            self.outs += [(sds(shape, BF16), pl.BlockSpec(memory_space=pltpu.VMEM)) for shape in (self.two_shape, self.three_shape)]

    def source(self, j, refs, fn):
        for i, (a, b, u0, unit) in enumerate(self.parts):
            if len(self.parts) == 1:
                fn(refs[i], *unit.at(u0 + j - 2))
            else:
                pl.when((j - 2 >= a) & (j - 2 < b))(lambda: fn(refs[i], *unit.at(u0 + j - 2 - a)))

    def bufs(self, refs):
        return refs[len(self.ins) + len(self.outs):]

    def local(self, j, refs, act):
        me, z, y, x, c = coords()
        own, ls = self.bufs(refs)[1], self.bufs(refs)[-1]
        slot = rest(j, 2)
        self.source(j, refs, lambda g, r, q: act(pltpu.make_async_copy(g.at[:, :, :, c, r, q], own.at[slot], ls.at[slot])))

    def swap(self, j, refs, act):
        me, z, y, x, c = coords()
        got, ss, rs = self.bufs(refs)[0], *self.bufs(refs)[-3:-1]
        cp = peers()[-1]
        self.source(j, refs, lambda g, r, q: act(remote(g.at[:, :, :, 1 - c, r, q], got.at[j - 2], ss.at[j, 0], rs.at[j, 0], cp)))

    def copies(self, stage, j, refs):
        got, own, two, three, four, ss, rs, ls = self.bufs(refs)
        me, z, y, x, c = coords()
        zs, yp, xp, cp = peers()
        a, b = pl.ds(0, HALF), pl.ds(HALF, HALF)
        if stage == 1:
            pairs = [(got.at[j - 2, :, 1 - y, :, :, a], two.at[j, 0], yp), (got.at[j - 2, :, :, 1 - x, :, b], two.at[j, 1], xp)]
        elif stage == 2:
            pairs = [(two.at[j, 0, :, 1 - x], three.at[j, :, :, a], xp), (two.at[j, 1, :, 1 - y], three.at[j, :, :, b], yp)]
        else:
            pairs = [(three.at[j, HERE['zs'][d]], four.at[j, d], zs[d]) for d in range(3)]
        return [remote(src, dst, ss.at[j, 2 * stage + i - 1], rs.at[j, 2 * stage + i - 1], dev) for i, (src, dst, dev) in enumerate(pairs)]

    def add(self, stage, j, refs):
        got, own, two, three, four, ss, rs, ls = self.bufs(refs)
        me, z, y, x, c = coords()
        a, b = pl.ds(0, HALF), pl.ds(HALF, HALF)
        slot = rest(j, 2)
        if stage == 1:
            @pl.loop(0, 4)
            def _(zz):
                for yy in range(2):
                    for xx in range(2):
                        got[j - 2, zz, yy, xx] += own[slot, zz, yy, xx]
        elif stage == 2:
            @pl.loop(0, 4)
            def _(zz):
                for i in range(2):
                    two[j, 0, zz, i] += got[j - 2, zz, y, i, :, a]
                    two[j, 1, zz, i] += got[j - 2, zz, i, x, :, b]
        elif stage == 3:
            for zz in range(4):
                three[j, zz, :, a] += two[j, 0, zz, x]
                three[j, zz, :, b] += two[j, 1, zz, y]
        else:
            total = three[j, z].astype(F32)
            for d in range(3):
                total += four[j, d].astype(F32)
            refs[len(self.ins)][0] = total

    def step(self, k, fire, refs):
        n, last = self.n, self.last
        got, own, two, three, four, ss, rs, ls = self.bufs(refs)
        start = lambda cp: cp.start()

        def go(stage, j):
            for cp in self.copies(stage, j, refs):
                cp.start()

        @pl.when(fire & (k == 0))
        def _():
            if self.carried:
                two[1] = refs[len(self.ins) - 2][...]
                three[0] = refs[len(self.ins) - 1][...]
                go(2, 1)
                go(3, 0)

            @pl.loop(2, n + 2)
            def _(j):
                self.swap(j, refs, start)

            for j in range(2, min(4, n + 2)):
                self.local(j, refs, start)

        for stage in (1, 2, 3, 4):
            j = k + 3 - stage
            low = (2, 2, 1, 0)[stage - 1] if self.carried else 2

            @pl.when(fire & (j >= low) & (j < n + 2))
            def _(stage=stage, j=j):
                if stage == 1:
                    self.swap(j, refs, lambda cp: cp.wait_recv())
                    self.local(j, refs, lambda cp: cp.wait())
                else:
                    for cp in self.copies(stage - 1, j, refs):
                        cp.wait_recv()
                self.add(stage, j, refs)
                if stage < 4:
                    if last or stage == 1:
                        go(stage, j)
                    else:
                        pl.when(k < n)(lambda: go(stage, j))
                if stage == 1:
                    pl.when(j < n)(lambda: self.local(j + 2, refs, start))

        @pl.when(fire & (k == self.k - 1))
        def _():
            for stage in (1, 2, 3):
                low = (2, 1, 0)[stage - 1] if self.carried else 2
                high = n + 2 if last else n + 3 - stage

                @pl.loop(low, high)
                def _(j):
                    for cp in self.copies(stage, j, refs):
                        cp.wait_send()

            @pl.loop(2, n + 2)
            def _(j):
                self.swap(j, refs, lambda cp: cp.wait_send())

            if not last:
                refs[len(self.ins) + 1][...] = two[n + 1]
                refs[len(self.ins) + 2][...] = three[n]


class SmallSum:
    def __init__(self, row, t0, d):
        self.t0, self.k = t0, 1
        self.ins = [(row, pl.BlockSpec(memory_space=pltpu.VMEM))]
        self.outs = [(sds((8, d), F32), pl.BlockSpec(memory_space=pltpu.VMEM))]
        self.alias = []
        self.scratch = [pltpu.VMEM((4, 8, d), F32), pltpu.VMEM((6, 8, d), F32), pltpu.SemaphoreType.DMA((6,)), pltpu.SemaphoreType.DMA((6,))]

    def run(self, t, mine, refs):
        row, out, acc, got, ss, rs = refs
        zs, yp, xp, cp = peers()
        near = (cp, xp, yp, *zs)
        n = len(near) - len(zs)
        copies = [remote(acc.at[min(i, n)], got.at[i], ss.at[i], rs.at[i], dev) for i, dev in enumerate(near)]

        for i in range(n + 2):
            @pl.when(t == self.t0 + i)
            def _(i=i):
                if not i:
                    acc[i] = jnp.zeros_like(acc[i])
                    acc[i, pl.ds(0, 1)] = mine[...]
                    acc[i, pl.ds(1, 1)] = row[...]
                elif i <= n:
                    copies[i - 1].wait_recv()
                    acc[i] = acc[i - 1] + got[i - 1]
                else:
                    total = acc[n]
                    for j in range(n, len(near)):
                        copies[j].wait_recv()
                        total += got[j]
                    out[...] = total
                    for copy in copies:
                        copy.wait_send()
                for copy in copies[i:i + 1] if i < n else copies[n:] if i == n else ():
                    copy.start()


def host(name, cid, phases, comms=(), shared=(), cost=None):
    k_all = max([c.k for c in comms], default=1)
    at = 0
    for p in phases:
        p.at = at
        at = at + p.n
    small = [c for c in comms if isinstance(c, SmallSum)]
    total = max(at + 5 * len(small), k_all)
    kmap = lambda t: t if total == k_all else quot(t * (k_all - 1), total - 1)
    ins, in_specs, outs, out_specs, scratch, alias, resident = [], [], [], [], [], {}, []
    for p in phases:
        for arr, block, index in p.ins:
            if block == 'smem':
                in_specs.append(pl.BlockSpec(memory_space=pltpu.SMEM))
            elif index is None:
                resident.append((len(ins), p.at))
                in_specs.append(pl.BlockSpec(memory_space=HBM))
            else:
                in_specs.append(pl.BlockSpec(block, functools.partial(lambda p, f, t: f(clip(t - p.at, p.n)), p, index)))
            ins.append(arr)
        for shape, block, index in p.outs:
            outs.append(shape)
            out_specs.append(pl.BlockSpec(block, functools.partial(lambda p, f, t: f(clip(t - p.at, p.n)), p, index)))
    for c in comms:
        if isinstance(c, Scatter):
            c.out_spec(kmap)
        alias.update({len(ins) + i: len(outs) + o for i, o in c.alias})
        for arr, spec in c.ins:
            ins.append(arr)
            in_specs.append(spec)
        for shape, spec in c.outs:
            outs.append(shape)
            out_specs.append(spec)
        scratch += c.scratch
    scratch += [pltpu.VMEM(ins[i].shape, ins[i].dtype) for i, _ in resident] + [pltpu.SemaphoreType.DMA((max(len(resident), 1),))]
    scratch += list(shared)

    def kernel(*refs):
        refs = list(refs)
        rin, rout, rscr = refs[:len(ins)], refs[len(ins):len(ins) + len(outs)], refs[len(ins) + len(outs):]
        t = pl.program_id(0)
        if comms:
            locate()

            @pl.when(t == 0)
            def _():
                zs, yp, xp, cp = peers()
                near = (*zs, yp, xp, cp)
                bar = pltpu.get_barrier_semaphore()
                for dev in near:
                    pl.semaphore_signal(bar, inc=1, device_id=(dev,), device_id_type=MESH)
                pl.semaphore_wait(bar, len(near))
        i, o, s = sum(len(p.ins) for p in phases), sum(len(p.outs) for p in phases), 0
        k = kmap(t)
        fire = (t == 0) | (k != kmap(jnp.maximum(t - 1, 0)))
        for c in comms:
            ni, no, ns = len(c.ins), len(c.outs), len(c.scratch)
            crefs = rin[i:i + ni] + rout[o:o + no] + rscr[s:s + ns]
            if c in small:
                small_refs = crefs
            else:
                c.step(k, fire, crefs)
            i, o, s = i + ni, o + no, s + ns
        held, rsem, extra = rscr[s:s + len(resident)], rscr[s + len(resident)], rscr[s + len(resident) + 1:]
        loads = [(pltpu.make_async_copy(rin[i], h, rsem.at[n]), at) for n, ((i, at), h) in enumerate(zip(resident, held))]
        if loads:
            @pl.when(t == 0)
            def _():
                for cp, _ in loads:
                    cp.start()
        for cp, at in loads:
            pl.when(t == at)(cp.wait)
        for (i, _), h in zip(resident, held):
            rin[i] = h
        i = o = 0
        for p in phases:
            pi, po = rin[i:i + len(p.ins)], rout[o:o + len(p.outs)]
            i, o = i + len(p.ins), o + len(p.outs)

            @pl.when((t >= p.at) & (t < p.at + p.n))
            def _(p=p, pi=pi, po=po):
                p.body(t - p.at, pi, po, extra)

        for c in small:
            c.run(t, rout[o - 1], small_refs)

    params = dict(dimension_semantics=("arbitrary",), vmem_limit_bytes=VMEM_LIMIT)
    if comms:
        params.update(collective_id=cid, has_side_effects=True)
    got = pl.pallas_call(kernel, grid=(total,), in_specs=in_specs, out_specs=out_specs, out_shape=outs, scratch_shapes=scratch,
                         input_output_aliases=alias, compiler_params=pltpu.CompilerParams(**params), name=name,
                         cost_estimate=pl.CostEstimate(flops=2 ** 34, bytes_accessed=2 ** 25, transcendentals=0))(*ins)
    return list(got)


def norm_parts(t):
    mean = row_mean(t)
    cen = t - mean
    rstd = lax.rsqrt(row_mean(cen * cen) + EPS)
    return cen * rstd, rstd


def norm_back(d, t, w):
    xhat, rstd = norm_parts(t)
    dh = d * w
    m1 = row_mean(dh)
    m2 = row_mean(dh * xhat)
    return rstd * (dh - m1 - xhat * m2), jnp.sum(d * xhat, axis=0, keepdims=True)


def alibi_slopes(n_heads):
    padded = 2 ** math.ceil(math.log2(n_heads))
    base = [2.0 ** (-8.0 * (k + 1) / padded) for k in range(padded)]
    ordered = base if padded == n_heads else base[1::2] + base[0::2]
    return jnp.array(ordered[:n_heads], dtype=F32)


def causal(i, tq, slope):
    row = lax.broadcasted_iota(jnp.int32, (tq, tq), 0)
    col = lax.broadcasted_iota(jnp.int32, (tq, tq), 1)
    rel = (row - col).astype(F32)
    diag = slope * rel
    past = None
    if i:
        r = lax.broadcasted_iota(jnp.int32, (tq, i * tq), 0) + i * tq
        q = lax.broadcasted_iota(jnp.int32, (tq, i * tq), 1)
        past = slope * (r - q).astype(F32)
    return past, diag, row >= col


def attn_fwd(q_ref, k_ref, v_ref, o_ref, l_ref, slope, scale, tq):
    n = q_ref.shape[0] // tq
    for i in range(n):
        rows, before = pl.ds(i * tq, tq), pl.ds(0, i * tq)
        q = q_ref[rows]
        past, diag, keep = causal(i, tq, slope)
        sd = jnp.where(keep, dot_t(q, k_ref[rows]) * scale - diag, -jnp.inf)
        m = row_max(sd)
        if i:
            sp = dot_t(q, k_ref[before]) * scale - past
            m = jnp.maximum(m, row_max(sp))
            ep = jnp.exp(sp - m)
        ed = jnp.exp(sd - m)
        l = row_sum(ed)
        if i:
            l = l + row_sum(ep)
        inv = 1.0 / l
        o = dot((ed * inv).astype(BF16), v_ref[rows])
        if i:
            o = o + dot((ep * inv).astype(BF16), v_ref[before])
        o_ref[rows] = o.astype(BF16)
        l_ref[rows] = m + jnp.log(l)


def attn_bwd(q_ref, k_ref, v_ref, a_ref, da_ref, l_ref, dq_ref, dk_ref, dv_ref, dk_s, dv_s, slope, scale, tq):
    n = q_ref.shape[0] // tq
    dk_s[...] = jnp.zeros_like(dk_s)
    dv_s[...] = jnp.zeros_like(dv_s)
    for i in range(n):
        rows, before = pl.ds(i * tq, tq), pl.ds(0, i * tq)
        q, da = q_ref[rows], da_ref[rows]
        lse = l_ref[rows]
        delta = row_sum(da.astype(F32) * a_ref[rows].astype(F32))
        past, diag, keep = causal(i, tq, slope)
        dq = None
        for own in ((True,) if i == 0 else (True, False)):
            keys = rows if own else before
            kk, vv = k_ref[keys], v_ref[keys]
            s = dot_t(q, kk) * scale - (diag if own else past)
            p = jnp.exp(s - lse)
            if own:
                p = jnp.where(keep, p, 0.0)
            ds = (p * (dot_t(da, vv) - delta) * scale).astype(BF16)
            dv_s[keys] += t_dot(p.astype(BF16), da)
            dk_s[keys] += t_dot(ds, q)
            part = dot(ds, kk)
            dq = part if dq is None else dq + part
        dq_ref[rows] = dq.astype(BF16)
    dk_ref[...] = dk_s[...].astype(BF16)
    dv_ref[...] = dv_s[...].astype(BF16)


def row_map(i):
    return i, 0


def col_map(i):
    return 0, i


def rows_of(a, n):
    return a, (n, a.shape[1]), row_map


def cols_of(a, n):
    return a, (a.shape[0], n), col_map


def heads_of(a, n, off=0):
    return a, (n,) + a.shape[1:], lambda i: (i + off, 0, 0)


def whole(a):
    return a, a.shape, None


def put(ref, i, part):
    @pl.when(i == 0)
    def _():
        ref[...] = part

    @pl.when(i > 0)
    def _():
        ref[...] += part


def side_by_side(ref, n):
    return jnp.concatenate([ref[j] for j in range(n)], axis=1)


def local_step(x, ln1, wq, wo, ln2, wu, wd, dy, comm=True):
    seq, d = x.shape
    heads, hd, ft = 12, 128, 512
    ff, nq, per = wu.shape[1], 3 * d, SUB // hd
    scale = 1 / math.sqrt(hd)
    tq = min(256, seq)
    tm = tq // 2
    nm, nf = seq // tm, ff // ft
    slopes = (alibi_slopes(heads), 'smem', None)
    b16 = lambda *shape: sds(shape, BF16)
    f32 = lambda *shape: sds(shape, F32)
    vm16 = lambda *shape: pltpu.VMEM(shape, BF16)
    vm32 = lambda *shape: pltpu.VMEM(shape, F32)
    act, wide, vec = b16(seq, d), b16(seq, ff), f32(1, d)
    one_vec = (vec, vec.shape, lambda i: (0, 0))
    band = lambda i: pl.ds(pl.multiple_of(i * tm, tm), tm)
    flat = lambda full: full.reshape(-1, full.shape[-1])
    order = [Unit(*w.shape).count for w in (wq, wo, wu, wd)]
    qs, os, us, ds = (sum(order[:i]) for i in range(4))
    ends = [os + 2, ds + 2, sum(order) + 2]

    def G(*window):
        return [Gather(*window)] if comm else []

    def S(parts, **kw):
        return [Scatter([(a.reshape(*CHIPS, 2, -1, a.shape[-1]), u0, n) for a, u0, n in parts], **kw)] if comm else []

    if comm:
        tile = jnp.pad(jnp.stack([ln1, ln2]), ((0, 6), (0, 128 - ln1.shape[0])))
        fq, fo, fu, lns = host('ag_qkv', 1, [], G([(wq, None, qs), (wo, None, os), (wu, None, us)], 0, ends[0]) + [GatherSmall(tile)])
        fq = flat(fq)
        w1, w2 = lns.reshape(-1, 8, 128)[:, :2, :ln1.shape[0]].transpose(1, 0, 2).reshape(2, 1, d)
    else:
        fq, fo, fu, w1, w2 = wq, wo, wu, ln1.reshape(1, d), ln2.reshape(1, d)

    def ln1_body(i, ins, outs, ext):
        (xr, lw), (ht,), (_, h1) = ins, outs, ext
        xhat, _ = norm_parts(xr[...].astype(F32))
        h = (xhat * lw[...]).astype(BF16)
        h1[band(i)] = h
        ht[...] = h.T

    def qkv_body(i, ins, outs, ext):
        (w,), (o,), (qkv, h1) = ins, outs, ext
        r = dot(h1[...], w[...]).astype(BF16)
        for j in range(per):
            qkv[i * per + j] = r[:, j * hd:(j + 1) * hd]
            o[j] = r[:, j * hd:(j + 1) * hd]

    def attn_body(i, ins, outs, ext):
        (sl,), (o, l), (qkv, _) = ins, outs, ext
        attn_fwd(qkv.at[i], qkv.at[heads + i], qkv.at[2 * heads + i], o, l.at[0], sl[i], scale, tq)

    pb = [Phase(nm, [rows_of(x, tm), whole(w1)], [cols_of(b16(d, seq), tm)], ln1_body),
          Phase(nq // SUB, [cols_of(fq, SUB)], [heads_of(b16(3 * heads, seq, hd), per)], qkv_body),
          Phase(heads, [slopes], [cols_of(act, hd), heads_of(f32(heads, seq, 1), 1)], attn_body)]
    h1t, qkv, attn, lse, *full = host('attn_fwd', 2, pb, G([(wo, fo, os), (wu, fu, us), (wd, None, ds)], ends[0], ends[1]),
                                      shared=[vm16(3 * heads, seq, hd), vm16(seq, d)])
    if comm:
        fo, fu, fd = full
        fo, fu = flat(fo), flat(fu)

    def out_body(i, ins, outs, ext):
        (xs, a, w, lw), (o, ht), (h2,) = ins, outs, ext
        x1 = (xs[...].astype(F32) + dot(a[...], w[...])).astype(BF16)
        o[...] = x1
        xhat, _ = norm_parts(x1.astype(F32))
        h = (xhat * lw[...]).astype(BF16)
        h2[band(i)] = h
        ht[...] = h.T

    def up_body(i, ins, outs, ext):
        (w, dyr), (go, gpo, gd), (h2,) = ins, outs, ext
        u = dot(h2[...], w[...])
        cdf = 0.5 * (1.0 + lax.erf(u * math.sqrt(0.5)))
        g = (u * cdf).astype(BF16)
        go[...] = g
        gpo[...] = cdf + u * (jnp.exp(-0.5 * u * u) * math.sqrt(0.5 / math.pi))
        gd[...] = t_dot(g, dyr[...]).astype(BF16)

    pc = [Phase(nm, [rows_of(x, tm), rows_of(attn, tm), whole(fo), whole(w2)], [rows_of(act, tm), cols_of(b16(d, seq), tm)], out_body),
          Phase(nf, [cols_of(fu, ft), whole(dy)], [cols_of(wide, ft), cols_of(f32(seq, ff), ft), rows_of(b16(ff, d), ft)], up_body)]
    x1, h2t, g, gp, g_down, *full = host('up', 3, pc, G([(wd, fd, ds)], ends[1], ends[2]) if comm else [], shared=[vm16(seq, d)])
    fd, = map(flat, full) if comm else (wd,)

    def dup_body(i, ins, outs, ext):
        (dyr, w, gr, gpr, ht), (duo, gu), (acc,) = ins, outs, ext
        du = (dot_t(dyr[...], w[...]) * gpr[...]).astype(BF16)
        duo[...] = du
        gu[...] = dot(ht[...], du).astype(BF16)
        put(acc, i, dot(gr[...], w[...]))

    def y_body(i, ins, outs, ext):
        (xr,), (o,), (acc,) = ins, outs, ext
        o[...] = (xr[...].astype(F32) + acc[band(i)]).astype(BF16)

    pd = [Phase(nf, [whole(dy), rows_of(fd, ft), cols_of(g, ft), cols_of(gp, ft), whole(h2t)], [cols_of(wide, ft), cols_of(b16(d, ff), ft)], dup_body),
          Phase(nm, [rows_of(x1, tm)], [rows_of(act, tm)], y_body)]
    n_down = Unit(ff // 32, d).count
    d_up, g_up, y, *r1 = host('dup', 4, pd, S([(g_down, 0, n_down)]), shared=[vm32(seq, d)])

    def dh2_body(i, ins, outs, ext):
        (du, w), (acc, _) = ins, ext
        put(acc, i, dot_t(du[...], w[...]))

    def ln2b_body(i, ins, outs, ext):
        (xr, dyr, lw), (dmo, gwo), (acc, dmb) = ins, outs, ext
        dx, gw = norm_back(acc[band(i)], xr[...].astype(F32), lw[...])
        dm = dyr[...].astype(F32) + dx
        dmo[...] = dm
        dmb[band(i)] = dm.astype(BF16)
        put(gwo, i, gw)

    def dattn_body(i, ins, outs, ext):
        (w, a), (da, go), (_, dmb) = ins, outs, ext
        da[...] = dot_t(dmb[...], w[...]).astype(BF16)
        go[...] = t_dot(a[...], dmb[...]).astype(BF16)

    pe = [Phase(nf, [cols_of(d_up, ft), cols_of(fu, ft)], [], dh2_body),
          Phase(nm, [rows_of(x1, tm), rows_of(dy, tm), whole(w2)], [rows_of(f32(seq, d), tm), one_vec], ln2b_body),
          Phase(d // ft, [rows_of(fo, ft), cols_of(attn, ft)], [cols_of(act, ft), rows_of(b16(d, d), ft)], dattn_body)]
    half = n_down // 2
    d_mid, g_ln2, d_attn, g_out, *r2 = host('dh2', 5, pe, S([(g_up, 0, half)], carry=r1[1:]), shared=[vm32(seq, d), vm16(seq, d)])

    def battn_body(i, ins, outs, ext):
        (q, k, v, a, da, l, sl), (o,), (dk, dv) = ins, outs, ext
        attn_bwd(q.at[0], k.at[0], v.at[0], a, da, l.at[0], *(o.at[j, 0] for j in range(3)), dk, dv, sl[i], scale, tq)

    pf = [Phase(heads, [*(heads_of(qkv, 1, j * heads) for j in range(3)), cols_of(attn, hd), cols_of(d_attn, hd), heads_of(lse, 1), slopes],
                [(b16(3, heads, seq, hd), (3, 1, seq, hd), lambda i: (0, i, 0, 0))], battn_body)]
    d_qkv, *r3 = host('attn_bwd', 6, pf, S([(g_up, half, half)], carry=r2[1:]), shared=[vm32(seq, hd), vm32(seq, hd)])
    d_qkv = d_qkv.reshape(3 * heads, seq, hd)

    def gqkv_body(i, ins, outs, ext):
        (ht, dq), (o,) = ins, outs
        o[...] = dot(ht[...], side_by_side(dq, per)).astype(BF16)

    g_qkv, *r4 = host('gqkv', 7, [Phase(nq // SUB, [whole(h1t), heads_of(d_qkv, per)], [cols_of(b16(d, nq), SUB)], gqkv_body)],
                      S([(g_out, 0, d // SUB)], carry=r3[1:]))

    def dh1_body(i, ins, outs, ext):
        (dq, w), (acc,) = ins, ext
        put(acc, i, dot_t(side_by_side(dq, 3), w[...]))

    def ln1b_body(i, ins, outs, ext):
        (xr, dm, lw), (o, gwo), (acc,) = ins, outs, ext
        dx, gw = norm_back(acc[band(i)], xr[...].astype(F32), lw[...])
        o[...] = (dm[...] + dx).astype(BF16)
        put(gwo, i, gw)

    ph = [Phase(heads, [heads_of(d_qkv, 3), cols_of(fq, 3 * hd)], [], dh1_body),
          Phase(nm, [rows_of(x, tm), rows_of(d_mid, tm), whole(w1)], [rows_of(act, tm), one_vec], ln1b_body)]
    comms = S([(g_qkv, 0, nq // SUB)], carry=r4[1:], last=True) + [SmallSum(g_ln2, heads + nm, d)] if comm else []
    dx, g_ln1, *r5 = host('dh1', 8, ph, comms, shared=[vm32(seq, d)])
    if not comm:
        return y, dx, g_ln1, g_qkv, g_out, g_ln2, g_up, g_down
    units = jnp.concatenate([r[0] for r in (r1, r2, r3, r4, r5)])
    nc = d // SUB
    g_down, g_up, g_out, g_qkv = jnp.split(units, (n_down, 2 * n_down, 2 * n_down + nc))
    flat_rows = lambda u: u.transpose(1, 0, 2).reshape(RB, -1)
    g_down = g_down.reshape(-1, nc, RB, SUB).transpose(0, 2, 1, 3).reshape(-1, d)
    return y, dx, r5[1], flat_rows(g_qkv), flat_rows(g_out), None, flat_rows(g_up), g_down


def solution(mesh):
    row_spec = P('fsdp')

    def step(x_in, ln1_w, w_qkv, w_out, ln2_w, w_up, w_down, dy_out):
        rows, _, heads, hd = w_qkv.shape
        d = x_in.shape[-1]
        y, dx, sums, g_qkv, g_out, _, g_up, g_down = local_step(
            x_in[0], ln1_w, w_qkv.reshape(rows, -1), w_out, ln2_w, w_up, w_down, dy_out[0])
        mine = lax.dynamic_slice_in_dim(sums, lax.axis_index('fsdp') * rows, rows, axis=1)
        return (y[None], dx[None], mine[0], g_qkv.reshape(rows, 3, heads, hd), g_out, mine[1], g_up, g_down)

    return jax.shard_map(step, mesh=mesh, in_specs=(row_spec,) * 8, out_specs=(row_spec,) * 8, check_vma=False)
```

time: 749 us -> 688 us (0.919)
  Pallas kernels: 727 us -> 664 us
    pallas_call x8, Pallas kernels: 709 us -> 664 us  [host(): pl.pallas_call(kernel, grid=(total,), in_specs=in_specs, out_specs=out_sp...]
    pallas_call x1 -> x0, Pallas kernels: 18.1 us -> none  [small_sum(): pl.pallas_call(kernel, in_specs=[vm], out_specs=vm, out_shape=sds(shape,...]
where the time goes in v2:
time: 688 us; the launch traced here: 687 us
  Pallas kernels  664 us (97%)
  local copies, waits for them, and re-layouts  18.7 us (3%)
    pallas_call x8, Pallas kernels, host(): pl.pallas_call(kernel, grid=(total,), in_specs=in_specs, out_specs=out_sp...  664 us

profile of v2, /device:TPU:0, one launch (start us, length us, event | category | flops | bytes accessed | tf_op | source)
XLA Modules:
  0.0 687.4 jit_solution(8076018798609017827)
XLA Ops:
  0.6 1.2 copy.23
  1.8 1.1 reshape.67.refs_0_
  2.9 1.3 select_maximum_fusion.refs_3_
  4.1 88.2 %ag_qkv.1 = (bf16[4,2,2,2,48,4608]{5,4,3,2,1,0:T(8,128)(2,1)}, bf16[4,2,2,2,48,1536]{5,4,3,2,1,0:T(8,128)(2,1)}, bf16[4,2,2,2,48,6144]{5,4,3,2,1,0:T(8,128)(2,1)}, f32[4,2,2,2,8,128]{5,4,3,2,1,0:T(8,128)}) custom-call(bf16[48,4608]{1,0:T(8,128)(2,1)} %reshape.67.refs_0_, bf16[48,1536]{1,0:T(8,128)(2,1)} %refs_4_.1, bf16[48,6144]{1,0:T(8,128)(2,1)} %refs_6_.3, ...), custom_call_target="tpu_custom_call" | custom-call | flops 17179869184 | bytes 33554432 | tf_op jit(solution)/shard_map/ag_qkv/pallas_call | solution.py:517
  92.3 0.9 slice.17
  93.3 0.7 unstack.13.refs_1_.refs_4_
  94.0 109.0 %attn_fwd.1 = (bf16[1536,1024]{1,0:T(8,128)(2,1)}, bf16[36,1024,128]{2,1,0:T(8,128)(2,1)}, bf16[1024,1536]{1,0:T(8,128)(2,1)}, f32[12,1024,1]{2,1,0:T(8,128)}, b...) custom-call(bf16[1024,1536]{1,0:T(8,128)(2,1)} %bitcast.61, ...), custom_call_target="tpu_custom_call", output_to_operand_aliasing={{4}: (5, {}), {5}: (7, {})} | custom-call | flops 17179869184 | bytes 33554432 | tf_op jit(solution)/shard_map/attn_fwd/pallas_call | solution.py:517
  203.0 0.7 unstack.15.refs_3_.refs_4_
  203.7 97.7 %up.1 = (bf16[1024,1536]{1,0:T(8,128)(2,1)}, bf16[1536,1024]{1,0:T(8,128)(2,1)}, bf16[1024,6144]{1,0:T(8,128)(2,1)}, f32[1024,6144]{1,0:T(8,128)}, bf16[6144,153...) custom-call(bf16[1024,1536]{1,0:T(8,128)(2,1)} %bitcast.62, ...), custom_call_target="tpu_custom_call", output_to_operand_aliasing={{5}: (7, {})} | custom-call | flops 17179869184 | bytes 33554432 | tf_op jit(solution)/shard_map/up/pallas_call | solution.py:517
  301.4 123.5 %dup.1 = (bf16[1024,6144]{1,0:T(8,128)(2,1)}, bf16[1536,6144]{1,0:T(8,128)(2,1)}, bf16[1024,1536]{1,0:T(8,128)(2,1)}, f32[10,48,512]{2,1,0:T(8,128)}, bf16[2,4,2...) custom-call(bf16[1024,1536]{1,0:T(8,128)(2,1)} %bitcast.45, bf16[6144,1536]{1,0:T(8,128)(2,1)} %bitcast.42, ...), custom_call_target="tpu_custom_call" | custom-call | flops 17179869184 | bytes 33554432 | tf_op jit(solution)/shard_map/dup/pallas_call | solution.py:517
  425.0 67.6 %dh2.1 = (f32[1024,1536]{1,0:T(8,128)}, f32[1,1536]{1,0:T(1,128)}, bf16[1024,1536]{1,0:T(8,128)(2,1)}, bf16[1536,1536]{1,0:T(8,128)(2,1)}, f32[6,48,512]{2,1,0:T...) custom-call(bf16[1024,6144]{1,0:T(8,128)(2,1)} %get-tuple-element.65.refs_0_, ...), custom_call_target="tpu_custom_call" | custom-call | flops 17179869184 | bytes 33554432 | tf_op jit(solution)/shard_map/dh2/pallas_call | solution.py:517
  492.6 57.4 %attn_bwd.1 = (bf16[3,12,1024,128]{3,2,1,0:T(8,128)(2,1)}, f32[6,48,512]{2,1,0:T(8,128)}, bf16[2,4,2,48,256]{4,3,2,1,0:T(8,128)(2,1)}, bf16[4,48,512]{2,1,0:T(8,128)(2,1)}) custom-call(bf16[36,1024,128]{2,1,0:T(8,128)(2,1)} %get-tuple-element.64.refs_0_.refs_1_.refs_2_, bf16[36,1024,128]{2,1,0:T(8,128)(2,1)} %get-tuple-element.64.refs_0_.refs_1_.refs_2_, ...), custom_call_target="tpu_custom_call" | custom-call | flops 17179869184 | bytes 33554432 | tf_op jit(solution)/shard_map/attn_bwd/pallas_call | solution.py:517
  550.0 0.0 copy-start.2
  550.0 0.0 copy-start.3
  550.0 31.7 %gqkv.1 = (bf16[1536,4608]{1,0:T(8,128)(2,1)}, f32[3,48,512]{2,1,0:T(8,128)}, bf16[2,4,2,48,256]{4,3,2,1,0:T(8,128)(2,1)}, bf16[4,48,512]{2,1,0:T(8,128)(2,1)}) custom-call(bf16[1536,1024]{1,0:T(8,128)(2,1)} %get-tuple-element.75.refs_0_, bf16[36,1024,128]{2,1,0:T(8,128)(2,1)} %bitcast.67, bf16[4,2,2,2,48,1536]{5,4,3,2,1,0:T(8,128)(2,1)} %bitcast.60, ...), custom_call_target="tpu_custom_call" | custom-call | flops 17179869184 | bytes 33554432 | tf_op jit(solution)/shard_map/gqkv/pallas_call | solution.py:517
  581.7 0.0 copy-done.2
  581.7 0.0 copy-done.3
  581.7 1.5 pad_maximum_fusion
  583.2 0.8 copy.28
  584.0 1.5 copy.33
  585.5 1.1 copy.32
  586.6 88.9 %dh1.1 = (bf16[1024,1536]{1,0:T(8,128)(2,1)}, f32[1,1536]{1,0:T(1,128)}, f32[11,48,512]{2,1,0:T(8,128)}, f32[8,1536]{1,0:T(8,128)}) custom-call(bf16[36,1024,128]{2,1,0:T(8,128)(2,1)} %bitcast.68, bf16[1536,4608]{1,0:T(8,128)(2,1)} %bitcast.65, bf16[1024,1536]{1,0:T(8,128)(2,1)} %bitcast.63, f32[1024,1536]{1,0:T(8,128)} %get-tuple-element.74.refs_3_, ...), custom_call_target="tpu_custom_call" | custom-call | flops 17179869184 | bytes 33554432 | tf_op jit(solution)/shard_map/dh1/pallas_call | solution.py:517
  675.6 0.9 fusion.1
  676.5 0.7 copy.31
  677.2 1.2 slice_bitcast_fusion
  678.5 0.6 copy.25
  679.1 0.2 reshape_reshape.3
  679.3 1.2 copy.29
  680.5 0.8 constant_dynamic-slice_fusion
  681.3 0.5 slice_bitcast_fusion.1
  681.8 3.9 copy.41
  685.7 1.7 copy.42
  (6 shorter events, 0.0 us)
Async XLA Ops:
  550.0 31.7 %copy-start.2 = (f32[10,48,512]{2,1,0:T(8,128)S(1)}, f32[10,48,512]{2,1,0:T(8,128)}, u32[]{:S(2)}) copy-start(f32[10,48,512]{2,1,0:T(8,128)} %get-tuple-element.89) | copy-start | bytes 2949124
  550.0 31.7 %copy-start.3 = (f32[6,48,512]{2,1,0:T(8,128)S(1)}, f32[6,48,512]{2,1,0:T(8,128)}, u32[]{:S(2)}) copy-start(f32[6,48,512]{2,1,0:T(8,128)} %get-tuple-element.87) | copy-start | bytes 1769476
  586.6 89.0 %copy-start.1 = (f32[3,48,512]{2,1,0:T(8,128)S(1)}, f32[3,48,512]{2,1,0:T(8,128)}, u32[]{:S(2)}) copy-start(f32[3,48,512]{2,1,0:T(8,128)} %get-tuple-element.86) | copy-start | bytes 884740
  681.8 3.9 copy-start

commit v3 on v2

--- a/solution.py
+++ b/solution.py
@@ -11,6 +11,8 @@
 EPS = 1e-5
 SUB = 512
 HALF = SUB // 2
+LAG = 2
+CARRY = 2 * LAG
 LEAD = 3
 RB = 48
 F32, BF16 = jnp.float32, jnp.bfloat16
@@ -111,7 +113,7 @@
                 self.alias.append((len(self.ins), len(self.outs)))
                 self.ins.append((full, pl.BlockSpec(memory_space=HBM)))
             self.outs.append((sds(CHIPS + (2,) + shard.shape, BF16), pl.BlockSpec(memory_space=HBM)))
-        self.base = max(k0 - 2, 0)
+        self.base = max(k0 - 2 * LAG, 0)
         n = self.z1 - self.base
         self.scratch = [pltpu.SemaphoreType.DMA((n, 8)), pltpu.SemaphoreType.DMA((n, 8)), pltpu.SemaphoreType.DMA((len(weights),))]
 
@@ -162,7 +164,7 @@
     def step(self, k, fire, refs):
         me, z, y, x, c = coords()
         k0, k1, k = self.k0, self.k1, k + self.k0
-        span = [(self.z0, self.z1), (k0, k1), (max(k0 - 1, 0), k1 - 1), (max(k0 - 2, 0), k1 - 2)]
+        span = [(self.z0, self.z1)] + [(max(k0 - i * LAG, 0), k1 - i * LAG) for i in range(3)]
 
         @pl.when(fire & (k == k0))
         def _():
@@ -179,7 +181,7 @@
         def _():
             self.each(*span[0], k + LEAD, lambda w, u: self.go(0, w, u, refs))
             for stage in (1, 2, 3):
-                u = k + 1 - stage
+                u = k + LAG * (1 - stage)
                 lo, hi = span[stage - 1]
                 self.each(lo, hi, u, lambda w, u: self.arrive(stage - 1, w, u, refs))
                 self.each(*span[stage], u, lambda w, u: self.go(stage, w, u, refs))
@@ -188,7 +190,7 @@
         def _():
             for stage in range(4):
                 lo, hi = span[stage]
-                self.each(max(lo, k1 - stage) if stage < 3 else lo, hi, None, lambda w, u: self.arrive(stage, w, u, refs))
+                self.each(max(lo, k1 - stage * LAG) if stage < 3 else lo, hi, None, lambda w, u: self.arrive(stage, w, u, refs))
                 self.each(lo, hi, None, lambda w, u: self.left(stage, w, u, refs))
 
 
@@ -240,33 +242,32 @@
             self.ins.append((g, pl.BlockSpec(memory_space=HBM)))
             n += m
         self.n = n
-        self.first = 0 if self.carried else 2
-        self.done = n + (2 if last else 0)
-        self.k = n + (3 if last else 1)
+        self.first = 0 if self.carried else CARRY
+        self.end = n + CARRY
+        self.done = self.end if last else n
+        self.k = n + (3 * LAG if last else 1)
         self.two_shape, self.three_shape = (2, 4, 2, RB, HALF), (4, RB, SUB)
         if self.carried:
             self.ins += [(a, pl.BlockSpec(memory_space=pltpu.VMEM)) for a in carry]
         self.scratch = [
             pltpu.VMEM((n, *CHIPS, RB, SUB), BF16),
             pltpu.VMEM((2, *CHIPS, RB, SUB), BF16),
-            pltpu.VMEM((n + 2,) + self.two_shape, BF16),
-            pltpu.VMEM((n + 2,) + self.three_shape, BF16),
-            pltpu.VMEM((n + 2, 3, RB, SUB), BF16),
-            pltpu.SemaphoreType.DMA((n + 2, 8)), pltpu.SemaphoreType.DMA((n + 2, 8)), pltpu.SemaphoreType.DMA((2,))]
+            pltpu.VMEM((self.end, *self.two_shape), BF16),
+            pltpu.VMEM((self.end, *self.three_shape), BF16),
+            pltpu.VMEM((self.end, 3, RB, SUB), BF16),
+            pltpu.SemaphoreType.DMA((self.end, 8)), pltpu.SemaphoreType.DMA((self.end, 8)), pltpu.SemaphoreType.DMA((2,))]
+        outs = [sds((self.done - self.first, RB, SUB), F32)]
+        if not last:
+            outs += [sds((LAG, *shape), BF16) for shape in (self.two_shape, self.three_shape)]
+        self.outs = [(o, pl.BlockSpec(memory_space=pltpu.VMEM)) for o in outs]
         self.alias = []
-
-    def out_spec(self, kmap):
-        lo, count = self.first, self.done - self.first
-        self.outs = [(sds((count, RB, SUB), F32), pl.BlockSpec((1, RB, SUB), lambda t: (clip(kmap(t) - 1 - lo, count), 0, 0)))]
-        if not self.last:
-            self.outs += [(sds(shape, BF16), pl.BlockSpec(memory_space=pltpu.VMEM)) for shape in (self.two_shape, self.three_shape)]
 
     def source(self, j, refs, fn):
         for i, (a, b, u0, unit) in enumerate(self.parts):
             if len(self.parts) == 1:
-                fn(refs[i], *unit.at(u0 + j - 2))
+                fn(refs[i], *unit.at(u0 + j - CARRY))
             else:
-                pl.when((j - 2 >= a) & (j - 2 < b))(lambda: fn(refs[i], *unit.at(u0 + j - 2 - a)))
+                pl.when((j - CARRY >= a) & (j - CARRY < b))(lambda: fn(refs[i], *unit.at(u0 + j - CARRY - a)))
 
     def bufs(self, refs):
         return refs[len(self.ins) + len(self.outs):]
@@ -281,7 +282,7 @@
         me, z, y, x, c = coords()
         got, ss, rs = self.bufs(refs)[0], *self.bufs(refs)[-3:-1]
         cp = peers()[-1]
-        self.source(j, refs, lambda g, r, q: act(remote(g.at[:, :, :, 1 - c, r, q], got.at[j - 2], ss.at[j, 0], rs.at[j, 0], cp)))
+        self.source(j, refs, lambda g, r, q: act(remote(g.at[:, :, :, 1 - c, r, q], got.at[j - CARRY], ss.at[j, 0], rs.at[j, 0], cp)))
 
     def copies(self, stage, j, refs):
         got, own, two, three, four, ss, rs, ls = self.bufs(refs)
@@ -289,7 +290,7 @@
         zs, yp, xp, cp = peers()
         a, b = pl.ds(0, HALF), pl.ds(HALF, HALF)
         if stage == 1:
-            pairs = [(got.at[j - 2, :, 1 - y, :, :, a], two.at[j, 0], yp), (got.at[j - 2, :, :, 1 - x, :, b], two.at[j, 1], xp)]
+            pairs = [(got.at[j - CARRY, :, 1 - y, :, :, a], two.at[j, 0], yp), (got.at[j - CARRY, :, :, 1 - x, :, b], two.at[j, 1], xp)]
         elif stage == 2:
             pairs = [(two.at[j, 0, :, 1 - x], three.at[j, :, :, a], xp), (two.at[j, 1, :, 1 - y], three.at[j, :, :, b], yp)]
         else:
@@ -306,13 +307,13 @@
             def _(zz):
                 for yy in range(2):
                     for xx in range(2):
-                        got[j - 2, zz, yy, xx] += own[slot, zz, yy, xx]
+                        got[j - CARRY, zz, yy, xx] += own[slot, zz, yy, xx]
         elif stage == 2:
             @pl.loop(0, 4)
             def _(zz):
                 for i in range(2):
-                    two[j, 0, zz, i] += got[j - 2, zz, y, i, :, a]
-                    two[j, 1, zz, i] += got[j - 2, zz, i, x, :, b]
+                    two[j, 0, zz, i] += got[j - CARRY, zz, y, i, :, a]
+                    two[j, 1, zz, i] += got[j - CARRY, zz, i, x, :, b]
         elif stage == 3:
             for zz in range(4):
                 three[j, zz, :, a] += two[j, 0, zz, x]
@@ -321,10 +322,10 @@
             total = three[j, z].astype(F32)
             for d in range(3):
                 total += four[j, d].astype(F32)
-            refs[len(self.ins)][0] = total
+            refs[len(self.ins)][j - self.first] = total
 
     def step(self, k, fire, refs):
-        n, last = self.n, self.last
+        n, end, last = self.n, self.end, self.last
         got, own, two, three, four, ss, rs, ls = self.bufs(refs)
         start = lambda cp: cp.start()
 
@@ -332,60 +333,65 @@
             for cp in self.copies(stage, j, refs):
                 cp.start()
 
+        def take(stage, j):
+            for cp in self.copies(stage - 1, j, refs):
+                cp.wait_recv()
+            self.add(stage, j, refs)
+
         @pl.when(fire & (k == 0))
         def _():
-            if self.carried:
-                two[1] = refs[len(self.ins) - 2][...]
-                three[0] = refs[len(self.ins) - 1][...]
-                go(2, 1)
-                go(3, 0)
-
-            @pl.loop(2, n + 2)
+            @pl.loop(CARRY, end)
             def _(j):
                 self.swap(j, refs, start)
 
-            for j in range(2, min(4, n + 2)):
+            for j in range(CARRY, min(CARRY + 2, end)):
                 self.local(j, refs, start)
-
-        for stage in (1, 2, 3, 4):
-            j = k + 3 - stage
-            low = (2, 2, 1, 0)[stage - 1] if self.carried else 2
-
-            @pl.when(fire & (j >= low) & (j < n + 2))
+            if self.carried:
+                for i in range(LAG):
+                    two[LAG + i] = refs[len(self.ins) - 2][i]
+                    three[i] = refs[len(self.ins) - 1][i]
+                    go(2, LAG + i)
+                    go(3, i)
+
+        @pl.when(fire & (k < n))
+        def _():
+            j = k + CARRY
+            self.swap(j, refs, lambda cp: cp.wait_recv())
+            self.local(j, refs, lambda cp: cp.wait())
+            self.add(1, j, refs)
+            go(1, j)
+            pl.when(j + 2 < end)(lambda: self.local(j + 2, refs, start))
+
+        lows = [CARRY, LAG, 0] if self.carried else [CARRY] * 3
+        for stage, low in zip((2, 3, 4), lows):
+            j = k + (3 - stage) * LAG
+
+            @pl.when(fire & (j >= low) & (j < end) & ((k < n) | last))
             def _(stage=stage, j=j):
-                if stage == 1:
-                    self.swap(j, refs, lambda cp: cp.wait_recv())
-                    self.local(j, refs, lambda cp: cp.wait())
-                else:
-                    for cp in self.copies(stage - 1, j, refs):
-                        cp.wait_recv()
-                self.add(stage, j, refs)
+                take(stage, j)
                 if stage < 4:
-                    if last or stage == 1:
-                        go(stage, j)
-                    else:
-                        pl.when(k < n)(lambda: go(stage, j))
-                if stage == 1:
-                    pl.when(j < n)(lambda: self.local(j + 2, refs, start))
+                    go(stage, j)
 
         @pl.when(fire & (k == self.k - 1))
         def _():
-            for stage in (1, 2, 3):
-                low = (2, 1, 0)[stage - 1] if self.carried else 2
-                high = n + 2 if last else n + 3 - stage
-
-                @pl.loop(low, high)
+            for stage, low in zip((2, 3, 4), lows):
+                a = n + (3 - stage) * LAG
+                if not last:
+                    pl.loop(max(a, low), a + LAG)(functools.partial(take, stage))
+
+                @pl.loop(CARRY if stage == 2 else low, end if last else a + LAG)
                 def _(j):
-                    for cp in self.copies(stage, j, refs):
+                    for cp in self.copies(stage - 1, j, refs):
                         cp.wait_send()
 
-            @pl.loop(2, n + 2)
+            @pl.loop(CARRY, end)
             def _(j):
                 self.swap(j, refs, lambda cp: cp.wait_send())
 
             if not last:
-                refs[len(self.ins) + 1][...] = two[n + 1]
-                refs[len(self.ins) + 2][...] = three[n]
+                for i in range(LAG):
+                    refs[len(self.ins) + 1][i] = two[n + LAG + i]
+                    refs[len(self.ins) + 2][i] = three[n + i]
 
 
 class SmallSum:
@@ -449,8 +455,6 @@
             outs.append(shape)
             out_specs.append(pl.BlockSpec(block, functools.partial(lambda p, f, t: f(clip(t - p.at, p.n)), p, index)))
     for c in comms:
-        if isinstance(c, Scatter):
-            c.out_spec(kmap)
         alias.update({len(ins) + i: len(outs) + o for i, o in c.alias})
         for arr, spec in c.ins:
             ins.append(arr)
@@ -664,7 +668,7 @@
     flat = lambda full: full.reshape(-1, full.shape[-1])
     order = [Unit(*w.shape).count for w in (wq, wo, wu, wd)]
     qs, os, us, ds = (sum(order[:i]) for i in range(4))
-    ends = [os + 2, ds + 2, sum(order) + 2]
+    ends = [i + 2 * LAG for i in (os, ds, sum(order))]
 
     def G(*window):
         return [Gather(*window)] if comm else []

time: 688 us -> 687 us (level); the launches traced: 687 us -> 678 us
  Pallas kernels: 664 us -> 655 us
    pallas_call x8, Pallas kernels: 664 us -> 655 us  [host(): pl.pallas_call(kernel, grid=(total,), in_specs=in_specs, out_specs=out_sp...]
where the time goes in v3:
time: 687 us; the launch traced here: 678 us
  Pallas kernels  655 us (95%)
  local copies, waits for them, and re-layouts  19.9 us (3%)
    pallas_call x8, Pallas kernels, host(): pl.pallas_call(kernel, grid=(total,), in_specs=in_specs, out_specs=out_sp...  655 us

profile of v3, /device:TPU:0, one launch (start us, length us, event | category | flops | bytes accessed | tf_op | source)
XLA Modules:
  0.0 678.4 jit_solution(14760318794173921139)
XLA Ops:
  0.6 1.2 copy.23
  1.8 1.1 reshape.67.refs_0_
  2.9 1.3 select_maximum_fusion.refs_3_
  4.1 101.1 %ag_qkv.1 = (bf16[4,2,2,2,48,4608]{5,4,3,2,1,0:T(8,128)(2,1)}, bf16[4,2,2,2,48,1536]{5,4,3,2,1,0:T(8,128)(2,1)}, bf16[4,2,2,2,48,6144]{5,4,3,2,1,0:T(8,128)(2,1)}, f32[4,2,2,2,8,128]{5,4,3,2,1,0:T(8,128)}) custom-call(bf16[48,4608]{1,0:T(8,128)(2,1)} %reshape.67.refs_0_, bf16[48,1536]{1,0:T(8,128)(2,1)} %refs_4_.1, bf16[48,6144]{1,0:T(8,128)(2,1)} %refs_6_.3, ...), custom_call_target="tpu_custom_call" | custom-call | flops 17179869184 | bytes 33554432 | tf_op jit(solution)/shard_map/ag_qkv/pallas_call | solution.py:521
  105.3 0.9 slice.16
  106.2 0.7 unstack.13.refs_1_.refs_4_
  106.9 108.7 %attn_fwd.1 = (bf16[1536,1024]{1,0:T(8,128)(2,1)}, bf16[36,1024,128]{2,1,0:T(8,128)(2,1)}, bf16[1024,1536]{1,0:T(8,128)(2,1)}, f32[12,1024,1]{2,1,0:T(8,128)}, b...) custom-call(bf16[1024,1536]{1,0:T(8,128)(2,1)} %bitcast.61, ...), custom_call_target="tpu_custom_call", output_to_operand_aliasing={{4}: (5, {}), {5}: (7, {})} | custom-call | flops 17179869184 | bytes 33554432 | tf_op jit(solution)/shard_map/attn_fwd/pallas_call | solution.py:521
  215.6 0.7 unstack.15.refs_3_.refs_4_
  216.3 85.1 %up.1 = (bf16[1024,1536]{1,0:T(8,128)(2,1)}, bf16[1536,1024]{1,0:T(8,128)(2,1)}, bf16[1024,6144]{1,0:T(8,128)(2,1)}, f32[1024,6144]{1,0:T(8,128)}, bf16[6144,153...) custom-call(bf16[1024,1536]{1,0:T(8,128)(2,1)} %bitcast.62, ...), custom_call_target="tpu_custom_call", output_to_operand_aliasing={{5}: (7, {})} | custom-call | flops 17179869184 | bytes 33554432 | tf_op jit(solution)/shard_map/up/pallas_call | solution.py:521
  301.4 119.9 %dup.1 = (bf16[1024,6144]{1,0:T(8,128)(2,1)}, bf16[1536,6144]{1,0:T(8,128)(2,1)}, bf16[1024,1536]{1,0:T(8,128)(2,1)}, f32[8,48,512]{2,1,0:T(8,128)}, bf16[2,2,4,...) custom-call(bf16[1024,1536]{1,0:T(8,128)(2,1)} %bitcast.45, bf16[6144,1536]{1,0:T(8,128)(2,1)} %bitcast.42, ...), custom_call_target="tpu_custom_call" | custom-call | flops 17179869184 | bytes 33554432 | tf_op jit(solution)/shard_map/dup/pallas_call | solution.py:521
  421.3 65.4 %dh2.1 = (f32[1024,1536]{1,0:T(8,128)}, f32[1,1536]{1,0:T(1,128)}, bf16[1024,1536]{1,0:T(8,128)(2,1)}, bf16[1536,1536]{1,0:T(8,128)(2,1)}, f32[6,48,512]{2,1,0:T...) custom-call(bf16[1024,6144]{1,0:T(8,128)(2,1)} %get-tuple-element.65.refs_0_, ...), custom_call_target="tpu_custom_call" | custom-call | flops 17179869184 | bytes 33554432 | tf_op jit(solution)/shard_map/dh2/pallas_call | solution.py:521
  486.7 56.3 %attn_bwd.1 = (bf16[3,12,1024,128]{3,2,1,0:T(8,128)(2,1)}, f32[6,48,512]{2,1,0:T(8,128)}, bf16[2,2,4,2,48,256]{5,4,3,2,1,0:T(8,128)(2,1)}, bf16[2,4,48,512]{3,2,1,0:T(8,128)(2,1)}) custom-call(bf16[36,1024,128]{2,1,0:T(8,128)(2,1)} %get-tuple-element.64.refs_0_.refs_1_.refs_2_, bf16[36,1024,128]{2,1,0:T(8,128)(2,1)} %get-tuple-element.64.refs_0_.refs_1_.refs_2_, ...), custom_call_target="tpu_custom_call" | custom-call | flops 17179869184 | bytes 33554432 | tf_op jit(solution)/shard_map/attn_bwd/pallas_call | solution.py:521
  543.0 32.4 %gqkv.1 = (bf16[1536,4608]{1,0:T(8,128)(2,1)}, f32[3,48,512]{2,1,0:T(8,128)}, bf16[2,2,4,2,48,256]{5,4,3,2,1,0:T(8,128)(2,1)}, bf16[2,4,48,512]{3,2,1,0:T(8,128)(2,1)}) custom-call(bf16[1536,1024]{1,0:T(8,128)(2,1)} %get-tuple-element.75.refs_0_, bf16[36,1024,128]{2,1,0:T(8,128)(2,1)} %bitcast.67, bf16[4,2,2,2,48,1536]{5,4,3,2,1,0:T(8,128)(2,1)} %bitcast.60, ...), custom_call_target="tpu_custom_call" | custom-call | flops 17179869184 | bytes 33554432 | tf_op jit(solution)/shard_map/gqkv/pallas_call | solution.py:521
  575.4 0.0 copy-start.2
  575.4 0.0 copy-start.3
  575.4 0.0 copy-start.4
  575.4 86.2 %dh1.1 = (bf16[1024,1536]{1,0:T(8,128)(2,1)}, f32[1,1536]{1,0:T(1,128)}, f32[13,48,512]{2,1,0:T(8,128)}, f32[8,1536]{1,0:T(8,128)}) custom-call(bf16[36,1024,128]{2,1,0:T(8,128)(2,1)} %bitcast.68, bf16[1536,4608]{1,0:T(8,128)(2,1)} %bitcast.65, bf16[1024,1536]{1,0:T(8,128)(2,1)} %bitcast.63, f32[1024,1536]{1,0:T(8,128)} %get-tuple-element.74.refs_3_, ...), custom_call_target="tpu_custom_call" | custom-call | flops 17179869184 | bytes 33554432 | tf_op jit(solution)/shard_map/dh1/pallas_call | solution.py:521
  661.6 0.0 copy-done.2
  661.6 0.0 copy-done.3
  661.6 1.2 pad_maximum_fusion
  662.8 0.8 copy.28
  663.7 1.5 copy.33
  665.1 1.1 copy.32
  666.3 0.1 slice_bitcast_fusion
  666.3 0.6 copy.25
  666.9 1.3 reshape_reshape.3
  668.1 2.4 copy.29
  670.6 0.7 copy.31
  671.4 0.8 constant_dynamic-slice_fusion
  672.1 0.5 slice_bitcast_fusion.2
  672.6 3.9 copy.41
  676.6 1.7 copy.42
  (8 shorter events, 0.0 us)
Async XLA Ops:
  575.4 86.2 %copy-start.2 = (f32[8,48,512]{2,1,0:T(8,128)S(1)}, f32[8,48,512]{2,1,0:T(8,128)}, u32[]{:S(2)}) copy-start(f32[8,48,512]{2,1,0:T(8,128)} %get-tuple-element.89) | copy-start | bytes 2359300
  575.4 86.2 %copy-start.3 = (f32[6,48,512]{2,1,0:T(8,128)S(1)}, f32[6,48,512]{2,1,0:T(8,128)}, u32[]{:S(2)}) copy-start(f32[6,48,512]{2,1,0:T(8,128)} %get-tuple-element.86) | copy-start | bytes 1769476
  575.4 86.2 %copy-start.4 = (f32[6,48,512]{2,1,0:T(8,128)S(1)}, f32[6,48,512]{2,1,0:T(8,128)}, u32[]{:S(2)}) copy-start(f32[6,48,512]{2,1,0:T(8,128)} %get-tuple-element.87) | copy-start | bytes 1769476
  663.7 2.6 copy-start
  672.6 3.9 copy-start.1

commit v4 on v3

--- a/solution.py
+++ b/solution.py
@@ -16,7 +16,7 @@
 LEAD = 3
 RB = 48
 F32, BF16 = jnp.float32, jnp.bfloat16
-VMEM_LIMIT = 62 * 1024 * 1024
+VMEM_LIMIT = 67_000_000
 MESH = pl.DeviceIdType.MESH
 HBM = pltpu.MemorySpace.HBM
 CHIPS = (4, 2, 2)
@@ -50,8 +50,21 @@
 
 
 class Phase:
-    def __init__(self, n, ins, outs, body):
-        self.n, self.ins, self.outs, self.body = n, ins, outs, body
+    def __init__(self, n, ins, outs, body, at=None, stride=1):
+        self.n, self.ins, self.outs, self.body, self.at, self.stride = n, ins, outs, body, at, stride
+
+    def own(self, t):
+        return quot(t - self.at, self.stride)
+
+    def on(self, t):
+        here = (t >= self.at) & (t < self.end())
+        return here if self.stride == 1 else here & (rest(t - self.at, self.stride) == 0)
+
+    def end(self):
+        return self.at + (self.n - 1) * self.stride + 1
+
+    def index(self, f):
+        return lambda t: f(clip(self.own(jnp.maximum(t, self.at)), self.n))
 
 
 def quot(a, b):
@@ -237,10 +250,15 @@
     def __init__(self, grads, carry=None, last=False):
         self.last, self.carried = last, carry is not None
         self.parts, self.ins, n = [], [], 0
+        self.late = None
         for g, u0, m in grads:
             self.parts.append((n, n + m, u0, Unit(*g.shape[-2:])))
-            self.ins.append((g, pl.BlockSpec(memory_space=HBM)))
+            if isinstance(g, jax.ShapeDtypeStruct):
+                self.late = g
+            else:
+                self.ins.append((g, pl.BlockSpec(memory_space=HBM)))
             n += m
+        self.known = n - m if self.late else n
         self.n = n
         self.first = 0 if self.carried else CARRY
         self.end = n + CARRY
@@ -260,14 +278,24 @@
         if not last:
             outs += [sds((LAG, *shape), BF16) for shape in (self.two_shape, self.three_shape)]
         self.outs = [(o, pl.BlockSpec(memory_space=pltpu.VMEM)) for o in outs]
+        if self.late:
+            self.outs.append((self.late, pl.BlockSpec(memory_space=HBM)))
         self.alias = []
 
     def source(self, j, refs, fn):
         for i, (a, b, u0, unit) in enumerate(self.parts):
+            ref = self.written() if self.late and a == self.known else refs[i]
+            u = j - CARRY
             if len(self.parts) == 1:
-                fn(refs[i], *unit.at(u0 + j - CARRY))
+                fn(ref, *unit.at(u0 + u))
             else:
-                pl.when((j - CARRY >= a) & (j - CARRY < b))(lambda: fn(refs[i], *unit.at(u0 + j - CARRY - a)))
+                pl.when((u >= a) & (u < b))(functools.partial(lambda ref, unit, u: fn(ref, *unit.at(u)), ref, unit, u0 + u - a))
+
+    def written(self):
+        return self.refs[len(self.ins) + len(self.outs) - 1]
+
+    def ship(self, u):
+        self.swap(CARRY + self.known + u, self.refs, lambda cp: cp.start())
 
     def bufs(self, refs):
         return refs[len(self.ins) + len(self.outs):]
@@ -340,7 +368,7 @@
 
         @pl.when(fire & (k == 0))
         def _():
-            @pl.loop(CARRY, end)
+            @pl.loop(CARRY, CARRY + self.known)
             def _(j):
                 self.swap(j, refs, start)
 
@@ -395,8 +423,8 @@
 
 
 class SmallSum:
-    def __init__(self, row, t0, d):
-        self.t0, self.k = t0, 1
+    def __init__(self, row, at, t0, d):
+        self.at, self.t0, self.k = at, t0, 1
         self.ins = [(row, pl.BlockSpec(memory_space=pltpu.VMEM))]
         self.outs = [(sds((8, d), F32), pl.BlockSpec(memory_space=pltpu.VMEM))]
         self.alias = []
@@ -435,10 +463,11 @@
     k_all = max([c.k for c in comms], default=1)
     at = 0
     for p in phases:
-        p.at = at
-        at = at + p.n
+        if p.at is None:
+            p.at = at
+        at = max(at, p.end())
     small = [c for c in comms if isinstance(c, SmallSum)]
-    total = max(at + 5 * len(small), k_all)
+    total = max([at, k_all] + [c.t0 + 5 for c in small])
     kmap = lambda t: t if total == k_all else quot(t * (k_all - 1), total - 1)
     ins, in_specs, outs, out_specs, scratch, alias, resident = [], [], [], [], [], {}, []
     for p in phases:
@@ -449,11 +478,11 @@
                 resident.append((len(ins), p.at))
                 in_specs.append(pl.BlockSpec(memory_space=HBM))
             else:
-                in_specs.append(pl.BlockSpec(block, functools.partial(lambda p, f, t: f(clip(t - p.at, p.n)), p, index)))
+                in_specs.append(pl.BlockSpec(block, p.index(index)))
             ins.append(arr)
         for shape, block, index in p.outs:
             outs.append(shape)
-            out_specs.append(pl.BlockSpec(block, functools.partial(lambda p, f, t: f(clip(t - p.at, p.n)), p, index)))
+            out_specs.append(pl.BlockSpec(block, p.index(index)))
     for c in comms:
         alias.update({len(ins) + i: len(outs) + o for i, o in c.alias})
         for arr, spec in c.ins:
@@ -487,9 +516,8 @@
         for c in comms:
             ni, no, ns = len(c.ins), len(c.outs), len(c.scratch)
             crefs = rin[i:i + ni] + rout[o:o + no] + rscr[s:s + ns]
-            if c in small:
-                small_refs = crefs
-            else:
+            c.refs = crefs
+            if c not in small:
                 c.step(k, fire, crefs)
             i, o, s = i + ni, o + no, s + ns
         held, rsem, extra = rscr[s:s + len(resident)], rscr[s + len(resident)], rscr[s + len(resident) + 1:]
@@ -508,12 +536,12 @@
             pi, po = rin[i:i + len(p.ins)], rout[o:o + len(p.outs)]
             i, o = i + len(p.ins), o + len(p.outs)
 
-            @pl.when((t >= p.at) & (t < p.at + p.n))
+            @pl.when(p.on(t))
             def _(p=p, pi=pi, po=po):
-                p.body(t - p.at, pi, po, extra)
+                p.body(p.own(t), pi, po, extra)
 
         for c in small:
-            c.run(t, rout[o - 1], small_refs)
+            c.run(t, rout[c.at], c.refs)
 
     params = dict(dimension_semantics=("arbitrary",), vmem_limit_bytes=VMEM_LIMIT)
     if comms:
@@ -670,11 +698,14 @@
     qs, os, us, ds = (sum(order[:i]) for i in range(4))
     ends = [i + 2 * LAG for i in (os, ds, sum(order))]
 
+    nu = nq // SUB
+    pack = sds((*CHIPS, 2, RB, nq), BF16)
+
     def G(*window):
         return [Gather(*window)] if comm else []
 
     def S(parts, **kw):
-        return [Scatter([(a.reshape(*CHIPS, 2, -1, a.shape[-1]), u0, n) for a, u0, n in parts], **kw)] if comm else []
+        return [Scatter([(a if a is pack else a.reshape(*CHIPS, 2, -1, a.shape[-1]), u0, n) for a, u0, n in parts], **kw)] if comm else []
 
     if comm:
         tile = jnp.pad(jnp.stack([ln1, ln2]), ((0, 6), (0, 128 - ln1.shape[0])))
@@ -735,27 +766,21 @@
     fd, = map(flat, full) if comm else (wd,)
 
     def dup_body(i, ins, outs, ext):
-        (dyr, w, gr, gpr, ht), (duo, gu), (acc,) = ins, outs, ext
+        (dyr, w, gpr, ht), (duo, gu) = ins, outs
         du = (dot_t(dyr[...], w[...]) * gpr[...]).astype(BF16)
         duo[...] = du
         gu[...] = dot(ht[...], du).astype(BF16)
-        put(acc, i, dot(gr[...], w[...]))
-
-    def y_body(i, ins, outs, ext):
-        (xr,), (o,), (acc,) = ins, outs, ext
-        o[...] = (xr[...].astype(F32) + acc[band(i)]).astype(BF16)
-
-    pd = [Phase(nf, [whole(dy), rows_of(fd, ft), cols_of(g, ft), cols_of(gp, ft), whole(h2t)], [cols_of(wide, ft), cols_of(b16(d, ff), ft)], dup_body),
-          Phase(nm, [rows_of(x1, tm)], [rows_of(act, tm)], y_body)]
+
+    pd = [Phase(nf, [whole(dy), rows_of(fd, ft), cols_of(gp, ft), whole(h2t)], [cols_of(wide, ft), cols_of(b16(d, ff), ft)], dup_body)]
     n_down = Unit(ff // 32, d).count
-    d_up, g_up, y, *r1 = host('dup', 4, pd, S([(g_down, 0, n_down)]), shared=[vm32(seq, d)])
+    d_up, g_up, *r1 = host('dup', 4, pd, S([(g_down, 0, n_down)]))
 
     def dh2_body(i, ins, outs, ext):
-        (du, w), (acc, _) = ins, ext
+        (du, w), acc = ins, ext[0]
         put(acc, i, dot_t(du[...], w[...]))
 
     def ln2b_body(i, ins, outs, ext):
-        (xr, dyr, lw), (dmo, gwo), (acc, dmb) = ins, outs, ext
+        (xr, dyr, lw), (dmo, gwo), (acc, dmb, *_) = ins, outs, ext
         dx, gw = norm_back(acc[band(i)], xr[...].astype(F32), lw[...])
         dm = dyr[...].astype(F32) + dx
         dmo[...] = dm
@@ -763,54 +788,85 @@
         put(gwo, i, gw)
 
     def dattn_body(i, ins, outs, ext):
-        (w, a), (da, go), (_, dmb) = ins, outs, ext
-        da[...] = dot_t(dmb[...], w[...]).astype(BF16)
-        go[...] = t_dot(a[...], dmb[...]).astype(BF16)
+        (w,), (_, dmb, da, *_) = ins, ext
+        r = dot_t(dmb[...], w[...]).astype(BF16)
+        for j in range(ft // hd):
+            da[i * (ft // hd) + j] = r[:, j * hd:(j + 1) * hd]
+
+    def battn_body(i, ins, outs, ext):
+        (q, k, v, a, l, sl), (o,), (acc, _, da) = ins, outs, ext
+        dk, dv = (acc.at[:, pl.ds(j * hd, hd)] for j in range(2))
+        attn_bwd(q.at[0], k.at[0], v.at[0], a, da.at[i], l.at[0], *(o.at[j, 0] for j in range(3)), dk, dv, sl[i], scale, tq)
+
+    def gout_body(i, ins, outs, ext):
+        (a,), (o,), (_, dmb, *_) = ins, outs, ext
+        o[...] = t_dot(a[...], dmb[...]).astype(BF16)
 
     pe = [Phase(nf, [cols_of(d_up, ft), cols_of(fu, ft)], [], dh2_body),
           Phase(nm, [rows_of(x1, tm), rows_of(dy, tm), whole(w2)], [rows_of(f32(seq, d), tm), one_vec], ln2b_body),
-          Phase(d // ft, [rows_of(fo, ft), cols_of(attn, ft)], [cols_of(act, ft), rows_of(b16(d, d), ft)], dattn_body)]
-    half = n_down // 2
-    d_mid, g_ln2, d_attn, g_out, *r2 = host('dh2', 5, pe, S([(g_up, 0, half)], carry=r1[1:]), shared=[vm32(seq, d), vm16(seq, d)])
-
-    def battn_body(i, ins, outs, ext):
-        (q, k, v, a, da, l, sl), (o,), (dk, dv) = ins, outs, ext
-        attn_bwd(q.at[0], k.at[0], v.at[0], a, da, l.at[0], *(o.at[j, 0] for j in range(3)), dk, dv, sl[i], scale, tq)
-
-    pf = [Phase(heads, [*(heads_of(qkv, 1, j * heads) for j in range(3)), cols_of(attn, hd), cols_of(d_attn, hd), heads_of(lse, 1), slopes],
-                [(b16(3, heads, seq, hd), (3, 1, seq, hd), lambda i: (0, i, 0, 0))], battn_body)]
-    d_qkv, *r3 = host('attn_bwd', 6, pf, S([(g_up, half, half)], carry=r2[1:]), shared=[vm32(seq, hd), vm32(seq, hd)])
+          Phase(d // ft, [rows_of(fo, ft)], [], dattn_body),
+          Phase(heads, [*(heads_of(qkv, 1, j * heads) for j in range(3)), cols_of(attn, hd), heads_of(lse, 1), slopes],
+                [(b16(3, heads, seq, hd), (3, 1, seq, hd), lambda i: (0, i, 0, 0))], battn_body),
+          Phase(d // ft, [cols_of(attn, ft)], [rows_of(b16(d, d), ft)], gout_body)]
+    d_mid, g_ln2, d_qkv, g_out, *r2 = host('dh2', 5, pe, S([(g_up, 0, n_down)], carry=r1[1:]),
+                                          shared=[vm32(seq, d), vm16(seq, d), vm16(heads, seq, hd)])
     d_qkv = d_qkv.reshape(3 * heads, seq, hd)
 
-    def gqkv_body(i, ins, outs, ext):
-        (ht, dq), (o,) = ins, outs
-        o[...] = dot(ht[...], side_by_side(dq, per)).astype(BF16)
-
-    g_qkv, *r4 = host('gqkv', 7, [Phase(nq // SUB, [whole(h1t), heads_of(d_qkv, per)], [cols_of(b16(d, nq), SUB)], gqkv_body)],
-                      S([(g_out, 0, d // SUB)], carry=r3[1:]))
-
-    def dh1_body(i, ins, outs, ext):
-        (dq, w), (acc,) = ins, ext
-        put(acc, i, dot_t(side_by_side(dq, 3), w[...]))
+    scat = S([(g_out, 0, d // SUB), (pack, 0, nu)], carry=r2[1:], last=True)
+
+    def tile_copy(i, ext):
+        at = Unit(RB, nq).at(i)
+        return pltpu.make_async_copy(ext[2].at[rest(i, 2)], scat[0].written().at[:, :, :, :, at[0], at[1]], ext[3].at[rest(i, 2)])
+
+    def macro_body(i, ins, outs, ext):
+        (ht, dq, w), acc = ins, ext[0]
+        tile = side_by_side(dq, per)
+        r = dot(ht[...], tile).astype(BF16)
+        if comm:
+            ext[2][rest(i, 2)] = r.reshape(*CHIPS, 2, RB, SUB)
+            tile_copy(i, ext).start()
+        else:
+            outs[0][...] = r
+        put(acc, i, dot_t(tile, w[...]))
+
+    def ship_body(i, ins, outs, ext):
+        tile_copy(i, ext).wait()
+        scat[0].ship(i)
 
     def ln1b_body(i, ins, outs, ext):
-        (xr, dm, lw), (o, gwo), (acc,) = ins, outs, ext
-        dx, gw = norm_back(acc[band(i)], xr[...].astype(F32), lw[...])
+        (xr, dm, lw), (o, gwo) = ins, outs
+        dx, gw = norm_back(ext[0][band(i)], xr[...].astype(F32), lw[...])
         o[...] = (dm[...] + dx).astype(BF16)
         put(gwo, i, gw)
 
-    ph = [Phase(heads, [heads_of(d_qkv, 3), cols_of(fq, 3 * hd)], [], dh1_body),
-          Phase(nm, [rows_of(x, tm), rows_of(d_mid, tm), whole(w1)], [rows_of(act, tm), one_vec], ln1b_body)]
-    comms = S([(g_qkv, 0, nq // SUB)], carry=r4[1:], last=True) + [SmallSum(g_ln2, heads + nm, d)] if comm else []
-    dx, g_ln1, *r5 = host('dh1', 8, ph, comms, shared=[vm32(seq, d)])
+    def ydot_body(i, ins, outs, ext):
+        (gr, w) = ins
+        put(ext[1], i, dot(gr[...], w[...]))
+
+    def y_body(i, ins, outs, ext):
+        (xr,), (o,) = ins, outs
+        o[...] = (xr[...].astype(F32) + ext[1][band(i)]).astype(BF16)
+
+    first = [] if comm else [cols_of(b16(d, nq), SUB)]
+    pf = [Phase(nu, [whole(h1t), heads_of(d_qkv, per), cols_of(fq, SUB)], first, macro_body, 0, 2),
+          Phase(nm, [rows_of(x, tm), rows_of(d_mid, tm), whole(w1)], [rows_of(act, tm), one_vec], ln1b_body, 2 * nu, 2),
+          Phase(nf, [cols_of(g, ft), rows_of(fd, ft)], [], ydot_body, 1, 2),
+          Phase(nm, [rows_of(x1, tm)], [rows_of(act, tm)], y_body, 2 * nf + 1, 2)]
+    if comm:
+        pf.append(Phase(nu, [], [], ship_body, 1, 2))
+        scat.append(SmallSum(g_ln2, 1, pf[1].end(), d))
+    shared = [vm32(seq, d), vm32(seq, d), vm16(2, *CHIPS, 2, RB, SUB), pltpu.SemaphoreType.DMA((2,))]
+    got = host('last', 6, pf, scat, shared=shared)
     if not comm:
+        g_qkv, dx, g_ln1, y = got
         return y, dx, g_ln1, g_qkv, g_out, g_ln2, g_up, g_down
-    units = jnp.concatenate([r[0] for r in (r1, r2, r3, r4, r5)])
+    dx, _, y, r3, _, sums = got
+    units = jnp.concatenate([r1[0], r2[0], r3])
     nc = d // SUB
     g_down, g_up, g_out, g_qkv = jnp.split(units, (n_down, 2 * n_down, 2 * n_down + nc))
     flat_rows = lambda u: u.transpose(1, 0, 2).reshape(RB, -1)
     g_down = g_down.reshape(-1, nc, RB, SUB).transpose(0, 2, 1, 3).reshape(-1, d)
-    return y, dx, r5[1], flat_rows(g_qkv), flat_rows(g_out), None, flat_rows(g_up), g_down
+    return y, dx, sums, flat_rows(g_qkv), flat_rows(g_out), None, flat_rows(g_up), g_down
 
 
 def solution(mesh):

time: 687 us -> 653 us (0.951); the launches traced: 678 us -> 652 us
  Pallas kernels: 655 us -> 629 us
    pallas_call x8 -> x6, Pallas kernels: 655 us -> 629 us  [host(): pl.pallas_call(kernel, grid=(total,), in_specs=in_specs, out_specs=out_sp...]
where the time goes in v4:
time: 653 us; the launch traced here: 652 us
  Pallas kernels  629 us (96%)
  local copies, waits for them, and re-layouts  19.8 us (3%)
    pallas_call x6, Pallas kernels, host(): pl.pallas_call(kernel, grid=(total,), in_specs=in_specs, out_specs=out_sp...  629 us

profile of v4, /device:TPU:0, one launch (start us, length us, event | category | flops | bytes accessed | tf_op | source)
XLA Modules:
  0.0 652.3 jit_solution(16681660892422662179)
XLA Ops:
  0.6 1.2 copy.23
  1.8 1.1 reshape.63.refs_0_
  2.9 1.3 select_maximum_fusion.refs_3_
  4.1 101.1 %ag_qkv.1 = (bf16[4,2,2,2,48,4608]{5,4,3,2,1,0:T(8,128)(2,1)}, bf16[4,2,2,2,48,1536]{5,4,3,2,1,0:T(8,128)(2,1)}, bf16[4,2,2,2,48,6144]{5,4,3,2,1,0:T(8,128)(2,1)}, f32[4,2,2,2,8,128]{5,4,3,2,1,0:T(8,128)}) custom-call(bf16[48,4608]{1,0:T(8,128)(2,1)} %reshape.63.refs_0_, bf16[48,1536]{1,0:T(8,128)(2,1)} %refs_4_.1, bf16[48,6144]{1,0:T(8,128)(2,1)} %refs_6_.2, ...), custom_call_target="tpu_custom_call" | custom-call | flops 17179869184 | bytes 33554432 | tf_op jit(solution)/shard_map/ag_qkv/pallas_call | solution.py:549
  105.3 0.9 slice.16
  106.2 0.7 unstack.13.refs_1_.refs_5_
  106.9 108.6 %attn_fwd.1 = (bf16[1536,1024]{1,0:T(8,128)(2,1)}, bf16[36,1024,128]{2,1,0:T(8,128)(2,1)}, bf16[1024,1536]{1,0:T(8,128)(2,1)}, f32[12,1024,1]{2,1,0:T(8,128)}, b...) custom-call(bf16[1024,1536]{1,0:T(8,128)(2,1)} %bitcast.54, ...), custom_call_target="tpu_custom_call", output_to_operand_aliasing={{4}: (5, {}), {5}: (7, {})} | custom-call | flops 17179869184 | bytes 33554432 | tf_op jit(solution)/shard_map/attn_fwd/pallas_call | solution.py:549
  215.5 0.7 unstack.15.refs_3_.refs_4_
  216.2 85.2 %up.1 = (bf16[1024,1536]{1,0:T(8,128)(2,1)}, bf16[1536,1024]{1,0:T(8,128)(2,1)}, bf16[1024,6144]{1,0:T(8,128)(2,1)}, f32[1024,6144]{1,0:T(8,128)}, bf16[6144,153...) custom-call(bf16[1024,1536]{1,0:T(8,128)(2,1)} %bitcast.55, ...), custom_call_target="tpu_custom_call", output_to_operand_aliasing={{5}: (7, {})} | custom-call | flops 17179869184 | bytes 33554432 | tf_op jit(solution)/shard_map/up/pallas_call | solution.py:549
  301.4 87.2 %dup.1 = (bf16[1024,6144]{1,0:T(8,128)(2,1)}, bf16[1536,6144]{1,0:T(8,128)(2,1)}, f32[8,48,512]{2,1,0:T(8,128)}, bf16[2,2,4,2,48,256]{5,4,3,2,1,0:T(8,128)(2,1)}, bf16[2,4,48,512]{3,2,1,0:T(8,128)(2,1)}) custom-call(bf16[1024,1536]{1,0:T(8,128)(2,1)} %bitcast.46, bf16[6144,1536]{1,0:T(8,128)(2,1)} %bitcast.37, f32[1024,6144]{1,0:T(8,128)} %get-tuple-element.51.refs_2_, ...), custom_call_target="tpu_custom_call" | custom-call | flops 17179869184 | bytes 33554432 | tf_op jit(solution)/shard_map/dup/pallas_call | solution.py:549
  388.7 115.9 %dh2.1 = (f32[1024,1536]{1,0:T(8,128)}, f32[1,1536]{1,0:T(1,128)}, bf16[3,12,1024,128]{3,2,1,0:T(8,128)(2,1)}, bf16[1536,1536]{1,0:T(8,128)(2,1)}, f32[12,48,512...) custom-call(bf16[1024,6144]{1,0:T(8,128)(2,1)} %get-tuple-element.54.refs_0_, ...), custom_call_target="tpu_custom_call" | custom-call | flops 17179869184 | bytes 33554432 | tf_op jit(solution)/shard_map/dh2/pallas_call | solution.py:549
  504.5 130.5 %last.1 = (bf16[1024,1536]{1,0:T(8,128)(2,1)}, f32[1,1536]{1,0:T(1,128)}, bf16[1024,1536]{1,0:T(8,128)(2,1)}, f32[16,48,512]{2,1,0:T(8,128)}, bf16[4,2,2,2,48,46...) custom-call(bf16[1536,1024]{1,0:T(8,128)(2,1)} %get-tuple-element.45.refs_0_, bf16[36,1024,128]{2,1,0:T(8,128)(2,1)} %bitcast.48, ...), custom_call_target="tpu_custom_call" | custom-call | flops 17179869184 | bytes 33554432 | tf_op jit(solution)/shard_map/last/pallas_call | solution.py:549
  635.1 1.8 pad_maximum_fusion
  636.9 0.8 copy.28
  637.7 0.0 copy-start
  637.7 1.5 copy.33
  639.2 1.1 copy.32
  640.3 0.0 copy-done
  640.3 0.1 slice_bitcast_fusion
  640.4 0.6 copy.25
  640.9 1.3 reshape_reshape.3
  642.2 2.4 copy.29
  644.6 0.7 copy.31
  645.4 0.8 constant_dynamic-slice_fusion
  646.1 0.5 slice_bitcast_fusion.2
  646.7 0.0 copy-start.1
  646.7 3.9 copy.41
  650.6 0.0 copy-done.1
  650.6 1.7 copy.42
  (3 shorter events, 0.0 us)
Async XLA Ops:
  637.7 2.6 copy-start
  646.7 3.9 copy-start.1

commit v5 on v4

--- a/solution.py
+++ b/solution.py
@@ -10,8 +10,10 @@
 
 EPS = 1e-5
 SUB = 512
+WIDE = 768
 HALF = SUB // 2
 LAG = 2
+GLAG = 1
 CARRY = 2 * LAG
 LEAD = 3
 RB = 48
@@ -50,8 +52,8 @@
 
 
 class Phase:
-    def __init__(self, n, ins, outs, body, at=None, stride=1):
-        self.n, self.ins, self.outs, self.body, self.at, self.stride = n, ins, outs, body, at, stride
+    def __init__(self, n, cost, ins, outs, body, at=None, stride=1):
+        self.n, self.cost, self.ins, self.outs, self.body, self.at, self.stride = n, cost, ins, outs, body, at, stride
 
     def own(self, t):
         return quot(t - self.at, self.stride)
@@ -80,9 +82,14 @@
 
 def locate():
     me = lax.axis_index('fsdp')
-    z, y, x, c = quot(me, 8), rest(quot(me, 4), 2), rest(quot(me, 2), 2), rest(me, 2)
-    HERE.update(coords=(me, z, y, x, c), peers=([rest(me + 8 * d, 32) for d in (1, 2, 3)], me + 4 - 8 * y, me + 2 - 4 * x, me + 1 - 2 * c),
-                zs=[rest(z + d, 4) for d in (1, 2, 3)])
+    left, place = me, []
+    for n in (2, *reversed(CHIPS)):
+        place.append(rest(left, n))
+        left = quot(left, n)
+    c, x, y, z = place
+    n, step, ways = CHIPS[0], 8, (1, 2, 3)
+    cp, xp, yp = (me + s - 2 * s * b for s, b in zip((1, 2, 4), place))
+    HERE.update(coords=(me, z, y, x, c), peers=([rest(me + step * d, step * n) for d in ways], yp, xp, cp), zs=[rest(z + d, n) for d in ways])
 
 
 def coords():
@@ -98,35 +105,35 @@
 
 
 class Unit:
-    def __init__(self, rows, cols):
-        self.nc, self.nr = cols // SUB, rows // RB
+    def __init__(self, rows, cols, width=SUB):
+        self.width, self.nc, self.nr = width, cols // width, rows // RB
         self.count = self.nc * self.nr
 
     def at(self, u, half=None):
-        col = pl.multiple_of(rest(u, self.nc) * SUB, HALF)
-        width = SUB
+        lanes, col = self.width, rest(u, self.nc) * self.width
         if half is not None:
-            col, width = pl.multiple_of(col + half * HALF, HALF), HALF
+            lanes //= 2
+            col = col + half * lanes
         rows = slice(None) if self.nr == 1 else pl.ds(pl.multiple_of(quot(u, self.nc) * RB, 16), RB)
-        return rows, pl.ds(col, width)
+        return rows, pl.ds(pl.multiple_of(col, 128), lanes)
 
 
 class Gather:
     def __init__(self, weights, k0, k1):
         self.k0, self.k1 = k0, k1
-        self.k = k1 - k0 + 1
+        self.k, self.tail = k1 - k0 + 1, 0
         self.z0 = k0 + LEAD if k0 else 0
         self.z1 = k1 + LEAD
         self.w, self.ins, self.outs, self.alias = [], [], [], []
         for shard, full, first in weights:
-            unit = Unit(*shard.shape)
+            unit = Unit(*shard.shape, WIDE)
             self.w.append((len(self.ins), unit, first, first + unit.count, full is None))
             self.ins.append((shard, pl.BlockSpec(memory_space=pltpu.VMEM)))
             if full is not None:
                 self.alias.append((len(self.ins), len(self.outs)))
                 self.ins.append((full, pl.BlockSpec(memory_space=HBM)))
             self.outs.append((sds(CHIPS + (2,) + shard.shape, BF16), pl.BlockSpec(memory_space=HBM)))
-        self.base = max(k0 - 2 * LAG, 0)
+        self.base = max(k0 - 2 * GLAG, 0)
         n = self.z1 - self.base
         self.scratch = [pltpu.SemaphoreType.DMA((n, 8)), pltpu.SemaphoreType.DMA((n, 8)), pltpu.SemaphoreType.DMA((len(weights),))]
 
@@ -177,7 +184,7 @@
     def step(self, k, fire, refs):
         me, z, y, x, c = coords()
         k0, k1, k = self.k0, self.k1, k + self.k0
-        span = [(self.z0, self.z1)] + [(max(k0 - i * LAG, 0), k1 - i * LAG) for i in range(3)]
+        span = [(self.z0, self.z1)] + [(max(k0 - i * GLAG, 0), k1 - i * GLAG) for i in range(3)]
 
         @pl.when(fire & (k == k0))
         def _():
@@ -194,7 +201,7 @@
         def _():
             self.each(*span[0], k + LEAD, lambda w, u: self.go(0, w, u, refs))
             for stage in (1, 2, 3):
-                u = k + LAG * (1 - stage)
+                u = k + GLAG * (1 - stage)
                 lo, hi = span[stage - 1]
                 self.each(lo, hi, u, lambda w, u: self.arrive(stage - 1, w, u, refs))
                 self.each(*span[stage], u, lambda w, u: self.go(stage, w, u, refs))
@@ -203,13 +210,13 @@
         def _():
             for stage in range(4):
                 lo, hi = span[stage]
-                self.each(max(lo, k1 - stage * LAG) if stage < 3 else lo, hi, None, lambda w, u: self.arrive(stage, w, u, refs))
+                self.each(max(lo, k1 - stage * GLAG) if stage < 3 else lo, hi, None, lambda w, u: self.arrive(stage, w, u, refs))
                 self.each(lo, hi, None, lambda w, u: self.left(stage, w, u, refs))
 
 
 class GatherSmall:
     def __init__(self, tile):
-        self.k, self.alias = 5, []
+        self.k, self.alias, self.tail = 5, [], 0
         self.ins = [(tile, pl.BlockSpec(memory_space=pltpu.VMEM))]
         self.outs = [(sds(CHIPS + (2,) + tile.shape, F32), pl.BlockSpec(memory_space=HBM))]
         self.scratch = [pltpu.SemaphoreType.DMA((6,)), pltpu.SemaphoreType.DMA((6,)), pltpu.SemaphoreType.DMA]
@@ -264,6 +271,7 @@
         self.end = n + CARRY
         self.done = self.end if last else n
         self.k = n + (3 * LAG if last else 1)
+        self.tail = 3 * LAG - 1 if last else 0
         self.two_shape, self.three_shape = (2, 4, 2, RB, HALF), (4, RB, SUB)
         if self.carried:
             self.ins += [(a, pl.BlockSpec(memory_space=pltpu.VMEM)) for a in carry]
@@ -372,8 +380,7 @@
             def _(j):
                 self.swap(j, refs, start)
 
-            for j in range(CARRY, min(CARRY + 2, end)):
-                self.local(j, refs, start)
+            self.local(CARRY, refs, start)
             if self.carried:
                 for i in range(LAG):
                     two[LAG + i] = refs[len(self.ins) - 2][i]
@@ -384,11 +391,11 @@
         @pl.when(fire & (k < n))
         def _():
             j = k + CARRY
+            pl.when(j + 1 < end)(lambda: self.local(j + 1, refs, start))
             self.swap(j, refs, lambda cp: cp.wait_recv())
             self.local(j, refs, lambda cp: cp.wait())
             self.add(1, j, refs)
             go(1, j)
-            pl.when(j + 2 < end)(lambda: self.local(j + 2, refs, start))
 
         lows = [CARRY, LAG, 0] if self.carried else [CARRY] * 3
         for stage, low in zip((2, 3, 4), lows):
@@ -424,7 +431,7 @@
 
 class SmallSum:
     def __init__(self, row, at, t0, d):
-        self.at, self.t0, self.k = at, t0, 1
+        self.at, self.t0, self.k, self.tail = at, t0, 1, 0
         self.ins = [(row, pl.BlockSpec(memory_space=pltpu.VMEM))]
         self.outs = [(sds((8, d), F32), pl.BlockSpec(memory_space=pltpu.VMEM))]
         self.alias = []
@@ -459,7 +466,10 @@
                     copy.start()
 
 
-def host(name, cid, phases, comms=(), shared=(), cost=None):
+KERNELS = ['gather', 'attention', 'up', 'down', 'back', 'last']
+
+
+def host(name, phases, comms=(), shared=(), pace=1):
     k_all = max([c.k for c in comms], default=1)
     at = 0
     for p in phases:
@@ -467,8 +477,14 @@
             p.at = at
         at = max(at, p.end())
     small = [c for c in comms if isinstance(c, SmallSum)]
-    total = max([at, k_all] + [c.t0 + 5 for c in small])
-    kmap = lambda t: t if total == k_all else quot(t * (k_all - 1), total - 1)
+    tail = max([c.tail for c in comms], default=0)
+    spread, clock, fires = k_all - 1 - tail, [0.0], [0]
+    for t in range(at):
+        clock.append(clock[-1] + sum(p.cost for p in phases if p.at <= t < p.end() and (t - p.at) % p.stride == 0))
+    for k in range(1, k_all):
+        t = at if k >= spread else min(t for t in range(at + 1) if clock[t] * spread >= clock[at] * k)
+        fires.append(max(t, fires[-1] + 1, pace * k))
+    total = max([at, fires[-1] + 1] + [c.t0 + 5 for c in small])
     ins, in_specs, outs, out_specs, scratch, alias, resident = [], [], [], [], [], {}, []
     for p in phases:
         for arr, block, index in p.ins:
@@ -511,8 +527,8 @@
                     pl.semaphore_signal(bar, inc=1, device_id=(dev,), device_id_type=MESH)
                 pl.semaphore_wait(bar, len(near))
         i, o, s = sum(len(p.ins) for p in phases), sum(len(p.outs) for p in phases), 0
-        k = kmap(t)
-        fire = (t == 0) | (k != kmap(jnp.maximum(t - 1, 0)))
+        k = sum([(t >= f).astype(jnp.int32) for f in fires[1:]], 0 * t)
+        fire = functools.reduce(jnp.logical_or, [t == f for f in fires])
         for c in comms:
             ni, no, ns = len(c.ins), len(c.outs), len(c.scratch)
             crefs = rin[i:i + ni] + rout[o:o + no] + rscr[s:s + ns]
@@ -545,7 +561,7 @@
 
     params = dict(dimension_semantics=("arbitrary",), vmem_limit_bytes=VMEM_LIMIT)
     if comms:
-        params.update(collective_id=cid, has_side_effects=True)
+        params.update(collective_id=KERNELS.index(name), has_side_effects=True)
     got = pl.pallas_call(kernel, grid=(total,), in_specs=in_specs, out_specs=out_specs, out_shape=outs, scratch_shapes=scratch,
                          input_output_aliases=alias, compiler_params=pltpu.CompilerParams(**params), name=name,
                          cost_estimate=pl.CostEstimate(flops=2 ** 34, bytes_accessed=2 ** 25, transcendentals=0))(*ins)
@@ -694,9 +710,9 @@
     one_vec = (vec, vec.shape, lambda i: (0, 0))
     band = lambda i: pl.ds(pl.multiple_of(i * tm, tm), tm)
     flat = lambda full: full.reshape(-1, full.shape[-1])
-    order = [Unit(*w.shape).count for w in (wq, wo, wu, wd)]
+    order = [Unit(*w.shape, WIDE).count for w in (wq, wo, wu, wd)]
     qs, os, us, ds = (sum(order[:i]) for i in range(4))
-    ends = [i + 2 * LAG for i in (os, ds, sum(order))]
+    ends = [i + 2 * GLAG for i in (os, ds, sum(order))]
 
     nu = nq // SUB
     pack = sds((*CHIPS, 2, RB, nq), BF16)
@@ -709,7 +725,7 @@
 
     if comm:
         tile = jnp.pad(jnp.stack([ln1, ln2]), ((0, 6), (0, 128 - ln1.shape[0])))
-        fq, fo, fu, lns = host('ag_qkv', 1, [], G([(wq, None, qs), (wo, None, os), (wu, None, us)], 0, ends[0]) + [GatherSmall(tile)])
+        fq, fo, fu, lns = host('gather', [], G([(wq, None, qs), (wo, None, os), (wu, None, us)], 0, ends[0]) + [GatherSmall(tile)])
         fq = flat(fq)
         w1, w2 = lns.reshape(-1, 8, 128)[:, :2, :ln1.shape[0]].transpose(1, 0, 2).reshape(2, 1, d)
     else:
@@ -733,10 +749,10 @@
         (sl,), (o, l), (qkv, _) = ins, outs, ext
         attn_fwd(qkv.at[i], qkv.at[heads + i], qkv.at[2 * heads + i], o, l.at[0], sl[i], scale, tq)
 
-    pb = [Phase(nm, [rows_of(x, tm), whole(w1)], [cols_of(b16(d, seq), tm)], ln1_body),
-          Phase(nq // SUB, [cols_of(fq, SUB)], [heads_of(b16(3 * heads, seq, hd), per)], qkv_body),
-          Phase(heads, [slopes], [cols_of(act, hd), heads_of(f32(heads, seq, 1), 1)], attn_body)]
-    h1t, qkv, attn, lse, *full = host('attn_fwd', 2, pb, G([(wo, fo, os), (wu, fu, us), (wd, None, ds)], ends[0], ends[1]),
+    pb = [Phase(nm, 0.5, [rows_of(x, tm), whole(w1)], [cols_of(b16(d, seq), tm)], ln1_body),
+          Phase(nq // SUB, 1.9, [cols_of(fq, SUB)], [heads_of(b16(3 * heads, seq, hd), per)], qkv_body),
+          Phase(heads, 1.8, [slopes], [cols_of(act, hd), heads_of(f32(heads, seq, 1), 1)], attn_body)]
+    h1t, qkv, attn, lse, *full = host('attention', pb, G([(wo, fo, os), (wu, fu, us), (wd, None, ds)], ends[0], ends[1]),
                                       shared=[vm16(3 * heads, seq, hd), vm16(seq, d)])
     if comm:
         fo, fu, fd = full
@@ -760,9 +776,9 @@
         gpo[...] = cdf + u * (jnp.exp(-0.5 * u * u) * math.sqrt(0.5 / math.pi))
         gd[...] = t_dot(g, dyr[...]).astype(BF16)
 
-    pc = [Phase(nm, [rows_of(x, tm), rows_of(attn, tm), whole(fo), whole(w2)], [rows_of(act, tm), cols_of(b16(d, seq), tm)], out_body),
-          Phase(nf, [cols_of(fu, ft), whole(dy)], [cols_of(wide, ft), cols_of(f32(seq, ff), ft), rows_of(b16(ff, d), ft)], up_body)]
-    x1, h2t, g, gp, g_down, *full = host('up', 3, pc, G([(wd, fd, ds)], ends[1], ends[2]) if comm else [], shared=[vm16(seq, d)])
+    pc = [Phase(nm, 1.4, [rows_of(x, tm), rows_of(attn, tm), whole(fo), whole(w2)], [rows_of(act, tm), cols_of(b16(d, seq), tm)], out_body),
+          Phase(nf, 4.0, [cols_of(fu, ft), whole(dy)], [cols_of(wide, ft), cols_of(f32(seq, ff), ft), rows_of(b16(ff, d), ft)], up_body)]
+    x1, h2t, g, gp, g_down, *full = host('up', pc, G([(wd, fd, ds)], ends[1], ends[2]) if comm else [], shared=[vm16(seq, d)])
     fd, = map(flat, full) if comm else (wd,)
 
     def dup_body(i, ins, outs, ext):
@@ -771,9 +787,9 @@
         duo[...] = du
         gu[...] = dot(ht[...], du).astype(BF16)
 
-    pd = [Phase(nf, [whole(dy), rows_of(fd, ft), cols_of(gp, ft), whole(h2t)], [cols_of(wide, ft), cols_of(b16(d, ff), ft)], dup_body)]
+    pd = [Phase(nf, 3.9, [whole(dy), rows_of(fd, ft), cols_of(gp, ft), whole(h2t)], [cols_of(wide, ft), cols_of(b16(d, ff), ft)], dup_body)]
     n_down = Unit(ff // 32, d).count
-    d_up, g_up, *r1 = host('dup', 4, pd, S([(g_down, 0, n_down)]))
+    d_up, g_up, *r1 = host('down', pd, S([(g_down, 0, n_down)]))
 
     def dh2_body(i, ins, outs, ext):
         (du, w), acc = ins, ext[0]
@@ -802,28 +818,28 @@
         (a,), (o,), (_, dmb, *_) = ins, outs, ext
         o[...] = t_dot(a[...], dmb[...]).astype(BF16)
 
-    pe = [Phase(nf, [cols_of(d_up, ft), cols_of(fu, ft)], [], dh2_body),
-          Phase(nm, [rows_of(x1, tm), rows_of(dy, tm), whole(w2)], [rows_of(f32(seq, d), tm), one_vec], ln2b_body),
-          Phase(d // ft, [rows_of(fo, ft)], [], dattn_body),
-          Phase(heads, [*(heads_of(qkv, 1, j * heads) for j in range(3)), cols_of(attn, hd), heads_of(lse, 1), slopes],
+    pe = [Phase(nf, 2.3, [cols_of(d_up, ft), cols_of(fu, ft)], [], dh2_body),
+          Phase(nm, 0.7, [rows_of(x1, tm), rows_of(dy, tm), whole(w2)], [rows_of(f32(seq, d), tm), one_vec], ln2b_body),
+          Phase(d // ft, 1.9, [rows_of(fo, ft)], [], dattn_body),
+          Phase(heads, 2.9, [*(heads_of(qkv, 1, j * heads) for j in range(3)), cols_of(attn, hd), heads_of(lse, 1), slopes],
                 [(b16(3, heads, seq, hd), (3, 1, seq, hd), lambda i: (0, i, 0, 0))], battn_body),
-          Phase(d // ft, [cols_of(attn, ft)], [rows_of(b16(d, d), ft)], gout_body)]
-    d_mid, g_ln2, d_qkv, g_out, *r2 = host('dh2', 5, pe, S([(g_up, 0, n_down)], carry=r1[1:]),
+          Phase(d // ft, 1.9, [cols_of(attn, ft)], [rows_of(b16(d, d), ft)], gout_body)]
+    d_mid, g_ln2, d_qkv, g_out, *r2 = host('back', pe, S([(g_up, 0, n_down)], carry=r1[1:]),
                                           shared=[vm32(seq, d), vm16(seq, d), vm16(heads, seq, hd)])
     d_qkv = d_qkv.reshape(3 * heads, seq, hd)
 
     scat = S([(g_out, 0, d // SUB), (pack, 0, nu)], carry=r2[1:], last=True)
 
     def tile_copy(i, ext):
-        at = Unit(RB, nq).at(i)
-        return pltpu.make_async_copy(ext[2].at[rest(i, 2)], scat[0].written().at[:, :, :, :, at[0], at[1]], ext[3].at[rest(i, 2)])
+        r, q = Unit(RB, nq).at(i)
+        return pltpu.make_async_copy(ext[2], scat[0].written().at[:, :, :, :, r, q], ext[3])
 
     def macro_body(i, ins, outs, ext):
         (ht, dq, w), acc = ins, ext[0]
         tile = side_by_side(dq, per)
         r = dot(ht[...], tile).astype(BF16)
         if comm:
-            ext[2][rest(i, 2)] = r.reshape(*CHIPS, 2, RB, SUB)
+            ext[2][...] = r.reshape(*CHIPS, 2, RB, SUB)
             tile_copy(i, ext).start()
         else:
             outs[0][...] = r
@@ -848,15 +864,15 @@
         o[...] = (xr[...].astype(F32) + ext[1][band(i)]).astype(BF16)
 
     first = [] if comm else [cols_of(b16(d, nq), SUB)]
-    pf = [Phase(nu, [whole(h1t), heads_of(d_qkv, per), cols_of(fq, SUB)], first, macro_body, 0, 2),
-          Phase(nm, [rows_of(x, tm), rows_of(d_mid, tm), whole(w1)], [rows_of(act, tm), one_vec], ln1b_body, 2 * nu, 2),
-          Phase(nf, [cols_of(g, ft), rows_of(fd, ft)], [], ydot_body, 1, 2),
-          Phase(nm, [rows_of(x1, tm)], [rows_of(act, tm)], y_body, 2 * nf + 1, 2)]
+    pf = [Phase(nu, 3.9, [whole(h1t), heads_of(d_qkv, per), cols_of(fq, SUB)], first, macro_body, 0, 2),
+          Phase(nm, 0.7, [rows_of(x, tm), rows_of(d_mid, tm), whole(w1)], [rows_of(act, tm), one_vec], ln1b_body, 2 * nu, 2),
+          Phase(nf, 2.3, [cols_of(g, ft), rows_of(fd, ft)], [], ydot_body, 1, 2),
+          Phase(nm, 0.4, [rows_of(x1, tm)], [rows_of(act, tm)], y_body, 2 * nf + 1, 2)]
     if comm:
-        pf.append(Phase(nu, [], [], ship_body, 1, 2))
+        pf.append(Phase(nu, 0, [], [], ship_body, 1, 2))
         scat.append(SmallSum(g_ln2, 1, pf[1].end(), d))
-    shared = [vm32(seq, d), vm32(seq, d), vm16(2, *CHIPS, 2, RB, SUB), pltpu.SemaphoreType.DMA((2,))]
-    got = host('last', 6, pf, scat, shared=shared)
+    shared = [vm32(seq, d), vm32(seq, d), vm16(*CHIPS, 2, RB, SUB), pltpu.SemaphoreType.DMA]
+    got = host('last', pf, scat, shared=shared, pace=2)
     if not comm:
         g_qkv, dx, g_ln1, y = got
         return y, dx, g_ln1, g_qkv, g_out, g_ln2, g_up, g_down

time: 653 us -> 643 us (0.985)
  Pallas kernels: 629 us -> 619 us
    pallas_call x6, Pallas kernels: 629 us -> 619 us  [host(): pl.pallas_call(kernel, grid=(total,), in_specs=in_specs, out_specs=out_sp...]
where the time goes in v5:
time: 643 us; the launch traced here: 642 us
  Pallas kernels  619 us (96%)
  local copies, waits for them, and re-layouts  19.8 us (3%)
    pallas_call x6, Pallas kernels, host(): pl.pallas_call(kernel, grid=(total,), in_specs=in_specs, out_specs=out_sp...  619 us

profile of v5, /device:TPU:0, one launch (start us, length us, event | category | flops | bytes accessed | tf_op | source)
XLA Modules:
  0.0 642.2 jit_solution(5508153233928592500)
XLA Ops:
  0.6 1.2 copy.23
  1.8 1.1 reshape.63.refs_0_
  2.9 1.3 select_maximum_fusion.refs_3_
  4.1 97.0 %gather.1 = (bf16[4,2,2,2,48,4608]{5,4,3,2,1,0:T(8,128)(2,1)}, bf16[4,2,2,2,48,1536]{5,4,3,2,1,0:T(8,128)(2,1)}, bf16[4,2,2,2,48,6144]{5,4,3,2,1,0:T(8,128)(2,1)}, f32[4,2,2,2,8,128]{5,4,3,2,1,0:T(8,128)}) custom-call(bf16[48,4608]{1,0:T(8,128)(2,1)} %reshape.63.refs_0_, bf16[48,1536]{1,0:T(8,128)(2,1)} %refs_4_.1, bf16[48,6144]{1,0:T(8,128)(2,1)} %refs_6_.2, ...), custom_call_target="tpu_custom_call" | custom-call | flops 17179869184 | bytes 33554432 | tf_op jit(solution)/shard_map/gather/pallas_call | solution.py:565
  101.1 0.9 slice.16
  102.0 0.7 unstack.13.refs_1_.refs_5_
  102.7 104.5 %attention.1 = (bf16[1536,1024]{1,0:T(8,128)(2,1)}, bf16[36,1024,128]{2,1,0:T(8,128)(2,1)}, bf16[1024,1536]{1,0:T(8,128)(2,1)}, f32[12,1024,1]{2,1,0:T(8,128)}, ...) custom-call(bf16[1024,1536]{1,0:T(8,128)(2,1)} %bitcast.54, ...), custom_call_target="tpu_custom_call", output_to_operand_aliasing={{4}: (5, {}), {5}: (7, {})} | custom-call | flops 17179869184 | bytes 33554432 | tf_op jit(solution)/shard_map/attention/pallas_call | solution.py:565
  207.2 0.7 unstack.15.refs_3_.refs_4_
  207.9 79.1 %up.1 = (bf16[1024,1536]{1,0:T(8,128)(2,1)}, bf16[1536,1024]{1,0:T(8,128)(2,1)}, bf16[1024,6144]{1,0:T(8,128)(2,1)}, f32[1024,6144]{1,0:T(8,128)}, bf16[6144,153...) custom-call(bf16[1024,1536]{1,0:T(8,128)(2,1)} %bitcast.55, ...), custom_call_target="tpu_custom_call", output_to_operand_aliasing={{5}: (7, {})} | custom-call | flops 17179869184 | bytes 33554432 | tf_op jit(solution)/shard_map/up/pallas_call | solution.py:565
  287.0 89.3 %down.1 = (bf16[1024,6144]{1,0:T(8,128)(2,1)}, bf16[1536,6144]{1,0:T(8,128)(2,1)}, f32[8,48,512]{2,1,0:T(8,128)}, bf16[2,2,4,2,48,256]{5,4,3,2,1,0:T(8,128)(2,1)}, bf16[2,4,48,512]{3,2,1,0:T(8,128)(2,1)}) custom-call(bf16[1024,1536]{1,0:T(8,128)(2,1)} %bitcast.46, bf16[6144,1536]{1,0:T(8,128)(2,1)} %bitcast.37, f32[1024,6144]{1,0:T(8,128)} %get-tuple-element.51.refs_2_, ...), custom_call_target="tpu_custom_call" | custom-call | flops 17179869184 | bytes 33554432 | tf_op jit(solution)/shard_map/down/pallas_call | solution.py:565
  376.3 116.0 %back.1 = (f32[1024,1536]{1,0:T(8,128)}, f32[1,1536]{1,0:T(1,128)}, bf16[3,12,1024,128]{3,2,1,0:T(8,128)(2,1)}, bf16[1536,1536]{1,0:T(8,128)(2,1)}, f32[12,48,51...) custom-call(bf16[1024,6144]{1,0:T(8,128)(2,1)} %get-tuple-element.54.refs_0_, ...), custom_call_target="tpu_custom_call" | custom-call | flops 17179869184 | bytes 33554432 | tf_op jit(solution)/shard_map/back/pallas_call | solution.py:565
  492.3 132.7 %last.1 = (bf16[1024,1536]{1,0:T(8,128)(2,1)}, f32[1,1536]{1,0:T(1,128)}, bf16[1024,1536]{1,0:T(8,128)(2,1)}, f32[16,48,512]{2,1,0:T(8,128)}, bf16[4,2,2,2,48,46...) custom-call(bf16[1536,1024]{1,0:T(8,128)(2,1)} %get-tuple-element.45.refs_0_, bf16[36,1024,128]{2,1,0:T(8,128)(2,1)} %bitcast.48, ...), custom_call_target="tpu_custom_call" | custom-call | flops 17179869184 | bytes 33554432 | tf_op jit(solution)/shard_map/last/pallas_call | solution.py:565
  625.1 1.8 pad_maximum_fusion
  626.9 0.8 copy.28
  627.7 0.0 copy-start
  627.7 1.5 copy.33
  629.2 1.1 copy.32
  630.3 0.0 copy-done
  630.3 0.1 slice_bitcast_fusion
  630.3 0.6 copy.25
  630.9 1.3 reshape_reshape.3
  632.2 2.4 copy.29
  634.6 0.7 copy.31
  635.4 0.8 constant_dynamic-slice_fusion
  636.1 0.5 slice_bitcast_fusion.2
  636.7 0.0 copy-start.1
  636.7 3.9 copy.41
  640.6 0.0 copy-done.1
  640.6 1.7 copy.42
  (3 shorter events, 0.0 us)
Async XLA Ops:
  627.7 2.6 copy-start
  636.7 3.9 copy-start.1

commit v6 on v5

--- a/solution.py
+++ b/solution.py
@@ -9,11 +9,11 @@
 from jax.sharding import PartitionSpec as P
 
 EPS = 1e-5
+LOG2E = math.log2(math.e)
 SUB = 512
 WIDE = 768
 HALF = SUB // 2
-LAG = 2
-GLAG = 1
+LAG = 1
 CARRY = 2 * LAG
 LEAD = 3
 RB = 48
@@ -52,21 +52,14 @@
 
 
 class Phase:
-    def __init__(self, n, cost, ins, outs, body, at=None, stride=1):
-        self.n, self.cost, self.ins, self.outs, self.body, self.at, self.stride = n, cost, ins, outs, body, at, stride
-
-    def own(self, t):
-        return quot(t - self.at, self.stride)
+    def __init__(self, n, cost, ins, outs, body, at=None):
+        self.n, self.cost, self.ins, self.outs, self.body, self.at = n, cost, ins, outs, body, at
 
     def on(self, t):
-        here = (t >= self.at) & (t < self.end())
-        return here if self.stride == 1 else here & (rest(t - self.at, self.stride) == 0)
-
-    def end(self):
-        return self.at + (self.n - 1) * self.stride + 1
+        return (t >= self.at) & (t < self.at + self.n)
 
     def index(self, f):
-        return lambda t: f(clip(self.own(jnp.maximum(t, self.at)), self.n))
+        return lambda t: f(clip(t - self.at, self.n))
 
 
 def quot(a, b):
@@ -133,7 +126,7 @@
                 self.alias.append((len(self.ins), len(self.outs)))
                 self.ins.append((full, pl.BlockSpec(memory_space=HBM)))
             self.outs.append((sds(CHIPS + (2,) + shard.shape, BF16), pl.BlockSpec(memory_space=HBM)))
-        self.base = max(k0 - 2 * GLAG, 0)
+        self.base = max(k0 - 2 * LAG, 0)
         n = self.z1 - self.base
         self.scratch = [pltpu.SemaphoreType.DMA((n, 8)), pltpu.SemaphoreType.DMA((n, 8)), pltpu.SemaphoreType.DMA((len(weights),))]
 
@@ -184,7 +177,7 @@
     def step(self, k, fire, refs):
         me, z, y, x, c = coords()
         k0, k1, k = self.k0, self.k1, k + self.k0
-        span = [(self.z0, self.z1)] + [(max(k0 - i * GLAG, 0), k1 - i * GLAG) for i in range(3)]
+        span = [(self.z0, self.z1)] + [(max(k0 - i * LAG, 0), k1 - i * LAG) for i in range(3)]
 
         @pl.when(fire & (k == k0))
         def _():
@@ -201,7 +194,7 @@
         def _():
             self.each(*span[0], k + LEAD, lambda w, u: self.go(0, w, u, refs))
             for stage in (1, 2, 3):
-                u = k + GLAG * (1 - stage)
+                u = k + LAG * (1 - stage)
                 lo, hi = span[stage - 1]
                 self.each(lo, hi, u, lambda w, u: self.arrive(stage - 1, w, u, refs))
                 self.each(*span[stage], u, lambda w, u: self.go(stage, w, u, refs))
@@ -210,7 +203,7 @@
         def _():
             for stage in range(4):
                 lo, hi = span[stage]
-                self.each(max(lo, k1 - stage * GLAG) if stage < 3 else lo, hi, None, lambda w, u: self.arrive(stage, w, u, refs))
+                self.each(max(lo, k1 - stage * LAG) if stage < 3 else lo, hi, None, lambda w, u: self.arrive(stage, w, u, refs))
                 self.each(lo, hi, None, lambda w, u: self.left(stage, w, u, refs))
 
 
@@ -469,21 +462,21 @@
 KERNELS = ['gather', 'attention', 'up', 'down', 'back', 'last']
 
 
-def host(name, phases, comms=(), shared=(), pace=1):
+def host(name, phases, comms=(), shared=()):
     k_all = max([c.k for c in comms], default=1)
     at = 0
     for p in phases:
         if p.at is None:
             p.at = at
-        at = max(at, p.end())
+        at = max(at, p.at + p.n)
     small = [c for c in comms if isinstance(c, SmallSum)]
     tail = max([c.tail for c in comms], default=0)
     spread, clock, fires = k_all - 1 - tail, [0.0], [0]
     for t in range(at):
-        clock.append(clock[-1] + sum(p.cost for p in phases if p.at <= t < p.end() and (t - p.at) % p.stride == 0))
+        clock.append(clock[-1] + sum(p.cost for p in phases if p.at <= t < p.at + p.n))
     for k in range(1, k_all):
         t = at if k >= spread else min(t for t in range(at + 1) if clock[t] * spread >= clock[at] * k)
-        fires.append(max(t, fires[-1] + 1, pace * k))
+        fires.append(max(t, fires[-1] + 1))
     total = max([at, fires[-1] + 1] + [c.t0 + 5 for c in small])
     ins, in_specs, outs, out_specs, scratch, alias, resident = [], [], [], [], [], {}, []
     for p in phases:
@@ -554,7 +547,7 @@
 
             @pl.when(p.on(t))
             def _(p=p, pi=pi, po=po):
-                p.body(p.own(t), pi, po, extra)
+                p.body(t - p.at, pi, po, extra)
 
         for c in small:
             c.run(t, rout[c.at], c.refs)
@@ -590,68 +583,61 @@
     return jnp.array(ordered[:n_heads], dtype=F32)
 
 
-def causal(i, tq, slope):
-    row = lax.broadcasted_iota(jnp.int32, (tq, tq), 0)
-    col = lax.broadcasted_iota(jnp.int32, (tq, tq), 1)
-    rel = (row - col).astype(F32)
-    diag = slope * rel
-    past = None
-    if i:
-        r = lax.broadcasted_iota(jnp.int32, (tq, i * tq), 0) + i * tq
-        q = lax.broadcasted_iota(jnp.int32, (tq, i * tq), 1)
-        past = slope * (r - q).astype(F32)
-    return past, diag, row >= col
+def bias(i, tq, slope):
+    def ahead(n, first):
+        return lax.broadcasted_iota(jnp.int32, (1, n), 1).astype(F32) * slope + slope * first
+
+    row, col = (lax.broadcasted_iota(jnp.int32, (tq, tq), a) for a in range(2))
+    return ahead(tq, 0.0), ahead(i * tq, -float(i * tq)) if i else None, row >= col
 
 
 def attn_fwd(q_ref, k_ref, v_ref, o_ref, l_ref, slope, scale, tq):
-    n = q_ref.shape[0] // tq
-    for i in range(n):
+    slope, scale = slope * LOG2E, scale * LOG2E
+    for i in range(q_ref.shape[0] // tq):
         rows, before = pl.ds(i * tq, tq), pl.ds(0, i * tq)
         q = q_ref[rows]
-        past, diag, keep = causal(i, tq, slope)
-        sd = jnp.where(keep, dot_t(q, k_ref[rows]) * scale - diag, -jnp.inf)
+        near, far, keep = bias(i, tq, slope)
+        sd = jnp.where(keep, dot_t(q, k_ref[rows]) * scale + near, -jnp.inf)
         m = row_max(sd)
         if i:
-            sp = dot_t(q, k_ref[before]) * scale - past
+            sp = dot_t(q, k_ref[before]) * scale + far
             m = jnp.maximum(m, row_max(sp))
-            ep = jnp.exp(sp - m)
-        ed = jnp.exp(sd - m)
+            ep = jnp.exp2(sp - m)
+        ed = jnp.exp2(sd - m)
         l = row_sum(ed)
         if i:
             l = l + row_sum(ep)
-        inv = 1.0 / l
+        inv = 1 / l
         o = dot((ed * inv).astype(BF16), v_ref[rows])
         if i:
             o = o + dot((ep * inv).astype(BF16), v_ref[before])
         o_ref[rows] = o.astype(BF16)
-        l_ref[rows] = m + jnp.log(l)
+        l_ref[rows] = m + jnp.log2(l)
 
 
 def attn_bwd(q_ref, k_ref, v_ref, a_ref, da_ref, l_ref, dq_ref, dk_ref, dv_ref, dk_s, dv_s, slope, scale, tq):
-    n = q_ref.shape[0] // tq
+    slope2, scale2 = slope * LOG2E, scale * LOG2E
     dk_s[...] = jnp.zeros_like(dk_s)
     dv_s[...] = jnp.zeros_like(dv_s)
-    for i in range(n):
+    for i in range(q_ref.shape[0] // tq):
         rows, before = pl.ds(i * tq, tq), pl.ds(0, i * tq)
         q, da = q_ref[rows], da_ref[rows]
         lse = l_ref[rows]
         delta = row_sum(da.astype(F32) * a_ref[rows].astype(F32))
-        past, diag, keep = causal(i, tq, slope)
+        near, far, keep = bias(i, tq, slope2)
         dq = None
-        for own in ((True,) if i == 0 else (True, False)):
-            keys = rows if own else before
+        for keys, ahead in ((rows, near), (before, far))[:2 if i else 1]:
             kk, vv = k_ref[keys], v_ref[keys]
-            s = dot_t(q, kk) * scale - (diag if own else past)
-            p = jnp.exp(s - lse)
-            if own:
-                p = jnp.where(keep, p, 0.0)
-            ds = (p * (dot_t(da, vv) - delta) * scale).astype(BF16)
+            p = jnp.exp2(dot_t(q, kk) * scale2 + ahead - lse)
+            if keys is rows:
+                p = jnp.where(keep, p, 0)
+            ds = (p * (dot_t(da, vv) - delta)).astype(BF16)
             dv_s[keys] += t_dot(p.astype(BF16), da)
             dk_s[keys] += t_dot(ds, q)
             part = dot(ds, kk)
             dq = part if dq is None else dq + part
-        dq_ref[rows] = dq.astype(BF16)
-    dk_ref[...] = dk_s[...].astype(BF16)
+        dq_ref[rows] = (dq * scale).astype(BF16)
+    dk_ref[...] = (dk_s[...] * scale).astype(BF16)
     dv_ref[...] = dv_s[...].astype(BF16)
 
 
@@ -682,11 +668,9 @@
 def put(ref, i, part):
     @pl.when(i == 0)
     def _():
-        ref[...] = part
-
-    @pl.when(i > 0)
-    def _():
-        ref[...] += part
+        ref[...] = jnp.zeros_like(ref)
+
+    ref[...] += part()
 
 
 def side_by_side(ref, n):
@@ -699,7 +683,7 @@
     ff, nq, per = wu.shape[1], 3 * d, SUB // hd
     scale = 1 / math.sqrt(hd)
     tq = min(256, seq)
-    tm = tq // 2
+    tm = tq
     nm, nf = seq // tm, ff // ft
     slopes = (alibi_slopes(heads), 'smem', None)
     b16 = lambda *shape: sds(shape, BF16)
@@ -712,7 +696,7 @@
     flat = lambda full: full.reshape(-1, full.shape[-1])
     order = [Unit(*w.shape, WIDE).count for w in (wq, wo, wu, wd)]
     qs, os, us, ds = (sum(order[:i]) for i in range(4))
-    ends = [i + 2 * GLAG for i in (os, ds, sum(order))]
+    ends = [i + 2 * LAG for i in (os, ds, sum(order))]
 
     nu = nq // SUB
     pack = sds((*CHIPS, 2, RB, nq), BF16)
@@ -749,9 +733,9 @@
         (sl,), (o, l), (qkv, _) = ins, outs, ext
         attn_fwd(qkv.at[i], qkv.at[heads + i], qkv.at[2 * heads + i], o, l.at[0], sl[i], scale, tq)
 
-    pb = [Phase(nm, 0.5, [rows_of(x, tm), whole(w1)], [cols_of(b16(d, seq), tm)], ln1_body),
+    pb = [Phase(nm, 1, [rows_of(x, tm), whole(w1)], [cols_of(b16(d, seq), tm)], ln1_body),
           Phase(nq // SUB, 1.9, [cols_of(fq, SUB)], [heads_of(b16(3 * heads, seq, hd), per)], qkv_body),
-          Phase(heads, 1.8, [slopes], [cols_of(act, hd), heads_of(f32(heads, seq, 1), 1)], attn_body)]
+          Phase(heads, 2.2, [slopes], [cols_of(act, hd), heads_of(f32(heads, seq, 1), 1)], attn_body)]
     h1t, qkv, attn, lse, *full = host('attention', pb, G([(wo, fo, os), (wu, fu, us), (wd, None, ds)], ends[0], ends[1]),
                                       shared=[vm16(3 * heads, seq, hd), vm16(seq, d)])
     if comm:
@@ -776,24 +760,30 @@
         gpo[...] = cdf + u * (jnp.exp(-0.5 * u * u) * math.sqrt(0.5 / math.pi))
         gd[...] = t_dot(g, dyr[...]).astype(BF16)
 
-    pc = [Phase(nm, 1.4, [rows_of(x, tm), rows_of(attn, tm), whole(fo), whole(w2)], [rows_of(act, tm), cols_of(b16(d, seq), tm)], out_body),
+    pc = [Phase(nm, 3, [rows_of(x, tm), rows_of(attn, tm), whole(fo), whole(w2)], [rows_of(act, tm), cols_of(b16(d, seq), tm)], out_body),
           Phase(nf, 4.0, [cols_of(fu, ft), whole(dy)], [cols_of(wide, ft), cols_of(f32(seq, ff), ft), rows_of(b16(ff, d), ft)], up_body)]
     x1, h2t, g, gp, g_down, *full = host('up', pc, G([(wd, fd, ds)], ends[1], ends[2]) if comm else [], shared=[vm16(seq, d)])
     fd, = map(flat, full) if comm else (wd,)
 
     def dup_body(i, ins, outs, ext):
-        (dyr, w, gpr, ht), (duo, gu) = ins, outs
+        (dyr, w, gr, gpr, ht), (duo, gu), (acc,) = ins, outs, ext
         du = (dot_t(dyr[...], w[...]) * gpr[...]).astype(BF16)
         duo[...] = du
         gu[...] = dot(ht[...], du).astype(BF16)
-
-    pd = [Phase(nf, 3.9, [whole(dy), rows_of(fd, ft), cols_of(gp, ft), whole(h2t)], [cols_of(wide, ft), cols_of(b16(d, ff), ft)], dup_body)]
+        put(acc, i, lambda: dot(gr[...], w[...]))
+
+    def y_body(i, ins, outs, ext):
+        (xr,), (o,), (acc,) = ins, outs, ext
+        o[...] = (xr[...].astype(F32) + acc[band(i)]).astype(BF16)
+
+    pd = [Phase(nf, 6, [whole(dy), rows_of(fd, ft), cols_of(g, ft), cols_of(gp, ft), whole(h2t)], [cols_of(wide, ft), cols_of(b16(d, ff), ft)], dup_body),
+          Phase(nm, 1, [rows_of(x1, tm)], [rows_of(act, tm)], y_body)]
     n_down = Unit(ff // 32, d).count
-    d_up, g_up, *r1 = host('down', pd, S([(g_down, 0, n_down)]))
+    d_up, g_up, y, *r1 = host('down', pd, S([(g_down, 0, n_down)]), shared=[vm32(seq, d)])
 
     def dh2_body(i, ins, outs, ext):
         (du, w), acc = ins, ext[0]
-        put(acc, i, dot_t(du[...], w[...]))
+        put(acc, i, lambda: dot_t(du[...], w[...]))
 
     def ln2b_body(i, ins, outs, ext):
         (xr, dyr, lw), (dmo, gwo), (acc, dmb, *_) = ins, outs, ext
@@ -801,7 +791,7 @@
         dm = dyr[...].astype(F32) + dx
         dmo[...] = dm
         dmb[band(i)] = dm.astype(BF16)
-        put(gwo, i, gw)
+        put(gwo, i, lambda: gw)
 
     def dattn_body(i, ins, outs, ext):
         (w,), (_, dmb, da, *_) = ins, ext
@@ -818,10 +808,10 @@
         (a,), (o,), (_, dmb, *_) = ins, outs, ext
         o[...] = t_dot(a[...], dmb[...]).astype(BF16)
 
-    pe = [Phase(nf, 2.3, [cols_of(d_up, ft), cols_of(fu, ft)], [], dh2_body),
-          Phase(nm, 0.7, [rows_of(x1, tm), rows_of(dy, tm), whole(w2)], [rows_of(f32(seq, d), tm), one_vec], ln2b_body),
+    pe = [Phase(nf, 2.4, [cols_of(d_up, ft), cols_of(fu, ft)], [], dh2_body),
+          Phase(nm, 2, [rows_of(x1, tm), rows_of(dy, tm), whole(w2)], [rows_of(f32(seq, d), tm), one_vec], ln2b_body),
           Phase(d // ft, 1.9, [rows_of(fo, ft)], [], dattn_body),
-          Phase(heads, 2.9, [*(heads_of(qkv, 1, j * heads) for j in range(3)), cols_of(attn, hd), heads_of(lse, 1), slopes],
+          Phase(heads, 3.5, [*(heads_of(qkv, 1, j * heads) for j in range(3)), cols_of(attn, hd), heads_of(lse, 1), slopes],
                 [(b16(3, heads, seq, hd), (3, 1, seq, hd), lambda i: (0, i, 0, 0))], battn_body),
           Phase(d // ft, 1.9, [cols_of(attn, ft)], [rows_of(b16(d, d), ft)], gout_body)]
     d_mid, g_ln2, d_qkv, g_out, *r2 = host('back', pe, S([(g_up, 0, n_down)], carry=r1[1:]),
@@ -832,18 +822,18 @@
 
     def tile_copy(i, ext):
         r, q = Unit(RB, nq).at(i)
-        return pltpu.make_async_copy(ext[2], scat[0].written().at[:, :, :, :, r, q], ext[3])
+        return pltpu.make_async_copy(ext[1].at[rest(i, 2)], scat[0].written().at[:, :, :, :, r, q], ext[2].at[rest(i, 2)])
 
     def macro_body(i, ins, outs, ext):
         (ht, dq, w), acc = ins, ext[0]
         tile = side_by_side(dq, per)
         r = dot(ht[...], tile).astype(BF16)
         if comm:
-            ext[2][...] = r.reshape(*CHIPS, 2, RB, SUB)
+            ext[1][rest(i, 2)] = r.reshape(*CHIPS, 2, RB, SUB)
             tile_copy(i, ext).start()
         else:
             outs[0][...] = r
-        put(acc, i, dot_t(tile, w[...]))
+        put(acc, i, lambda: dot_t(tile, w[...]))
 
     def ship_body(i, ins, outs, ext):
         tile_copy(i, ext).wait()
@@ -853,30 +843,20 @@
         (xr, dm, lw), (o, gwo) = ins, outs
         dx, gw = norm_back(ext[0][band(i)], xr[...].astype(F32), lw[...])
         o[...] = (dm[...] + dx).astype(BF16)
-        put(gwo, i, gw)
-
-    def ydot_body(i, ins, outs, ext):
-        (gr, w) = ins
-        put(ext[1], i, dot(gr[...], w[...]))
-
-    def y_body(i, ins, outs, ext):
-        (xr,), (o,) = ins, outs
-        o[...] = (xr[...].astype(F32) + ext[1][band(i)]).astype(BF16)
+        put(gwo, i, lambda: gw)
 
     first = [] if comm else [cols_of(b16(d, nq), SUB)]
-    pf = [Phase(nu, 3.9, [whole(h1t), heads_of(d_qkv, per), cols_of(fq, SUB)], first, macro_body, 0, 2),
-          Phase(nm, 0.7, [rows_of(x, tm), rows_of(d_mid, tm), whole(w1)], [rows_of(act, tm), one_vec], ln1b_body, 2 * nu, 2),
-          Phase(nf, 2.3, [cols_of(g, ft), rows_of(fd, ft)], [], ydot_body, 1, 2),
-          Phase(nm, 0.4, [rows_of(x1, tm)], [rows_of(act, tm)], y_body, 2 * nf + 1, 2)]
+    pf = [Phase(nu, 3.9, [whole(h1t), heads_of(d_qkv, per), cols_of(fq, SUB)], first, macro_body),
+          Phase(nm, 2, [rows_of(x, tm), rows_of(d_mid, tm), whole(w1)], [rows_of(act, tm), one_vec], ln1b_body)]
     if comm:
-        pf.append(Phase(nu, 0, [], [], ship_body, 1, 2))
-        scat.append(SmallSum(g_ln2, 1, pf[1].end(), d))
-    shared = [vm32(seq, d), vm32(seq, d), vm16(*CHIPS, 2, RB, SUB), pltpu.SemaphoreType.DMA]
-    got = host('last', pf, scat, shared=shared, pace=2)
+        pf.append(Phase(nu, 0, [], [], ship_body, 1))
+        scat.append(SmallSum(g_ln2, 1, nu + nm, d))
+    shared = [vm32(seq, d), vm16(2, *CHIPS, 2, RB, SUB), pltpu.SemaphoreType.DMA((2,))]
+    got = host('last', pf, scat, shared=shared)
     if not comm:
-        g_qkv, dx, g_ln1, y = got
+        g_qkv, dx, g_ln1 = got
         return y, dx, g_ln1, g_qkv, g_out, g_ln2, g_up, g_down
-    dx, _, y, r3, _, sums = got
+    dx, _, r3, _, sums = got
     units = jnp.concatenate([r1[0], r2[0], r3])
     nc = d // SUB
     g_down, g_up, g_out, g_qkv = jnp.split(units, (n_down, 2 * n_down, 2 * n_down + nc))

time: 643 us -> 623 us (0.969)
  Pallas kernels: 619 us -> 599 us
    pallas_call x6, Pallas kernels: 619 us -> 599 us  [host(): pl.pallas_call(kernel, grid=(total,), in_specs=in_specs, out_specs=out_sp...]
where the time goes in v6:
time: 623 us; the launch traced here: 622 us
  Pallas kernels  599 us (96%)
  local copies, waits for them, and re-layouts  19.8 us (3%)
    pallas_call x6, Pallas kernels, host(): pl.pallas_call(kernel, grid=(total,), in_specs=in_specs, out_specs=out_sp...  599 us

profile of v6, /device:TPU:0, one launch (start us, length us, event | category | flops | bytes accessed | tf_op | source)
XLA Modules:
  0.0 622.5 jit_solution(11909534862637880430)
XLA Ops:
  0.6 1.2 copy.23
  1.8 1.1 reshape.63.refs_0_
  2.9 1.3 select_maximum_fusion.refs_3_
  4.1 97.0 %gather.1 = (bf16[4,2,2,2,48,4608]{5,4,3,2,1,0:T(8,128)(2,1)}, bf16[4,2,2,2,48,1536]{5,4,3,2,1,0:T(8,128)(2,1)}, bf16[4,2,2,2,48,6144]{5,4,3,2,1,0:T(8,128)(2,1)}, f32[4,2,2,2,8,128]{5,4,3,2,1,0:T(8,128)}) custom-call(bf16[48,4608]{1,0:T(8,128)(2,1)} %reshape.63.refs_0_, bf16[48,1536]{1,0:T(8,128)(2,1)} %refs_4_.1, bf16[48,6144]{1,0:T(8,128)(2,1)} %refs_6_.2, ...), custom_call_target="tpu_custom_call" | custom-call | flops 17179869184 | bytes 33554432 | tf_op jit(solution)/shard_map/gather/pallas_call | solution.py:558
  101.1 0.9 slice.16
  102.0 0.7 unstack.13.refs_1_.refs_5_
  102.7 104.7 %attention.1 = (bf16[1536,1024]{1,0:T(8,128)(2,1)}, bf16[36,1024,128]{2,1,0:T(8,128)(2,1)}, bf16[1024,1536]{1,0:T(8,128)(2,1)}, f32[12,1024,1]{2,1,0:T(8,128)}, ...) custom-call(bf16[1024,1536]{1,0:T(8,128)(2,1)} %bitcast.60, ...), custom_call_target="tpu_custom_call", output_to_operand_aliasing={{4}: (5, {}), {5}: (7, {})} | custom-call | flops 17179869184 | bytes 33554432 | tf_op jit(solution)/shard_map/attention/pallas_call | solution.py:558
  207.4 0.7 unstack.15.refs_3_.refs_4_
  208.1 78.6 %up.1 = (bf16[1024,1536]{1,0:T(8,128)(2,1)}, bf16[1536,1024]{1,0:T(8,128)(2,1)}, bf16[1024,6144]{1,0:T(8,128)(2,1)}, f32[1024,6144]{1,0:T(8,128)}, bf16[6144,153...) custom-call(bf16[1024,1536]{1,0:T(8,128)(2,1)} %bitcast.61, ...), custom_call_target="tpu_custom_call", output_to_operand_aliasing={{5}: (7, {})} | custom-call | flops 17179869184 | bytes 33554432 | tf_op jit(solution)/shard_map/up/pallas_call | solution.py:558
  286.8 101.8 %down.1 = (bf16[1024,6144]{1,0:T(8,128)(2,1)}, bf16[1536,6144]{1,0:T(8,128)(2,1)}, bf16[1024,1536]{1,0:T(8,128)(2,1)}, f32[10,48,512]{2,1,0:T(8,128)}, bf16[1,2,...) custom-call(bf16[1024,1536]{1,0:T(8,128)(2,1)} %bitcast.43, bf16[6144,1536]{1,0:T(8,128)(2,1)} %bitcast.40, ...), custom_call_target="tpu_custom_call" | custom-call | flops 17179869184 | bytes 33554432 | tf_op jit(solution)/shard_map/down/pallas_call | solution.py:558
  388.6 107.9 %back.1 = (f32[1024,1536]{1,0:T(8,128)}, f32[1,1536]{1,0:T(1,128)}, bf16[3,12,1024,128]{3,2,1,0:T(8,128)(2,1)}, bf16[1536,1536]{1,0:T(8,128)(2,1)}, f32[12,48,51...) custom-call(bf16[1024,6144]{1,0:T(8,128)(2,1)} %get-tuple-element.57.refs_0_, ...), custom_call_target="tpu_custom_call" | custom-call | flops 17179869184 | bytes 33554432 | tf_op jit(solution)/shard_map/back/pallas_call | solution.py:558
  496.5 108.7 %last.1 = (bf16[1024,1536]{1,0:T(8,128)(2,1)}, f32[1,1536]{1,0:T(1,128)}, f32[14,48,512]{2,1,0:T(8,128)}, bf16[4,2,2,2,48,4608]{5,4,3,2,1,0:T(8,128)(2,1)}, f32[8,1536]{1,0:T(8,128)}) custom-call(bf16[1536,1024]{1,0:T(8,128)(2,1)} %get-tuple-element.56.refs_0_, bf16[36,1024,128]{2,1,0:T(8,128)(2,1)} %bitcast.58, bf16[1536,4608]{1,0:T(8,128)(2,1)} %bitcast.64, ...), custom_call_target="tpu_custom_call" | custom-call | flops 17179869184 | bytes 33554432 | tf_op jit(solution)/shard_map/last/pallas_call | solution.py:558
  605.2 1.9 pad_maximum_fusion
  607.1 0.8 copy.28
  607.9 0.0 copy-start
  607.9 1.5 copy.33
  609.4 1.1 copy.32
  610.5 0.0 copy-done
  610.5 0.1 slice_bitcast_fusion
  610.6 0.6 copy.25
  611.1 1.3 reshape_reshape.3
  612.4 2.4 copy.29
  614.8 0.7 copy.31
  615.6 0.8 constant_dynamic-slice_fusion
  616.4 0.5 slice_bitcast_fusion.2
  616.9 0.0 copy-start.1
  616.9 3.9 copy.41
  620.8 0.0 copy-done.1
  620.8 1.7 copy.42
  (3 shorter events, 0.0 us)
Async XLA Ops:
  607.9 2.6 copy-start
  616.9 3.9 copy-start.1

commit v7 on v6

--- a/solution.py
+++ b/solution.py
@@ -13,7 +13,9 @@
 SUB = 512
 WIDE = 768
 HALF = SUB // 2
-LAG = 1
+LAG = 2
+GLAG = 1
+THIRD = 3
 CARRY = 2 * LAG
 LEAD = 3
 RB = 48
@@ -126,32 +128,45 @@
                 self.alias.append((len(self.ins), len(self.outs)))
                 self.ins.append((full, pl.BlockSpec(memory_space=HBM)))
             self.outs.append((sds(CHIPS + (2,) + shard.shape, BF16), pl.BlockSpec(memory_space=HBM)))
-        self.base = max(k0 - 2 * LAG, 0)
+        self.base = max(k0 - 2 * GLAG, 0)
         n = self.z1 - self.base
-        self.scratch = [pltpu.SemaphoreType.DMA((n, 8)), pltpu.SemaphoreType.DMA((n, 8)), pltpu.SemaphoreType.DMA((len(weights),))]
-
-    def copies(self, stage, w, u, refs):
+        self.scratch = [pltpu.SemaphoreType.DMA((n, 12)), pltpu.SemaphoreType.DMA((n, 12)), pltpu.SemaphoreType.DMA((len(weights),))]
+
+    def copies(self, stage, w, u, turned, refs):
         i, unit, first, _, _ = self.w[w]
         shard, full = refs[i], refs[len(self.ins) + w]
         sems = lambda i: (refs[-3].at[u - self.base, i], refs[-2].at[u - self.base, i])
         me, z, y, x, c = coords()
         zs, yp, xp, cp = peers()
         r, q = unit.at(u - first)
+        sides = [unit.at(u - first, half) for half in range(2)]
+        if stage == 0 and not turned:
+            return [remote(shard.at[r, q], full.at[z, y, x, c, r, q], *sems(d), dev) for d, dev in enumerate(zs)]
         if stage == 0:
-            return [remote(shard.at[r, q], full.at[z, y, x, c, r, q], *sems(d), zs[d]) for d in range(3)]
+            return [remote(shard.at[r, q], full.at[z, y, x, c, r, q], *sems(j), dev) for j, ((r, q), dev) in enumerate(zip(sides, (yp, xp)))]
         if stage == 3:
             v = full.at[:, :, :, c, r, q]
-            return [remote(v, v, *sems(7), cp)]
-        out = []
-        for half in range(2):
-            r, q = unit.at(u - first, half)
-            j = 2 * stage + 1 + half
-            if stage == 1:
-                v = full.at[:, y, x, c, r, q]
-            else:
-                v = full.at[:, y, :, c, r, q] if half else full.at[:, :, x, c, r, q]
-            out.append(remote(v, v, *sems(j), xp if half == stage % 2 else yp))
-        return out
+            return [remote(v, v, *sems(11), cp)]
+        (ra, qa), (rb, qb) = sides
+        if stage == 2:
+            views = [(full.at[:, :, x, c, ra, qa], xp), (full.at[:, y, :, c, rb, qb], yp)]
+        elif turned:
+            views = [(v, dev) for v in (full.at[z, :, x, c, ra, qa], full.at[z, y, :, c, rb, qb]) for dev in zs]
+        else:
+            views = [(full.at[:, y, x, c, ra, qa], yp), (full.at[:, y, x, c, rb, qb], xp)]
+        return [remote(v, v, *sems(6 * stage - 3 + j), dev) for j, (v, dev) in enumerate(views)]
+
+    def act(self, what, stage, w, u, refs):
+        def run(turned):
+            for cp in self.copies(stage, w, u, turned, refs):
+                getattr(cp, what)()
+
+        if stage < 2:
+            odd = rest(u, THIRD) == 1
+            pl.when(odd)(lambda: run(True))
+            pl.when(jnp.logical_not(odd))(lambda: run(False))
+        else:
+            run(False)
 
     def each(self, lo, hi, u, fn):
         for w, (_, _, first, last, _) in enumerate(self.w):
@@ -162,22 +177,19 @@
                 else:
                     pl.when((u >= a) & (u < b))(functools.partial(fn, w, u))
 
-    def go(self, stage, w, u, refs):
-        for cp in self.copies(stage, w, u, refs):
-            cp.start()
-
-    def arrive(self, stage, w, u, refs):
-        for cp in self.copies(stage, w, u, refs):
-            cp.wait_recv()
-
-    def left(self, stage, w, u, refs):
-        for cp in self.copies(stage, w, u, refs):
-            cp.wait_send()
+    def go(self, *args):
+        self.act('start', *args)
+
+    def arrive(self, *args):
+        self.act('wait_recv', *args)
+
+    def left(self, *args):
+        self.act('wait_send', *args)
 
     def step(self, k, fire, refs):
         me, z, y, x, c = coords()
         k0, k1, k = self.k0, self.k1, k + self.k0
-        span = [(self.z0, self.z1)] + [(max(k0 - i * LAG, 0), k1 - i * LAG) for i in range(3)]
+        span = [(self.z0, self.z1)] + [(max(k0 - i * GLAG, 0), k1 - i * GLAG) for i in range(3)]
 
         @pl.when(fire & (k == k0))
         def _():
@@ -194,7 +206,7 @@
         def _():
             self.each(*span[0], k + LEAD, lambda w, u: self.go(0, w, u, refs))
             for stage in (1, 2, 3):
-                u = k + LAG * (1 - stage)
+                u = k + GLAG * (1 - stage)
                 lo, hi = span[stage - 1]
                 self.each(lo, hi, u, lambda w, u: self.arrive(stage - 1, w, u, refs))
                 self.each(*span[stage], u, lambda w, u: self.go(stage, w, u, refs))
@@ -203,7 +215,7 @@
         def _():
             for stage in range(4):
                 lo, hi = span[stage]
-                self.each(max(lo, k1 - stage * LAG) if stage < 3 else lo, hi, None, lambda w, u: self.arrive(stage, w, u, refs))
+                self.each(max(lo, k1 - stage * GLAG) if stage < 3 else lo, hi, None, lambda w, u: self.arrive(stage, w, u, refs))
                 self.each(lo, hi, None, lambda w, u: self.left(stage, w, u, refs))
 
 
@@ -621,7 +633,7 @@
     dv_s[...] = jnp.zeros_like(dv_s)
     for i in range(q_ref.shape[0] // tq):
         rows, before = pl.ds(i * tq, tq), pl.ds(0, i * tq)
-        q, da = q_ref[rows], da_ref[rows]
+        q, da = q_ref[rows], da_ref[rows].astype(BF16)
         lse = l_ref[rows]
         delta = row_sum(da.astype(F32) * a_ref[rows].astype(F32))
         near, far, keep = bias(i, tq, slope2)
@@ -657,8 +669,8 @@
     return a, (a.shape[0], n), col_map
 
 
-def heads_of(a, n, off=0):
-    return a, (n,) + a.shape[1:], lambda i: (i + off, 0, 0)
+def heads_of(a, n):
+    return a, (n,) + a.shape[1:], lambda i: (i, 0, 0)
 
 
 def whole(a):
@@ -696,7 +708,7 @@
     flat = lambda full: full.reshape(-1, full.shape[-1])
     order = [Unit(*w.shape, WIDE).count for w in (wq, wo, wu, wd)]
     qs, os, us, ds = (sum(order[:i]) for i in range(4))
-    ends = [i + 2 * LAG for i in (os, ds, sum(order))]
+    ends = [i + 2 * GLAG for i in (os, ds, sum(order))]
 
     nu = nq // SUB
     pack = sds((*CHIPS, 2, RB, nq), BF16)
@@ -794,28 +806,27 @@
         put(gwo, i, lambda: gw)
 
     def dattn_body(i, ins, outs, ext):
-        (w,), (_, dmb, da, *_) = ins, ext
-        r = dot_t(dmb[...], w[...]).astype(BF16)
-        for j in range(ft // hd):
-            da[i * (ft // hd) + j] = r[:, j * hd:(j + 1) * hd]
+        (w,), (acc, dmb, *_) = ins, ext
+        acc[:, pl.ds(pl.multiple_of(i * ft, ft), ft)] = dot_t(dmb[...], w[...])
 
     def battn_body(i, ins, outs, ext):
-        (q, k, v, a, l, sl), (o,), (acc, _, da) = ins, outs, ext
-        dk, dv = (acc.at[:, pl.ds(j * hd, hd)] for j in range(2))
-        attn_bwd(q.at[0], k.at[0], v.at[0], a, da.at[i], l.at[0], *(o.at[j, 0] for j in range(3)), dk, dv, sl[i], scale, tq)
+        (qkv, a, l, sl), (o,), (acc, _, dk, dv) = ins, outs, ext
+        da = acc.at[:, pl.ds(pl.multiple_of(i * hd, hd), hd)]
+        attn_bwd(*(qkv.at[j, 0] for j in range(3)), a, da, l.at[0], *(o.at[j, 0] for j in range(3)), dk, dv, sl[i], scale, tq)
 
     def gout_body(i, ins, outs, ext):
         (a,), (o,), (_, dmb, *_) = ins, outs, ext
         o[...] = t_dot(a[...], dmb[...]).astype(BF16)
 
+    triple = lambda a: (a, (3, 1, seq, hd), lambda i: (0, i, 0, 0))
     pe = [Phase(nf, 2.4, [cols_of(d_up, ft), cols_of(fu, ft)], [], dh2_body),
           Phase(nm, 2, [rows_of(x1, tm), rows_of(dy, tm), whole(w2)], [rows_of(f32(seq, d), tm), one_vec], ln2b_body),
           Phase(d // ft, 1.9, [rows_of(fo, ft)], [], dattn_body),
-          Phase(heads, 3.5, [*(heads_of(qkv, 1, j * heads) for j in range(3)), cols_of(attn, hd), heads_of(lse, 1), slopes],
-                [(b16(3, heads, seq, hd), (3, 1, seq, hd), lambda i: (0, i, 0, 0))], battn_body),
+          Phase(heads, 3.5, [triple(qkv.reshape(3, heads, seq, hd)), cols_of(attn, hd), heads_of(lse, 1), slopes],
+                [triple(b16(3, heads, seq, hd))], battn_body),
           Phase(d // ft, 1.9, [cols_of(attn, ft)], [rows_of(b16(d, d), ft)], gout_body)]
     d_mid, g_ln2, d_qkv, g_out, *r2 = host('back', pe, S([(g_up, 0, n_down)], carry=r1[1:]),
-                                          shared=[vm32(seq, d), vm16(seq, d), vm16(heads, seq, hd)])
+                                          shared=[vm32(seq, d), vm16(seq, d), vm32(seq, hd), vm32(seq, hd)])
     d_qkv = d_qkv.reshape(3 * heads, seq, hd)
 
     scat = S([(g_out, 0, d // SUB), (pack, 0, nu)], carry=r2[1:], last=True)

time: 623 us -> 617 us (level)
  no operation moved by 1% of the time
where the time goes in v7:
time: 617 us
  Pallas kernels  593 us (96%)
  local copies, waits for them, and re-layouts  19.8 us (3%)
    pallas_call x6, Pallas kernels, host(): pl.pallas_call(kernel, grid=(total,), in_specs=in_specs, out_specs=out_sp...  593 us

profile of v7, /device:TPU:0, one launch (start us, length us, event | category | flops | bytes accessed | tf_op | source)
XLA Modules:
  0.0 616.8 jit_solution(10651708646949927113)
XLA Ops:
  0.6 1.2 copy.23
  1.8 1.1 reshape.66.refs_0_
  2.9 1.3 select_maximum_fusion.refs_3_
  4.1 92.7 %gather.1 = (bf16[4,2,2,2,48,4608]{5,4,3,2,1,0:T(8,128)(2,1)}, bf16[4,2,2,2,48,1536]{5,4,3,2,1,0:T(8,128)(2,1)}, bf16[4,2,2,2,48,6144]{5,4,3,2,1,0:T(8,128)(2,1)}, f32[4,2,2,2,8,128]{5,4,3,2,1,0:T(8,128)}) custom-call(bf16[48,4608]{1,0:T(8,128)(2,1)} %reshape.66.refs_0_, bf16[48,1536]{1,0:T(8,128)(2,1)} %refs_4_.1, bf16[48,6144]{1,0:T(8,128)(2,1)} %refs_6_.2, ...), custom_call_target="tpu_custom_call" | custom-call | flops 17179869184 | bytes 33554432 | tf_op jit(solution)/shard_map/gather/pallas_call | solution.py:570
  96.9 0.9 slice.16
  97.8 0.7 unstack.13.refs_1_.refs_5_
  98.5 105.0 %attention.1 = (bf16[1536,1024]{1,0:T(8,128)(2,1)}, bf16[36,1024,128]{2,1,0:T(8,128)(2,1)}, bf16[1024,1536]{1,0:T(8,128)(2,1)}, f32[12,1024,1]{2,1,0:T(8,128)}, ...) custom-call(bf16[1024,1536]{1,0:T(8,128)(2,1)} %bitcast.62, ...), custom_call_target="tpu_custom_call", output_to_operand_aliasing={{4}: (5, {}), {5}: (7, {})} | custom-call | flops 17179869184 | bytes 33554432 | tf_op jit(solution)/shard_map/attention/pallas_call | solution.py:570
  203.5 0.7 unstack.15.refs_3_.refs_4_
  204.1 84.3 %up.1 = (bf16[1024,1536]{1,0:T(8,128)(2,1)}, bf16[1536,1024]{1,0:T(8,128)(2,1)}, bf16[1024,6144]{1,0:T(8,128)(2,1)}, f32[1024,6144]{1,0:T(8,128)}, bf16[6144,153...) custom-call(bf16[1024,1536]{1,0:T(8,128)(2,1)} %bitcast.63, ...), custom_call_target="tpu_custom_call", output_to_operand_aliasing={{5}: (7, {})} | custom-call | flops 17179869184 | bytes 33554432 | tf_op jit(solution)/shard_map/up/pallas_call | solution.py:570
  288.4 100.3 %down.1 = (bf16[1024,6144]{1,0:T(8,128)(2,1)}, bf16[1536,6144]{1,0:T(8,128)(2,1)}, bf16[1024,1536]{1,0:T(8,128)(2,1)}, f32[8,48,512]{2,1,0:T(8,128)}, bf16[2,2,4...) custom-call(bf16[1024,1536]{1,0:T(8,128)(2,1)} %bitcast.44, bf16[6144,1536]{1,0:T(8,128)(2,1)} %bitcast.41, ...), custom_call_target="tpu_custom_call" | custom-call | flops 17179869184 | bytes 33554432 | tf_op jit(solution)/shard_map/down/pallas_call | solution.py:570
  388.7 104.5 %back.1 = (f32[1024,1536]{1,0:T(8,128)}, f32[1,1536]{1,0:T(1,128)}, bf16[3,12,1024,128]{3,2,1,0:T(8,128)(2,1)}, bf16[1536,1536]{1,0:T(8,128)(2,1)}, f32[12,48,51...) custom-call(bf16[1024,6144]{1,0:T(8,128)(2,1)} %get-tuple-element.57.refs_0_, ...), custom_call_target="tpu_custom_call" | custom-call | flops 17179869184 | bytes 33554432 | tf_op jit(solution)/shard_map/back/pallas_call | solution.py:570
  493.2 106.4 %last.1 = (bf16[1024,1536]{1,0:T(8,128)(2,1)}, f32[1,1536]{1,0:T(1,128)}, f32[16,48,512]{2,1,0:T(8,128)}, bf16[4,2,2,2,48,4608]{5,4,3,2,1,0:T(8,128)(2,1)}, f32[8,1536]{1,0:T(8,128)}) custom-call(bf16[1536,1024]{1,0:T(8,128)(2,1)} %get-tuple-element.56.refs_0_, bf16[36,1024,128]{2,1,0:T(8,128)(2,1)} %bitcast.60, bf16[1536,4608]{1,0:T(8,128)(2,1)} %bitcast.66, ...), custom_call_target="tpu_custom_call" | custom-call | flops 17179869184 | bytes 33554432 | tf_op jit(solution)/shard_map/last/pallas_call | solution.py:570
  599.6 1.8 pad_maximum_fusion
  601.4 0.8 copy.28
  602.3 0.0 copy-start
  602.3 1.5 copy.33
  603.7 1.1 copy.32
  604.8 0.0 copy-done
  604.8 0.1 slice_bitcast_fusion
  604.9 0.6 copy.25
  605.5 1.3 reshape_reshape.3
  606.7 2.4 copy.29
  609.2 0.7 copy.31
  609.9 0.8 constant_dynamic-slice_fusion
  610.7 0.5 slice_bitcast_fusion.2
  611.2 0.0 copy-start.1
  611.2 3.9 copy.41
  615.1 0.0 copy-done.1
  615.1 1.7 copy.42
  (3 shorter events, 0.0 us)
Async XLA Ops:
  602.3 2.6 copy-start
  611.2 3.9 copy-start.1

commit v8 on v6

--- a/solution.py
+++ b/solution.py
@@ -13,7 +13,8 @@
 SUB = 512
 WIDE = 768
 HALF = SUB // 2
-LAG = 1
+LAG = 2
+GLAG = 1
 CARRY = 2 * LAG
 LEAD = 3
 RB = 48
@@ -126,7 +127,7 @@
                 self.alias.append((len(self.ins), len(self.outs)))
                 self.ins.append((full, pl.BlockSpec(memory_space=HBM)))
             self.outs.append((sds(CHIPS + (2,) + shard.shape, BF16), pl.BlockSpec(memory_space=HBM)))
-        self.base = max(k0 - 2 * LAG, 0)
+        self.base = max(k0 - 2 * GLAG, 0)
         n = self.z1 - self.base
         self.scratch = [pltpu.SemaphoreType.DMA((n, 8)), pltpu.SemaphoreType.DMA((n, 8)), pltpu.SemaphoreType.DMA((len(weights),))]
 
@@ -177,7 +178,7 @@
     def step(self, k, fire, refs):
         me, z, y, x, c = coords()
         k0, k1, k = self.k0, self.k1, k + self.k0
-        span = [(self.z0, self.z1)] + [(max(k0 - i * LAG, 0), k1 - i * LAG) for i in range(3)]
+        span = [(self.z0, self.z1)] + [(max(k0 - i * GLAG, 0), k1 - i * GLAG) for i in range(3)]
 
         @pl.when(fire & (k == k0))
         def _():
@@ -194,56 +195,18 @@
         def _():
             self.each(*span[0], k + LEAD, lambda w, u: self.go(0, w, u, refs))
             for stage in (1, 2, 3):
-                u = k + LAG * (1 - stage)
+                u = k + GLAG * (1 - stage)
                 lo, hi = span[stage - 1]
                 self.each(lo, hi, u, lambda w, u: self.arrive(stage - 1, w, u, refs))
                 self.each(*span[stage], u, lambda w, u: self.go(stage, w, u, refs))
+            self.each(*span[3], k - 3 * GLAG, lambda w, u: self.arrive(3, w, u, refs))
 
         @pl.when(fire & (k == k1))
         def _():
             for stage in range(4):
                 lo, hi = span[stage]
-                self.each(max(lo, k1 - stage * LAG) if stage < 3 else lo, hi, None, lambda w, u: self.arrive(stage, w, u, refs))
+                self.each(max(lo, k1 - stage * GLAG), hi, None, lambda w, u: self.arrive(stage, w, u, refs))
                 self.each(lo, hi, None, lambda w, u: self.left(stage, w, u, refs))
-
-
-class GatherSmall:
-    def __init__(self, tile):
-        self.k, self.alias, self.tail = 5, [], 0
-        self.ins = [(tile, pl.BlockSpec(memory_space=pltpu.VMEM))]
-        self.outs = [(sds(CHIPS + (2,) + tile.shape, F32), pl.BlockSpec(memory_space=HBM))]
-        self.scratch = [pltpu.SemaphoreType.DMA((6,)), pltpu.SemaphoreType.DMA((6,)), pltpu.SemaphoreType.DMA]
-
-    def copies(self, stage, refs):
-        tile, full, ss, rs, _ = refs
-        me, z, y, x, c = coords()
-        zs, yp, xp, cp = peers()
-        if stage == 0:
-            return [remote(tile, full.at[z, y, x, c], ss.at[d], rs.at[d], zs[d]) for d in range(3)]
-        v, dev = ((full.at[:, y, x, c], yp), (full.at[:, :, x, c], xp), (full.at[:, :, :, c], cp))[stage - 1]
-        return [remote(v, v, ss.at[2 + stage], rs.at[2 + stage], dev)]
-
-    def step(self, k, fire, refs):
-        tile, full, ss, rs, ls = refs
-        me, z, y, x, c = coords()
-        for stage in range(5):
-            @pl.when(fire & (k == stage))
-            def _(stage=stage):
-                if stage == 0:
-                    own = pltpu.make_async_copy(tile, full.at[z, y, x, c], ls)
-                    own.start()
-                else:
-                    for cp in self.copies(stage - 1, refs):
-                        cp.wait_recv()
-                if stage < 4:
-                    for cp in self.copies(stage, refs):
-                        cp.start()
-                else:
-                    for st in range(4):
-                        for cp in self.copies(st, refs):
-                            cp.wait_send()
-                if stage == 0:
-                    own.wait()
 
 
 class Scatter:
@@ -423,15 +386,16 @@
 
 
 class SmallSum:
-    def __init__(self, row, at, t0, d):
+    def __init__(self, rows, t0, at=None):
+        d = rows.shape[1]
         self.at, self.t0, self.k, self.tail = at, t0, 1, 0
-        self.ins = [(row, pl.BlockSpec(memory_space=pltpu.VMEM))]
+        self.ins = [(rows, pl.BlockSpec(memory_space=pltpu.VMEM))]
         self.outs = [(sds((8, d), F32), pl.BlockSpec(memory_space=pltpu.VMEM))]
         self.alias = []
         self.scratch = [pltpu.VMEM((4, 8, d), F32), pltpu.VMEM((6, 8, d), F32), pltpu.SemaphoreType.DMA((6,)), pltpu.SemaphoreType.DMA((6,))]
 
-    def run(self, t, mine, refs):
-        row, out, acc, got, ss, rs = refs
+    def run(self, t, outs):
+        rows, out, acc, got, ss, rs = self.refs
         zs, yp, xp, cp = peers()
         near = (cp, xp, yp, *zs)
         n = len(near) - len(zs)
@@ -441,9 +405,9 @@
             @pl.when(t == self.t0 + i)
             def _(i=i):
                 if not i:
-                    acc[i] = jnp.zeros_like(acc[i])
-                    acc[i, pl.ds(0, 1)] = mine[...]
-                    acc[i, pl.ds(1, 1)] = row[...]
+                    acc[i] = rows[...]
+                    if self.at is not None:
+                        acc[i, pl.ds(self.at, 1)] = outs[self.at][...]
                 elif i <= n:
                     copies[i - 1].wait_recv()
                     acc[i] = acc[i - 1] + got[i - 1]
@@ -459,10 +423,10 @@
                     copy.start()
 
 
-KERNELS = ['gather', 'attention', 'up', 'down', 'back', 'last']
-
-
-def host(name, phases, comms=(), shared=()):
+KERNELS = ['forward', 'down', 'back', 'last']
+
+
+def host(name, phases, comms=(), shared=(), fires=None):
     k_all = max([c.k for c in comms], default=1)
     at = 0
     for p in phases:
@@ -471,18 +435,19 @@
         at = max(at, p.at + p.n)
     small = [c for c in comms if isinstance(c, SmallSum)]
     tail = max([c.tail for c in comms], default=0)
-    spread, clock, fires = k_all - 1 - tail, [0.0], [0]
-    for t in range(at):
-        clock.append(clock[-1] + sum(p.cost for p in phases if p.at <= t < p.at + p.n))
-    for k in range(1, k_all):
-        t = at if k >= spread else min(t for t in range(at + 1) if clock[t] * spread >= clock[at] * k)
-        fires.append(max(t, fires[-1] + 1))
+    if fires is None:
+        spread, clock, fires = k_all - 1 - tail, [0.0], [0]
+        for t in range(at):
+            clock.append(clock[-1] + sum(p.cost for p in phases if p.at <= t < p.at + p.n))
+        for k in range(1, k_all):
+            t = at if k >= spread else min(t for t in range(at + 1) if clock[t] * spread >= clock[at] * k)
+            fires.append(max(t, fires[-1] + 1))
     total = max([at, fires[-1] + 1] + [c.t0 + 5 for c in small])
     ins, in_specs, outs, out_specs, scratch, alias, resident = [], [], [], [], [], {}, []
     for p in phases:
         for arr, block, index in p.ins:
-            if block == 'smem':
-                in_specs.append(pl.BlockSpec(memory_space=pltpu.SMEM))
+            if isinstance(block, pltpu.MemorySpace):
+                in_specs.append(pl.BlockSpec(memory_space=block))
             elif index is None:
                 resident.append((len(ins), p.at))
                 in_specs.append(pl.BlockSpec(memory_space=HBM))
@@ -528,6 +493,8 @@
             c.refs = crefs
             if c not in small:
                 c.step(k, fire, crefs)
+            elif c.at is None:
+                c.run(t, rout)
             i, o, s = i + ni, o + no, s + ns
         held, rsem, extra = rscr[s:s + len(resident)], rscr[s + len(resident)], rscr[s + len(resident) + 1:]
         loads = [(pltpu.make_async_copy(rin[i], h, rsem.at[n]), at) for n, ((i, at), h) in enumerate(zip(resident, held))]
@@ -550,7 +517,8 @@
                 p.body(t - p.at, pi, po, extra)
 
         for c in small:
-            c.run(t, rout[c.at], c.refs)
+            if c.at is not None:
+                c.run(t, rout)
 
     params = dict(dimension_semantics=("arbitrary",), vmem_limit_bytes=VMEM_LIMIT)
     if comms:
@@ -621,7 +589,7 @@
     dv_s[...] = jnp.zeros_like(dv_s)
     for i in range(q_ref.shape[0] // tq):
         rows, before = pl.ds(i * tq, tq), pl.ds(0, i * tq)
-        q, da = q_ref[rows], da_ref[rows]
+        q, da = q_ref[rows], da_ref[rows].astype(BF16)
         lse = l_ref[rows]
         delta = row_sum(da.astype(F32) * a_ref[rows].astype(F32))
         near, far, keep = bias(i, tq, slope2)
@@ -657,8 +625,8 @@
     return a, (a.shape[0], n), col_map
 
 
-def heads_of(a, n, off=0):
-    return a, (n,) + a.shape[1:], lambda i: (i + off, 0, 0)
+def heads_of(a, n):
+    return a, (n,) + a.shape[1:], lambda i: (i, 0, 0)
 
 
 def whole(a):
@@ -677,7 +645,7 @@
     return jnp.concatenate([ref[j] for j in range(n)], axis=1)
 
 
-def local_step(x, ln1, wq, wo, ln2, wu, wd, dy, comm=True):
+def local_step(x, lns, wq, wo, wu, wd, dy, comm=True):
     seq, d = x.shape
     heads, hd, ft = 12, 128, 512
     ff, nq, per = wu.shape[1], 3 * d, SUB // hd
@@ -685,85 +653,125 @@
     tq = min(256, seq)
     tm = tq
     nm, nf = seq // tm, ff // ft
-    slopes = (alibi_slopes(heads), 'smem', None)
+    slopes = (alibi_slopes(heads), pltpu.SMEM, None)
     b16 = lambda *shape: sds(shape, BF16)
     f32 = lambda *shape: sds(shape, F32)
     vm16 = lambda *shape: pltpu.VMEM(shape, BF16)
     vm32 = lambda *shape: pltpu.VMEM(shape, F32)
-    act, wide, vec = b16(seq, d), b16(seq, ff), f32(1, d)
+    act, wide_act, vec = b16(seq, d), b16(seq, ff), f32(1, d)
     one_vec = (vec, vec.shape, lambda i: (0, 0))
-    band = lambda i: pl.ds(pl.multiple_of(i * tm, tm), tm)
-    flat = lambda full: full.reshape(-1, full.shape[-1])
-    order = [Unit(*w.shape, WIDE).count for w in (wq, wo, wu, wd)]
+    band = lambda i, n=tm: pl.ds(pl.multiple_of(i * n, n), n)
+    ts = tm // 2
+    ns = seq // ts
+    order = [Unit(w.shape[0] if comm else w.shape[0] // 32, w.shape[1], WIDE).count for w in (wq, wo, wu, wd)]
     qs, os, us, ds = (sum(order[:i]) for i in range(4))
-    ends = [i + 2 * LAG for i in (os, ds, sum(order))]
-
     nu = nq // SUB
     pack = sds((*CHIPS, 2, RB, nq), BF16)
 
-    def G(*window):
-        return [Gather(*window)] if comm else []
-
     def S(parts, **kw):
         return [Scatter([(a if a is pack else a.reshape(*CHIPS, 2, -1, a.shape[-1]), u0, n) for a, u0, n in parts], **kw)] if comm else []
 
+    blocks = lambda w: w.reshape(*CHIPS, 2, -1, w.shape[-1])
     if comm:
-        tile = jnp.pad(jnp.stack([ln1, ln2]), ((0, 6), (0, 128 - ln1.shape[0])))
-        fq, fo, fu, lns = host('gather', [], G([(wq, None, qs), (wo, None, os), (wu, None, us)], 0, ends[0]) + [GatherSmall(tile)])
-        fq = flat(fq)
-        w1, w2 = lns.reshape(-1, 8, 128)[:, :2, :ln1.shape[0]].transpose(1, 0, 2).reshape(2, 1, d)
-    else:
-        fq, fo, fu, w1, w2 = wq, wo, wu, ln1.reshape(1, d), ln2.reshape(1, d)
+        gather = Gather([(wq, None, qs), (wo, None, os), (wu, None, us), (wd, None, ds)], 0, sum(order) + 2 * GLAG)
+        lnsum = SmallSum(lns, 0)
+    held = {}
+
+    def load(u, ext):
+        out = []
+        for w, (first, last) in enumerate(((qs, os), (os, us), (us, ds))):
+            if first <= u[0] < last:
+                full = gather.refs[len(gather.ins) + w] if comm else held['weights'][w]
+                r, q = Unit(RB, WIDE * (last - first), WIDE).at(u[1] - first)
+                slot = rest(u[1], 2)
+                out.append(pltpu.make_async_copy(full.at[:, :, :, :, r, q], ext[3].at[slot], ext[4].at[slot]))
+        return out[0]
+
+    def weight(u, ext):
+        return ext[3][rest(u, 2)].reshape(d, WIDE)
+
+    def gain(row):
+        return (lnsum.refs[1] if comm else held['lns'])[pl.ds(row, 1)]
+
+    def start_body(i, ins, outs, ext):
+        load((qs, qs), ext).start()
+        load((qs, qs + 1), ext).start()
 
     def ln1_body(i, ins, outs, ext):
-        (xr, lw), (ht,), (_, h1) = ins, outs, ext
+        (xr, *more), (ht,), (_, h, *_) = ins, outs, ext
+        if more:
+            held.update(weights=more[1:], lns=more[0])
         xhat, _ = norm_parts(xr[...].astype(F32))
-        h = (xhat * lw[...]).astype(BF16)
-        h1[band(i)] = h
-        ht[...] = h.T
+        h1 = (xhat * gain(0)).astype(BF16)
+        h[band(i, ts)] = h1
+        ht[...] = h1.T
 
     def qkv_body(i, ins, outs, ext):
-        (w,), (o,), (qkv, h1) = ins, outs, ext
-        r = dot(h1[...], w[...]).astype(BF16)
-        for j in range(per):
-            qkv[i * per + j] = r[:, j * hd:(j + 1) * hd]
-            o[j] = r[:, j * hd:(j + 1) * hd]
+        (o,), (qkv, h, *_) = outs, ext
+        load((qs, i), ext).wait()
+        r = dot(h[...], weight(i, ext)).astype(BF16)
+        for j in range(wide):
+            head = r[:, j * hd:(j + 1) * hd]
+            qkv[i * wide + j] = head
+            o[j] = head
+        pl.when(i + 2 < os)(lambda: load((qs, i + 2), ext).start())
+        pl.when(i + 2 >= os)(lambda: load((os, i + 2), ext).start())
 
     def attn_body(i, ins, outs, ext):
-        (sl,), (o, l), (qkv, _) = ins, outs, ext
+        (sl,), (o, l), (qkv, _, a, *_) = ins, outs, ext
         attn_fwd(qkv.at[i], qkv.at[heads + i], qkv.at[2 * heads + i], o, l.at[0], sl[i], scale, tq)
-
-    pb = [Phase(nm, 1, [rows_of(x, tm), whole(w1)], [cols_of(b16(d, seq), tm)], ln1_body),
-          Phase(nq // SUB, 1.9, [cols_of(fq, SUB)], [heads_of(b16(3 * heads, seq, hd), per)], qkv_body),
-          Phase(heads, 2.2, [slopes], [cols_of(act, hd), heads_of(f32(heads, seq, 1), 1)], attn_body)]
-    h1t, qkv, attn, lse, *full = host('attention', pb, G([(wo, fo, os), (wu, fu, us), (wd, None, ds)], ends[0], ends[1]),
-                                      shared=[vm16(3 * heads, seq, hd), vm16(seq, d)])
-    if comm:
-        fo, fu, fd = full
-        fo, fu = flat(fo), flat(fu)
+        a[:, pl.ds(pl.multiple_of(i * hd, hd), hd)] = o[...]
 
     def out_body(i, ins, outs, ext):
-        (xs, a, w, lw), (o, ht), (h2,) = ins, outs, ext
-        x1 = (xs[...].astype(F32) + dot(a[...], w[...])).astype(BF16)
+        (xs,), (o, ht), (_, h, a, *_) = ins, outs, ext
+
+        @pl.when(i == 0)
+        def _():
+            for u in range(os, us):
+                load((os, u), ext).wait()
+
+        ar = a[band(i, ts)]
+        r = jnp.concatenate([dot(ar, weight(u, ext)) for u in range(os, us)], axis=1)
+        x1 = (xs[...].astype(F32) + r).astype(BF16)
         o[...] = x1
         xhat, _ = norm_parts(x1.astype(F32))
-        h = (xhat * lw[...]).astype(BF16)
-        h2[band(i)] = h
-        ht[...] = h.T
+        h2 = (xhat * gain(1)).astype(BF16)
+        h[band(i, ts)] = h2
+        ht[...] = h2.T
+
+        @pl.when(i == ns - 1)
+        def _():
+            for u in range(us, us + 2):
+                load((us, u), ext).start()
 
     def up_body(i, ins, outs, ext):
-        (w, dyr), (go, gpo, gd), (h2,) = ins, outs, ext
-        u = dot(h2[...], w[...])
+        (dyr,), (go, gpo, gd), h = ins, outs, ext[1]
+        load((us, us + i), ext).wait()
+        u = dot(h[...], weight(us + i, ext))
         cdf = 0.5 * (1.0 + lax.erf(u * math.sqrt(0.5)))
         g = (u * cdf).astype(BF16)
         go[...] = g
         gpo[...] = cdf + u * (jnp.exp(-0.5 * u * u) * math.sqrt(0.5 / math.pi))
         gd[...] = t_dot(g, dyr[...]).astype(BF16)
-
-    pc = [Phase(nm, 3, [rows_of(x, tm), rows_of(attn, tm), whole(fo), whole(w2)], [rows_of(act, tm), cols_of(b16(d, seq), tm)], out_body),
-          Phase(nf, 4.0, [cols_of(fu, ft), whole(dy)], [cols_of(wide, ft), cols_of(f32(seq, ff), ft), rows_of(b16(ff, d), ft)], up_body)]
-    x1, h2t, g, gp, g_down, *full = host('up', pc, G([(wd, fd, ds)], ends[1], ends[2]) if comm else [], shared=[vm16(seq, d)])
-    fd, = map(flat, full) if comm else (wd,)
+        pl.when(us + i + 2 < ds)(lambda: load((us, us + i + 2), ext).start())
+
+    wide = WIDE // hd
+    more = [] if comm else [(lns, pltpu.VMEM, None)] + [(blocks(w), HBM, None) for w in (wq, wo, wu)]
+    pa = [Phase(ns, 1, [rows_of(x, ts), *more], [cols_of(b16(d, seq), ts)], ln1_body, 5),
+          Phase(1, 0, [], [], start_body, 4),
+          Phase(nq // WIDE, 3, [], [heads_of(b16(3 * heads, seq, hd), wide)], qkv_body, 5 + ns),
+          Phase(heads, 2.7, [slopes], [cols_of(act, hd), heads_of(f32(heads, seq, 1), 1)], attn_body, 5 + ns + nq // WIDE),
+          Phase(ns, 2, [rows_of(x, ts)], [rows_of(act, ts), cols_of(b16(d, seq), ts)], out_body, 5 + ns + nq // WIDE + heads),
+          Phase(ff // WIDE, 6, [whole(dy)], [cols_of(wide_act, WIDE), cols_of(f32(seq, ff), WIDE), rows_of(b16(ff, d), WIDE)], up_body, 5 + 2 * ns + nq // WIDE + heads)]
+    shared = [vm16(3 * heads, seq, hd), vm16(seq, d), vm16(seq, d), vm16(2, *CHIPS, 2, RB, WIDE), pltpu.SemaphoreType.DMA((2,))]
+    t_qkv, t_attn, t_out, t_up = (p.at for p in pa[2:])
+    fires = [*range(6), t_qkv - 4, t_qkv, t_qkv + 2, t_qkv + 4, t_attn - 1, *range(t_attn, t_up, 4), *range(t_up, t_up + ff // WIDE + 3)]
+    got = host('forward', pa, [gather, lnsum] if comm else [], shared=shared, fires=fires if comm else None)
+    h1t, qkv, attn, lse, x1, h2t, g, gp, g_down, *full = got
+    fq, fo, fu, fd = wq, wo, wu, wd
+    if comm:
+        fq, fo, fu, fd = (f.reshape(-1, f.shape[-1]) for f in full[:4])
+        lns = full[4]
 
     def dup_body(i, ins, outs, ext):
         (dyr, w, gr, gpr, ht), (duo, gu), (acc,) = ins, outs, ext
@@ -776,7 +784,7 @@
         (xr,), (o,), (acc,) = ins, outs, ext
         o[...] = (xr[...].astype(F32) + acc[band(i)]).astype(BF16)
 
-    pd = [Phase(nf, 6, [whole(dy), rows_of(fd, ft), cols_of(g, ft), cols_of(gp, ft), whole(h2t)], [cols_of(wide, ft), cols_of(b16(d, ff), ft)], dup_body),
+    pd = [Phase(nf, 6, [whole(dy), rows_of(fd, ft), cols_of(g, ft), cols_of(gp, ft), whole(h2t)], [cols_of(wide_act, ft), cols_of(b16(d, ff), ft)], dup_body),
           Phase(nm, 1, [rows_of(x1, tm)], [rows_of(act, tm)], y_body)]
     n_down = Unit(ff // 32, d).count
     d_up, g_up, y, *r1 = host('down', pd, S([(g_down, 0, n_down)]), shared=[vm32(seq, d)])
@@ -787,35 +795,34 @@
 
     def ln2b_body(i, ins, outs, ext):
         (xr, dyr, lw), (dmo, gwo), (acc, dmb, *_) = ins, outs, ext
-        dx, gw = norm_back(acc[band(i)], xr[...].astype(F32), lw[...])
+        dx, gw = norm_back(acc[band(i)], xr[...].astype(F32), lw[pl.ds(1, 1)])
         dm = dyr[...].astype(F32) + dx
         dmo[...] = dm
         dmb[band(i)] = dm.astype(BF16)
         put(gwo, i, lambda: gw)
 
     def dattn_body(i, ins, outs, ext):
-        (w,), (_, dmb, da, *_) = ins, ext
-        r = dot_t(dmb[...], w[...]).astype(BF16)
-        for j in range(ft // hd):
-            da[i * (ft // hd) + j] = r[:, j * hd:(j + 1) * hd]
+        (w,), (acc, dmb, *_) = ins, ext
+        acc[:, pl.ds(pl.multiple_of(i * ft, ft), ft)] = dot_t(dmb[...], w[...])
 
     def battn_body(i, ins, outs, ext):
-        (q, k, v, a, l, sl), (o,), (acc, _, da) = ins, outs, ext
-        dk, dv = (acc.at[:, pl.ds(j * hd, hd)] for j in range(2))
-        attn_bwd(q.at[0], k.at[0], v.at[0], a, da.at[i], l.at[0], *(o.at[j, 0] for j in range(3)), dk, dv, sl[i], scale, tq)
+        (qkv, a, l, sl), (o,), (acc, _, dk, dv) = ins, outs, ext
+        da = acc.at[:, pl.ds(pl.multiple_of(i * hd, hd), hd)]
+        attn_bwd(*(qkv.at[j, 0] for j in range(3)), a, da, l.at[0], *(o.at[j, 0] for j in range(3)), dk, dv, sl[i], scale, tq)
 
     def gout_body(i, ins, outs, ext):
         (a,), (o,), (_, dmb, *_) = ins, outs, ext
         o[...] = t_dot(a[...], dmb[...]).astype(BF16)
 
+    triple = lambda a: (a, (3, 1, seq, hd), lambda i: (0, i, 0, 0))
     pe = [Phase(nf, 2.4, [cols_of(d_up, ft), cols_of(fu, ft)], [], dh2_body),
-          Phase(nm, 2, [rows_of(x1, tm), rows_of(dy, tm), whole(w2)], [rows_of(f32(seq, d), tm), one_vec], ln2b_body),
+          Phase(nm, 2, [rows_of(x1, tm), rows_of(dy, tm), whole(lns)], [rows_of(f32(seq, d), tm), one_vec], ln2b_body),
           Phase(d // ft, 1.9, [rows_of(fo, ft)], [], dattn_body),
-          Phase(heads, 3.5, [*(heads_of(qkv, 1, j * heads) for j in range(3)), cols_of(attn, hd), heads_of(lse, 1), slopes],
-                [(b16(3, heads, seq, hd), (3, 1, seq, hd), lambda i: (0, i, 0, 0))], battn_body),
+          Phase(heads, 3.5, [triple(qkv.reshape(3, heads, seq, hd)), cols_of(attn, hd), heads_of(lse, 1), slopes],
+                [triple(b16(3, heads, seq, hd))], battn_body),
           Phase(d // ft, 1.9, [cols_of(attn, ft)], [rows_of(b16(d, d), ft)], gout_body)]
     d_mid, g_ln2, d_qkv, g_out, *r2 = host('back', pe, S([(g_up, 0, n_down)], carry=r1[1:]),
-                                          shared=[vm32(seq, d), vm16(seq, d), vm16(heads, seq, hd)])
+                                          shared=[vm32(seq, d), vm16(seq, d), vm32(seq, hd), vm32(seq, hd)])
     d_qkv = d_qkv.reshape(3 * heads, seq, hd)
 
     scat = S([(g_out, 0, d // SUB), (pack, 0, nu)], carry=r2[1:], last=True)
@@ -841,28 +848,37 @@
 
     def ln1b_body(i, ins, outs, ext):
         (xr, dm, lw), (o, gwo) = ins, outs
-        dx, gw = norm_back(ext[0][band(i)], xr[...].astype(F32), lw[...])
+        dx, gw = norm_back(ext[0][band(i)], xr[...].astype(F32), lw[pl.ds(0, 1)])
         o[...] = (dm[...] + dx).astype(BF16)
         put(gwo, i, lambda: gw)
 
     first = [] if comm else [cols_of(b16(d, nq), SUB)]
     pf = [Phase(nu, 3.9, [whole(h1t), heads_of(d_qkv, per), cols_of(fq, SUB)], first, macro_body),
-          Phase(nm, 2, [rows_of(x, tm), rows_of(d_mid, tm), whole(w1)], [rows_of(act, tm), one_vec], ln1b_body)]
+          Phase(nm, 2, [rows_of(x, tm), rows_of(d_mid, tm), whole(lns)], [rows_of(act, tm), one_vec], ln1b_body)]
     if comm:
         pf.append(Phase(nu, 0, [], [], ship_body, 1))
-        scat.append(SmallSum(g_ln2, 1, nu + nm, d))
+        scat.append(SmallSum(jnp.pad(g_ln2, ((0, 7), (0, 0))), nu + nm, 1))
     shared = [vm32(seq, d), vm16(2, *CHIPS, 2, RB, SUB), pltpu.SemaphoreType.DMA((2,))]
     got = host('last', pf, scat, shared=shared)
     if not comm:
         g_qkv, dx, g_ln1 = got
         return y, dx, g_ln1, g_qkv, g_out, g_ln2, g_up, g_down
     dx, _, r3, _, sums = got
-    units = jnp.concatenate([r1[0], r2[0], r3])
-    nc = d // SUB
-    g_down, g_up, g_out, g_qkv = jnp.split(units, (n_down, 2 * n_down, 2 * n_down + nc))
-    flat_rows = lambda u: u.transpose(1, 0, 2).reshape(RB, -1)
-    g_down = g_down.reshape(-1, nc, RB, SUB).transpose(0, 2, 1, 3).reshape(-1, d)
-    return y, dx, sums, flat_rows(g_qkv), flat_rows(g_out), None, flat_rows(g_up), g_down
+    parts, done = [r1[0], r2[0], r3], 0
+    grads = []
+    for count in (n_down, n_down, d // SUB, nu):
+        pieces, at = [], 0
+        for p in parts:
+            a, b = max(done - at, 0), min(done + count - at, p.shape[0])
+            if a < b:
+                pieces.append(p[a:b])
+            at += p.shape[0]
+        done += count
+        grads.append(jnp.concatenate(pieces))
+    g_down, *others = grads
+    g_down = g_down.reshape(-1, d // SUB, RB, SUB).transpose(0, 2, 1, 3).reshape(-1, d)
+    g_up, g_out, g_qkv = (u.transpose(1, 0, 2).reshape(RB, -1) for u in others)
+    return y, dx, sums, g_qkv, g_out, None, g_up, g_down
 
 
 def solution(mesh):
@@ -871,9 +887,10 @@
     def step(x_in, ln1_w, w_qkv, w_out, ln2_w, w_up, w_down, dy_out):
         rows, _, heads, hd = w_qkv.shape
         d = x_in.shape[-1]
+        lns = lax.dynamic_update_slice(jnp.zeros((8, d), F32), jnp.stack([ln1_w, ln2_w]), (0, lax.axis_index('fsdp') * rows))
         y, dx, sums, g_qkv, g_out, _, g_up, g_down = local_step(
-            x_in[0], ln1_w, w_qkv.reshape(rows, -1), w_out, ln2_w, w_up, w_down, dy_out[0])
+            x_in[0], lns, w_qkv.reshape(rows, -1), w_out, w_up, w_down, dy_out[0])
         mine = lax.dynamic_slice_in_dim(sums, lax.axis_index('fsdp') * rows, rows, axis=1)
-        return (y[None], dx[None], mine[0], g_qkv.reshape(rows, 3, heads, hd), g_out, mine[1], g_up, g_down)
+        return (y[None], dx[None], mine[1], g_qkv.reshape(rows, 3, heads, hd), g_out, mine[0], g_up, g_down)
 
     return jax.shard_map(step, mesh=mesh, in_specs=(row_spec,) * 8, out_specs=(row_spec,) * 8, check_vma=False)

time: 623 us -> 599 us (0.961)
  Pallas kernels: 599 us -> 575 us
    pallas_call x6 -> x4, Pallas kernels: 599 us -> 575 us  [host(): pl.pallas_call(kernel, grid=(total,), in_specs=in_specs, out_specs=out_sp...]
where the time goes in v8:
time: 599 us; the launch traced here: 598 us
  Pallas kernels  575 us (96%)
  local copies, waits for them, and re-layouts  22 us (4%)
    pallas_call x4, Pallas kernels, host(): pl.pallas_call(kernel, grid=(total,), in_specs=in_specs, out_specs=out_sp...  575 us

profile of v8, /device:TPU:0, one launch (start us, length us, event | category | flops | bytes accessed | tf_op | source)
XLA Modules:
  0.0 598.2 jit_solution(8542136676894073145)
XLA Ops:
  0.6 0.7 pad_maximum_fusion.1
  1.3 0.6 broadcast_in_dim.9
  1.9 1.4 dynamic_update_slice.3.refs_8_
  3.3 1.2 copy.19
  4.5 1.1 reshape.58.refs_4_
  5.5 263.7 %forward.1 = (bf16[1536,1024]{1,0:T(8,128)(2,1)}, bf16[36,1024,128]{2,1,0:T(8,128)(2,1)}, bf16[1024,1536]{1,0:T(8,128)(2,1)}, f32[12,1024,1]{2,1,0:T(8,128)}, bf...) custom-call(bf16[1024,1536]{1,0:T(8,128)(2,1)} %bitcast.54, ...), custom_call_target="tpu_custom_call" | custom-call | flops 17179869184 | bytes 33554432 | tf_op jit(solution)/shard_map/forward/pallas_call | solution.py:526
  269.2 100.7 %down.1 = (bf16[1024,6144]{1,0:T(8,128)(2,1)}, bf16[1536,6144]{1,0:T(8,128)(2,1)}, bf16[1024,1536]{1,0:T(8,128)(2,1)}, f32[8,48,512]{2,1,0:T(8,128)}, bf16[2,2,4...) custom-call(bf16[1024,1536]{1,0:T(8,128)(2,1)} %bitcast.39, bf16[6144,1536]{1,0:T(8,128)(2,1)} %bitcast.37, ...), custom_call_target="tpu_custom_call" | custom-call | flops 17179869184 | bytes 33554432 | tf_op jit(solution)/shard_map/down/pallas_call | solution.py:526
  369.9 104.2 %back.1 = (f32[1024,1536]{1,0:T(8,128)}, f32[1,1536]{1,0:T(1,128)}, bf16[3,12,1024,128]{3,2,1,0:T(8,128)(2,1)}, bf16[1536,1536]{1,0:T(8,128)(2,1)}, f32[12,48,51...) custom-call(bf16[1024,6144]{1,0:T(8,128)(2,1)} %get-tuple-element.46.refs_0_, ...), custom_call_target="tpu_custom_call" | custom-call | flops 17179869184 | bytes 33554432 | tf_op jit(solution)/shard_map/back/pallas_call | solution.py:526
  474.1 1.3 pad.4.refs_9_
  475.5 106.0 %last.1 = (bf16[1024,1536]{1,0:T(8,128)(2,1)}, f32[1,1536]{1,0:T(1,128)}, f32[16,48,512]{2,1,0:T(8,128)}, bf16[4,2,2,2,48,4608]{5,4,3,2,1,0:T(8,128)(2,1)}, f32[8,1536]{1,0:T(8,128)}) custom-call(bf16[1536,1024]{1,0:T(8,128)(2,1)} %get-tuple-element.45.refs_0_, bf16[36,1024,128]{2,1,0:T(8,128)(2,1)} %bitcast.52, bf16[1536,4608]{1,0:T(8,128)(2,1)} %bitcast.57, ...), custom_call_target="tpu_custom_call" | custom-call | flops 17179869184 | bytes 33554432 | tf_op jit(solution)/shard_map/last/pallas_call | solution.py:526
  581.5 0.0 copy-start.1
  581.5 0.9 constant_dynamic-slice_fusion
  582.3 0.5 slice_bitcast_fusion.2
  582.9 1.0 slice_bitcast_fusion.1
  583.8 0.7 copy.25
  584.6 1.0 slice.26
  585.6 1.2 slice_bitcast_fusion
  586.9 0.0 copy-done.1
  586.9 0.0 copy-start.2
  586.9 0.1 slice.25
  587.0 0.1 maximum_bitcast_fusion
  587.1 1.1 copy.26
  588.2 0.0 copy-done.2
  588.3 0.1 pad_maximum_fusion
  588.4 0.8 copy.23
  589.2 1.5 copy.27
  590.6 0.6 copy.20
  591.2 0.2 reshape_reshape.3
  591.5 1.2 copy.24
  592.6 3.9 copy.31
  596.6 0.0 copy-done
  596.6 1.7 copy.32
  (2 shorter events, 0.0 us)
Async XLA Ops:
  581.5 5.4 copy-start.1
  586.9 1.3 copy-start.2
  592.6 3.9 copy-start

commit v9 on v8

--- a/solution.py
+++ b/solution.py
@@ -17,6 +17,7 @@
 GLAG = 1
 CARRY = 2 * LAG
 LEAD = 3
+SIDE = -4
 RB = 48
 F32, BF16 = jnp.float32, jnp.bfloat16
 VMEM_LIMIT = 67_000_000
@@ -120,16 +121,20 @@
         self.z1 = k1 + LEAD
         self.w, self.ins, self.outs, self.alias = [], [], [], []
         for shard, full, first in weights:
-            unit = Unit(*shard.shape, WIDE)
-            self.w.append((len(self.ins), unit, first, first + unit.count, full is None))
+            heads, rows = shard.shape[:2] if shard.ndim == 3 else (0, shard.shape[0])
+            shape = (rows, shard.size // rows)
+            unit = Unit(*shape, WIDE)
+            self.w.append((SIDE if heads else len(self.ins), unit, first, first + unit.count, full is None))
             self.ins.append((shard, pl.BlockSpec(memory_space=pltpu.VMEM)))
+            if heads:
+                self.heads, side = (len(self.ins) - 1, heads), pltpu.VMEM(shape, BF16)
             if full is not None:
                 self.alias.append((len(self.ins), len(self.outs)))
                 self.ins.append((full, pl.BlockSpec(memory_space=HBM)))
-            self.outs.append((sds(CHIPS + (2,) + shard.shape, BF16), pl.BlockSpec(memory_space=HBM)))
+            self.outs.append((sds(CHIPS + (2,) + shape, BF16), pl.BlockSpec(memory_space=HBM)))
         self.base = max(k0 - 2 * GLAG, 0)
         n = self.z1 - self.base
-        self.scratch = [pltpu.SemaphoreType.DMA((n, 8)), pltpu.SemaphoreType.DMA((n, 8)), pltpu.SemaphoreType.DMA((len(weights),))]
+        self.scratch = [side, pltpu.SemaphoreType.DMA((n, 8)), pltpu.SemaphoreType.DMA((n, 8)), pltpu.SemaphoreType.DMA((len(weights),))]
 
     def copies(self, stage, w, u, refs):
         i, unit, first, _, _ = self.w[w]
@@ -175,13 +180,16 @@
         for cp in self.copies(stage, w, u, refs):
             cp.wait_send()
 
-    def step(self, k, fire, refs):
+    def step(self, k, fire, begin, refs):
         me, z, y, x, c = coords()
         k0, k1, k = self.k0, self.k1, k + self.k0
         span = [(self.z0, self.z1)] + [(max(k0 - i * GLAG, 0), k1 - i * GLAG) for i in range(3)]
 
         @pl.when(fire & (k == k0))
         def _():
+            i, heads = self.heads
+            for h in range(heads):
+                refs[SIDE][:, h * 128:(h + 1) * 128] = refs[i][h]
             own = [pltpu.make_async_copy(refs[i], refs[len(self.ins) + w].at[z, y, x, c], refs[-1].at[w])
                    for w, (i, _, _, _, fresh) in enumerate(self.w) if fresh]
             for cp in own:
@@ -210,18 +218,18 @@
 
 
 class Scatter:
-    def __init__(self, grads, carry=None, last=False):
+    def __init__(self, grads, layout, carry=None, last=False):
         self.last, self.carried = last, carry is not None
         self.parts, self.ins, n = [], [], 0
-        self.late = None
+        self.late = []
         for g, u0, m in grads:
             self.parts.append((n, n + m, u0, Unit(*g.shape[-2:])))
             if isinstance(g, jax.ShapeDtypeStruct):
-                self.late = g
+                self.late.append(g)
             else:
                 self.ins.append((g, pl.BlockSpec(memory_space=HBM)))
             n += m
-        self.known = n - m if self.late else n
+        self.known = sum(m for g, _, m in grads if not isinstance(g, jax.ShapeDtypeStruct))
         self.n = n
         self.first = 0 if self.carried else CARRY
         self.end = n + CARRY
@@ -238,28 +246,28 @@
             pltpu.VMEM((self.end, *self.three_shape), BF16),
             pltpu.VMEM((self.end, 3, RB, SUB), BF16),
             pltpu.SemaphoreType.DMA((self.end, 8)), pltpu.SemaphoreType.DMA((self.end, 8)), pltpu.SemaphoreType.DMA((2,))]
-        outs = [sds((self.done - self.first, RB, SUB), F32)]
+        self.layout = layout
+        outs = [sds((RB, n * SUB) if n > 0 else (-n * SUB // 128, RB, 128), F32) for n in layout]
         if not last:
             outs += [sds((LAG, *shape), BF16) for shape in (self.two_shape, self.three_shape)]
         self.outs = [(o, pl.BlockSpec(memory_space=pltpu.VMEM)) for o in outs]
-        if self.late:
-            self.outs.append((self.late, pl.BlockSpec(memory_space=HBM)))
+        self.outs += [(g, pl.BlockSpec(memory_space=HBM)) for g in self.late]
         self.alias = []
 
     def source(self, j, refs, fn):
         for i, (a, b, u0, unit) in enumerate(self.parts):
-            ref = self.written() if self.late and a == self.known else refs[i]
+            ref = self.written(i - len(self.parts)) if self.late and a >= self.known else refs[i]
             u = j - CARRY
             if len(self.parts) == 1:
                 fn(ref, *unit.at(u0 + u))
             else:
                 pl.when((u >= a) & (u < b))(functools.partial(lambda ref, unit, u: fn(ref, *unit.at(u)), ref, unit, u0 + u - a))
 
-    def written(self):
-        return self.refs[len(self.ins) + len(self.outs) - 1]
+    def written(self, i):
+        return self.refs[len(self.ins) + len(self.outs) + i]
 
     def ship(self, u):
-        self.swap(CARRY + self.known + u, self.refs, lambda cp: cp.start())
+        self.swap(CARRY + u, self.refs, lambda cp: cp.start())
 
     def bufs(self, refs):
         return refs[len(self.ins) + len(self.outs):]
@@ -314,9 +322,21 @@
             total = three[j, z].astype(F32)
             for d in range(3):
                 total += four[j, d].astype(F32)
-            refs[len(self.ins)][j - self.first] = total
-
-    def step(self, k, fire, refs):
+            a = self.first
+            for i, n in enumerate(self.layout):
+                b, out = a + abs(n), refs[len(self.ins) + i]
+
+                @pl.when((j >= a) & (j < b))
+                def _(out=out, a=a, n=n):
+                    if n > 0:
+                        out[:, pl.ds(pl.multiple_of((j - a) * SUB, SUB), SUB)] = total
+                    else:
+                        for h in range(SUB // 128):
+                            out[(j - a) * (SUB // 128) + h] = total[:, h * 128:(h + 1) * 128]
+
+                a = b
+
+    def step(self, k, fire, begin, refs):
         n, end, last = self.n, self.end, self.last
         got, own, two, three, four, ss, rs, ls = self.bufs(refs)
         start = lambda cp: cp.start()
@@ -330,13 +350,11 @@
                 cp.wait_recv()
             self.add(stage, j, refs)
 
-        @pl.when(fire & (k == 0))
+        @pl.when(begin)
         def _():
-            @pl.loop(CARRY, CARRY + self.known)
-            def _(j):
-                self.swap(j, refs, start)
-
-            self.local(CARRY, refs, start)
+            if self.known:
+                pl.loop(CARRY, CARRY + self.known)(lambda j: self.swap(j, refs, start))
+                self.local(CARRY, refs, start)
             if self.carried:
                 for i in range(LAG):
                     two[LAG + i] = refs[len(self.ins) - 2][i]
@@ -347,6 +365,8 @@
         @pl.when(fire & (k < n))
         def _():
             j = k + CARRY
+            if not self.known:
+                pl.when(j == CARRY)(lambda: self.local(j, refs, start))
             pl.when(j + 1 < end)(lambda: self.local(j + 1, refs, start))
             self.swap(j, refs, lambda cp: cp.wait_recv())
             self.local(j, refs, lambda cp: cp.wait())
@@ -381,8 +401,8 @@
 
             if not last:
                 for i in range(LAG):
-                    refs[len(self.ins) + 1][i] = two[n + LAG + i]
-                    refs[len(self.ins) + 2][i] = three[n + i]
+                    refs[len(self.ins) + len(self.layout)][i] = two[n + LAG + i]
+                    refs[len(self.ins) + len(self.layout) + 1][i] = three[n + i]
 
 
 class SmallSum:
@@ -390,12 +410,13 @@
         d = rows.shape[1]
         self.at, self.t0, self.k, self.tail = at, t0, 1, 0
         self.ins = [(rows, pl.BlockSpec(memory_space=pltpu.VMEM))]
-        self.outs = [(sds((8, d), F32), pl.BlockSpec(memory_space=pltpu.VMEM))]
+        self.outs = [(sds((8, d if at is None else 128), F32), pl.BlockSpec(memory_space=pltpu.VMEM))]
         self.alias = []
         self.scratch = [pltpu.VMEM((4, 8, d), F32), pltpu.VMEM((6, 8, d), F32), pltpu.SemaphoreType.DMA((6,)), pltpu.SemaphoreType.DMA((6,))]
 
     def run(self, t, outs):
         rows, out, acc, got, ss, rs = self.refs
+        me = coords()[0]
         zs, yp, xp, cp = peers()
         near = (cp, xp, yp, *zs)
         n = len(near) - len(zs)
@@ -405,9 +426,12 @@
             @pl.when(t == self.t0 + i)
             def _(i=i):
                 if not i:
-                    acc[i] = rows[...]
-                    if self.at is not None:
-                        acc[i, pl.ds(self.at, 1)] = outs[self.at][...]
+                    if self.at is None:
+                        acc[i] = pltpu.roll(rows[:], RB * me, 1)
+                    else:
+                        acc[i] = jnp.zeros_like(acc[i])
+                        acc[i, pl.ds(0, 1)] = rows[:]
+                        acc[i, pl.ds(self.at, 1)] = outs[self.at][:]
                 elif i <= n:
                     copies[i - 1].wait_recv()
                     acc[i] = acc[i - 1] + got[i - 1]
@@ -416,7 +440,7 @@
                     for j in range(n, len(near)):
                         copies[j].wait_recv()
                         total += got[j]
-                    out[...] = total
+                    out[:] = total if self.at is None else pltpu.roll(total, total.shape[1] - RB * me, 1)[:, :128]
                     for copy in copies:
                         copy.wait_send()
                 for copy in copies[i:i + 1] if i < n else copies[n:] if i == n else ():
@@ -492,7 +516,7 @@
             crefs = rin[i:i + ni] + rout[o:o + no] + rscr[s:s + ns]
             c.refs = crefs
             if c not in small:
-                c.step(k, fire, crefs)
+                c.step(k, fire, t == 0, crefs)
             elif c.at is None:
                 c.run(t, rout)
             i, o, s = i + ni, o + no, s + ns
@@ -585,8 +609,8 @@
 
 def attn_bwd(q_ref, k_ref, v_ref, a_ref, da_ref, l_ref, dq_ref, dk_ref, dv_ref, dk_s, dv_s, slope, scale, tq):
     slope2, scale2 = slope * LOG2E, scale * LOG2E
-    dk_s[...] = jnp.zeros_like(dk_s)
-    dv_s[...] = jnp.zeros_like(dv_s)
+    dk_s[:] = jnp.zeros_like(dk_s)
+    dv_s[:] = jnp.zeros_like(dv_s)
     for i in range(q_ref.shape[0] // tq):
         rows, before = pl.ds(i * tq, tq), pl.ds(0, i * tq)
         q, da = q_ref[rows], da_ref[rows].astype(BF16)
@@ -605,8 +629,8 @@
             part = dot(ds, kk)
             dq = part if dq is None else dq + part
         dq_ref[rows] = (dq * scale).astype(BF16)
-    dk_ref[...] = (dk_s[...] * scale).astype(BF16)
-    dv_ref[...] = dv_s[...].astype(BF16)
+    dk_ref[:] = (dk_s[:] * scale).astype(BF16)
+    dv_ref[:] = dv_s[:].astype(BF16)
 
 
 def row_map(i):
@@ -636,9 +660,9 @@
 def put(ref, i, part):
     @pl.when(i == 0)
     def _():
-        ref[...] = jnp.zeros_like(ref)
-
-    ref[...] += part()
+        ref[:] = jnp.zeros_like(ref)
+
+    ref[:] += part()
 
 
 def side_by_side(ref, n):
@@ -648,7 +672,7 @@
 def local_step(x, lns, wq, wo, wu, wd, dy, comm=True):
     seq, d = x.shape
     heads, hd, ft = 12, 128, 512
-    ff, nq, per = wu.shape[1], 3 * d, SUB // hd
+    ff, nq, per, slab = wu.shape[1], 3 * d, SUB // hd, d // 4
     scale = 1 / math.sqrt(hd)
     tq = min(256, seq)
     tm = tq
@@ -663,13 +687,13 @@
     band = lambda i, n=tm: pl.ds(pl.multiple_of(i * n, n), n)
     ts = tm // 2
     ns = seq // ts
-    order = [Unit(w.shape[0] if comm else w.shape[0] // 32, w.shape[1], WIDE).count for w in (wq, wo, wu, wd)]
+    order = [n // (WIDE * d) for n in (d * nq, d * d, d * ff, d * ff)]
     qs, os, us, ds = (sum(order[:i]) for i in range(4))
     nu = nq // SUB
-    pack = sds((*CHIPS, 2, RB, nq), BF16)
-
-    def S(parts, **kw):
-        return [Scatter([(a if a is pack else a.reshape(*CHIPS, 2, -1, a.shape[-1]), u0, n) for a, u0, n in parts], **kw)] if comm else []
+    packs = [sds((*CHIPS, 2, RB, n), BF16) for n in (d, nq)]
+
+    def S(parts, *args, **kw):
+        return [Scatter([(a.reshape(*CHIPS, 2, -1, a.shape[-1]) if isinstance(a, jax.Array) else a, 0, n) for a, n in parts], *args, **kw)] if comm else []
 
     blocks = lambda w: w.reshape(*CHIPS, 2, -1, w.shape[-1])
     if comm:
@@ -701,15 +725,15 @@
         (xr, *more), (ht,), (_, h, *_) = ins, outs, ext
         if more:
             held.update(weights=more[1:], lns=more[0])
-        xhat, _ = norm_parts(xr[...].astype(F32))
+        xhat, _ = norm_parts(xr[:].astype(F32))
         h1 = (xhat * gain(0)).astype(BF16)
         h[band(i, ts)] = h1
-        ht[...] = h1.T
+        ht[:] = h1.T
 
     def qkv_body(i, ins, outs, ext):
         (o,), (qkv, h, *_) = outs, ext
         load((qs, i), ext).wait()
-        r = dot(h[...], weight(i, ext)).astype(BF16)
+        r = dot(h[:], weight(i, ext)).astype(BF16)
         for j in range(wide):
             head = r[:, j * hd:(j + 1) * hd]
             qkv[i * wide + j] = head
@@ -720,7 +744,7 @@
     def attn_body(i, ins, outs, ext):
         (sl,), (o, l), (qkv, _, a, *_) = ins, outs, ext
         attn_fwd(qkv.at[i], qkv.at[heads + i], qkv.at[2 * heads + i], o, l.at[0], sl[i], scale, tq)
-        a[:, pl.ds(pl.multiple_of(i * hd, hd), hd)] = o[...]
+        a[:, pl.ds(pl.multiple_of(i * hd, hd), hd)] = o[:]
 
     def out_body(i, ins, outs, ext):
         (xs,), (o, ht), (_, h, a, *_) = ins, outs, ext
@@ -732,12 +756,12 @@
 
         ar = a[band(i, ts)]
         r = jnp.concatenate([dot(ar, weight(u, ext)) for u in range(os, us)], axis=1)
-        x1 = (xs[...].astype(F32) + r).astype(BF16)
-        o[...] = x1
+        x1 = (xs[:].astype(F32) + r).astype(BF16)
+        o[:] = x1
         xhat, _ = norm_parts(x1.astype(F32))
         h2 = (xhat * gain(1)).astype(BF16)
         h[band(i, ts)] = h2
-        ht[...] = h2.T
+        ht[:] = h2.T
 
         @pl.when(i == ns - 1)
         def _():
@@ -747,12 +771,12 @@
     def up_body(i, ins, outs, ext):
         (dyr,), (go, gpo, gd), h = ins, outs, ext[1]
         load((us, us + i), ext).wait()
-        u = dot(h[...], weight(us + i, ext))
+        u = dot(h[:], weight(us + i, ext))
         cdf = 0.5 * (1.0 + lax.erf(u * math.sqrt(0.5)))
         g = (u * cdf).astype(BF16)
-        go[...] = g
-        gpo[...] = cdf + u * (jnp.exp(-0.5 * u * u) * math.sqrt(0.5 / math.pi))
-        gd[...] = t_dot(g, dyr[...]).astype(BF16)
+        go[:] = g
+        gpo[:] = cdf + u * (jnp.exp(-0.5 * u * u) * math.sqrt(0.5 / math.pi))
+        gd[:] = t_dot(g, dyr[:]).astype(BF16)
         pl.when(us + i + 2 < ds)(lambda: load((us, us + i + 2), ext).start())
 
     wide = WIDE // hd
@@ -775,110 +799,114 @@
 
     def dup_body(i, ins, outs, ext):
         (dyr, w, gr, gpr, ht), (duo, gu), (acc,) = ins, outs, ext
-        du = (dot_t(dyr[...], w[...]) * gpr[...]).astype(BF16)
-        duo[...] = du
-        gu[...] = dot(ht[...], du).astype(BF16)
-        put(acc, i, lambda: dot(gr[...], w[...]))
+        du = (dot_t(dyr[:], w[:]) * gpr[:]).astype(BF16)
+        duo[:] = du
+        gu[:] = dot(ht[:], du).astype(BF16)
+        put(acc, i, lambda: dot(gr[:], w[:]))
 
     def y_body(i, ins, outs, ext):
         (xr,), (o,), (acc,) = ins, outs, ext
-        o[...] = (xr[...].astype(F32) + acc[band(i)]).astype(BF16)
+        o[:] = (xr[:].astype(F32) + acc[band(i)]).astype(BF16)
 
     pd = [Phase(nf, 6, [whole(dy), rows_of(fd, ft), cols_of(g, ft), cols_of(gp, ft), whole(h2t)], [cols_of(wide_act, ft), cols_of(b16(d, ff), ft)], dup_body),
           Phase(nm, 1, [rows_of(x1, tm)], [rows_of(act, tm)], y_body)]
     n_down = Unit(ff // 32, d).count
-    d_up, g_up, y, *r1 = host('down', pd, S([(g_down, 0, n_down)]), shared=[vm32(seq, d)])
+    d_up, g_up, y, *r1 = host('down', pd, S([(g_down, n_down)], [n_down - CARRY]), shared=[vm32(seq, d)])
 
     def dh2_body(i, ins, outs, ext):
         (du, w), acc = ins, ext[0]
-        put(acc, i, lambda: dot_t(du[...], w[...]))
+        put(acc, i, lambda: dot_t(du[:], w[:]))
 
     def ln2b_body(i, ins, outs, ext):
-        (xr, dyr, lw), (dmo, gwo), (acc, dmb, *_) = ins, outs, ext
-        dx, gw = norm_back(acc[band(i)], xr[...].astype(F32), lw[pl.ds(1, 1)])
-        dm = dyr[...].astype(F32) + dx
-        dmo[...] = dm
-        dmb[band(i)] = dm.astype(BF16)
+        (xr, dyr, lw), (dmo, dmbo, gwo), (acc, dmb, *_) = ins, outs, ext
+        dx, gw = norm_back(acc[band(i)], xr[:].astype(F32), lw[pl.ds(1, 1)])
+        dm = dyr[:].astype(F32) + dx
+        dmo[:] = dm
+        dmb[band(i)] = dmbo[:] = dm.astype(BF16)
         put(gwo, i, lambda: gw)
 
     def dattn_body(i, ins, outs, ext):
         (w,), (acc, dmb, *_) = ins, ext
-        acc[:, pl.ds(pl.multiple_of(i * ft, ft), ft)] = dot_t(dmb[...], w[...])
+        acc[:, pl.ds(pl.multiple_of(i * ft, ft), ft)] = dot_t(dmb[:], w[:])
 
     def battn_body(i, ins, outs, ext):
         (qkv, a, l, sl), (o,), (acc, _, dk, dv) = ins, outs, ext
         da = acc.at[:, pl.ds(pl.multiple_of(i * hd, hd), hd)]
         attn_bwd(*(qkv.at[j, 0] for j in range(3)), a, da, l.at[0], *(o.at[j, 0] for j in range(3)), dk, dv, sl[i], scale, tq)
 
-    def gout_body(i, ins, outs, ext):
-        (a,), (o,), (_, dmb, *_) = ins, outs, ext
-        o[...] = t_dot(a[...], dmb[...]).astype(BF16)
-
     triple = lambda a: (a, (3, 1, seq, hd), lambda i: (0, i, 0, 0))
     pe = [Phase(nf, 2.4, [cols_of(d_up, ft), cols_of(fu, ft)], [], dh2_body),
-          Phase(nm, 2, [rows_of(x1, tm), rows_of(dy, tm), whole(lns)], [rows_of(f32(seq, d), tm), one_vec], ln2b_body),
+          Phase(nm, 2, [rows_of(x1, tm), rows_of(dy, tm), whole(lns)], [rows_of(f32(seq, d), tm), rows_of(act, tm), one_vec], ln2b_body),
           Phase(d // ft, 1.9, [rows_of(fo, ft)], [], dattn_body),
           Phase(heads, 3.5, [triple(qkv.reshape(3, heads, seq, hd)), cols_of(attn, hd), heads_of(lse, 1), slopes],
-                [triple(b16(3, heads, seq, hd))], battn_body),
-          Phase(d // ft, 1.9, [cols_of(attn, ft)], [rows_of(b16(d, d), ft)], gout_body)]
-    d_mid, g_ln2, d_qkv, g_out, *r2 = host('back', pe, S([(g_up, 0, n_down)], carry=r1[1:]),
+                [triple(b16(3, heads, seq, hd))], battn_body)]
+    d_mid, d_mid_bf, g_ln2, d_qkv, *r2 = host('back', pe, S([(g_up, n_down)], [CARRY, n_down - CARRY], carry=r1[1:]),
                                           shared=[vm32(seq, d), vm16(seq, d), vm32(seq, hd), vm32(seq, hd)])
     d_qkv = d_qkv.reshape(3 * heads, seq, hd)
 
-    scat = S([(g_out, 0, d // SUB), (pack, 0, nu)], carry=r2[1:], last=True)
+    no = d // SUB
+    scat = S([*zip(packs, (no, nu))], [CARRY, no, -nu], carry=r2[2:], last=True)
 
     def tile_copy(i, ext):
         r, q = Unit(RB, nq).at(i)
-        return pltpu.make_async_copy(ext[1].at[rest(i, 2)], scat[0].written().at[:, :, :, :, r, q], ext[2].at[rest(i, 2)])
+        return pltpu.make_async_copy(ext[1].at[rest(i, 2)], scat[0].written(-1).at[:, :, :, :, r, q], ext[2].at[rest(i, 2)])
+
+    def slab_copy(i, ext):
+        return pltpu.make_async_copy(ext[3].at[rest(i, 2)], scat[0].written(-2).at[i], ext[2].at[2 + rest(i, 2)])
+
+    def gout_body(i, ins, outs, ext):
+        a, dm = ins
+        r = t_dot(a[:], dm[:]).astype(BF16)
+        if comm:
+            pl.when(i > 1)(lambda: slab_copy(i - 2, ext).wait())
+            ext[3][rest(i, 2)] = r.reshape(*CHIPS[1:], 2, RB, d)
+            slab_copy(i, ext).start()
+        else:
+            outs[0][:] = r
+
+    def ship_out_body(i, ins, outs, ext):
+        for j in (2, 3):
+            slab_copy(j, ext).wait()
+        for u in range(no):
+            scat[0].ship(u)
 
     def macro_body(i, ins, outs, ext):
         (ht, dq, w), acc = ins, ext[0]
         tile = side_by_side(dq, per)
-        r = dot(ht[...], tile).astype(BF16)
+        r = dot(ht[:], tile).astype(BF16)
         if comm:
             ext[1][rest(i, 2)] = r.reshape(*CHIPS, 2, RB, SUB)
             tile_copy(i, ext).start()
         else:
-            outs[0][...] = r
-        put(acc, i, lambda: dot_t(tile, w[...]))
+            outs[0][:] = r
+        put(acc, i, lambda: dot_t(tile, w[:]))
 
     def ship_body(i, ins, outs, ext):
         tile_copy(i, ext).wait()
-        scat[0].ship(i)
+        scat[0].ship(no + i)
 
     def ln1b_body(i, ins, outs, ext):
         (xr, dm, lw), (o, gwo) = ins, outs
-        dx, gw = norm_back(ext[0][band(i)], xr[...].astype(F32), lw[pl.ds(0, 1)])
-        o[...] = (dm[...] + dx).astype(BF16)
+        dx, gw = norm_back(ext[0][band(i)], xr[:].astype(F32), lw[pl.ds(0, 1)])
+        o[:] = (dm[:] + dx).astype(BF16)
         put(gwo, i, lambda: gw)
 
-    first = [] if comm else [cols_of(b16(d, nq), SUB)]
-    pf = [Phase(nu, 3.9, [whole(h1t), heads_of(d_qkv, per), cols_of(fq, SUB)], first, macro_body),
+    firsts = ([], []) if comm else ([rows_of(b16(d, d), slab)], [cols_of(b16(d, nq), SUB)])
+    pf = [Phase(4, 2, [cols_of(attn, slab), whole(d_mid_bf)], firsts[0], gout_body),
+          Phase(nu, 3.9, [whole(h1t), heads_of(d_qkv, per), cols_of(fq, SUB)], firsts[1], macro_body),
           Phase(nm, 2, [rows_of(x, tm), rows_of(d_mid, tm), whole(lns)], [rows_of(act, tm), one_vec], ln1b_body)]
     if comm:
-        pf.append(Phase(nu, 0, [], [], ship_body, 1))
-        scat.append(SmallSum(jnp.pad(g_ln2, ((0, 7), (0, 0))), nu + nm, 1))
-    shared = [vm32(seq, d), vm16(2, *CHIPS, 2, RB, SUB), pltpu.SemaphoreType.DMA((2,))]
-    got = host('last', pf, scat, shared=shared)
+        pf += [Phase(1, 0, [], [], ship_out_body, 4), Phase(nu, 0, [], [], ship_body, 5)]
+        scat.append(SmallSum(g_ln2, 4 + nu + nm, 1))
+    shared = [vm32(seq, d), vm16(2, *CHIPS, 2, RB, SUB), pltpu.SemaphoreType.DMA((4,)), vm16(2, *CHIPS[1:], 2, RB, d)]
+    got = host('last', pf, scat, shared=shared, fires=range(5, 5 + no + nu + 3 * LAG) if comm else None)
     if not comm:
-        g_qkv, dx, g_ln1 = got
+        g_out, g_qkv, dx, g_ln1 = got
         return y, dx, g_ln1, g_qkv, g_out, g_ln2, g_up, g_down
-    dx, _, r3, _, sums = got
-    parts, done = [r1[0], r2[0], r3], 0
-    grads = []
-    for count in (n_down, n_down, d // SUB, nu):
-        pieces, at = [], 0
-        for p in parts:
-            a, b = max(done - at, 0), min(done + count - at, p.shape[0])
-            if a < b:
-                pieces.append(p[a:b])
-            at += p.shape[0]
-        done += count
-        grads.append(jnp.concatenate(pieces))
-    g_down, *others = grads
-    g_down = g_down.reshape(-1, d // SUB, RB, SUB).transpose(0, 2, 1, 3).reshape(-1, d)
-    g_up, g_out, g_qkv = (u.transpose(1, 0, 2).reshape(RB, -1) for u in others)
-    return y, dx, sums, g_qkv, g_out, None, g_up, g_down
+    dx, _, up_b, g_out, g_qkv, _, _, sums = got
+    down_a, (down_b, up_a) = r1[0], r2[:2]
+    g_down = jnp.concatenate([down_a, down_b], axis=1).reshape(RB, -1, d).transpose(1, 0, 2).reshape(-1, d)
+    return y, dx, sums, g_qkv, g_out, None, jnp.concatenate([up_a, up_b], axis=1), g_down
 
 
 def solution(mesh):
@@ -887,10 +915,10 @@
     def step(x_in, ln1_w, w_qkv, w_out, ln2_w, w_up, w_down, dy_out):
         rows, _, heads, hd = w_qkv.shape
         d = x_in.shape[-1]
-        lns = lax.dynamic_update_slice(jnp.zeros((8, d), F32), jnp.stack([ln1_w, ln2_w]), (0, lax.axis_index('fsdp') * rows))
-        y, dx, sums, g_qkv, g_out, _, g_up, g_down = local_step(
-            x_in[0], lns, w_qkv.reshape(rows, -1), w_out, w_up, w_down, dy_out[0])
-        mine = lax.dynamic_slice_in_dim(sums, lax.axis_index('fsdp') * rows, rows, axis=1)
-        return (y[None], dx[None], mine[1], g_qkv.reshape(rows, 3, heads, hd), g_out, mine[0], g_up, g_down)
+        lns = jnp.pad(jnp.stack([ln1_w, ln2_w]), ((0, 6), (0, d - rows)))
+        wq = w_qkv.transpose(1, 2, 0, 3).reshape(-1, rows, hd)
+        y, dx, sums, g_qkv, g_out, _, g_up, g_down = local_step(x_in[0], lns, wq, w_out, w_up, w_down, dy_out[0])
+        g_qkv = g_qkv.reshape(3, heads, rows, hd).transpose(2, 0, 1, 3)
+        return y[None], dx[None], sums[1, :rows], g_qkv, g_out, sums[0, :rows], g_up, g_down
 
     return jax.shard_map(step, mesh=mesh, in_specs=(row_spec,) * 8, out_specs=(row_spec,) * 8, check_vma=False)

time: 599 us -> 594 us (level)
  local copies, waits for them, and re-layouts: 22 us -> 10.8 us
where the time goes in v9:
time: 594 us
  Pallas kernels  578 us (97%)
  local copies, waits for them, and re-layouts  10.8 us (2%)
    pallas_call x4, Pallas kernels, host(): pl.pallas_call(kernel, grid=(total,), in_specs=in_specs, out_specs=out_sp...  578 us

profile of v9, /device:TPU:0, one launch (start us, length us, event | category | flops | bytes accessed | tf_op | source)
XLA Modules:
  0.0 593.9 jit_solution(8659118317742464506)
XLA Ops:
  0.6 1.3 select_maximum_fusion.refs_8_
  1.9 263.5 %forward.1 = (bf16[1536,1024]{1,0:T(8,128)(2,1)}, bf16[36,1024,128]{2,1,0:T(8,128)(2,1)}, bf16[1024,1536]{1,0:T(8,128)(2,1)}, f32[12,1024,1]{2,1,0:T(8,128)}, bf...) custom-call(bf16[1024,1536]{1,0:T(8,128)(2,1)} %bitcast.43, ...), custom_call_target="tpu_custom_call" | custom-call | flops 17179869184 | bytes 33554432 | tf_op jit(solution)/shard_map/forward/pallas_call | solution.py:550
  265.4 101.0 %down.1 = (bf16[1024,6144]{1,0:T(8,128)(2,1)}, bf16[1536,6144]{1,0:T(8,128)(2,1)}, bf16[1024,1536]{1,0:T(8,128)(2,1)}, f32[48,4096]{1,0:T(8,128)}, bf16[2,2,4,2,...) custom-call(bf16[1024,1536]{1,0:T(8,128)(2,1)} %bitcast.31, bf16[6144,1536]{1,0:T(8,128)(2,1)} %bitcast.29, ...), custom_call_target="tpu_custom_call" | custom-call | flops 17179869184 | bytes 33554432 | tf_op jit(solution)/shard_map/down/pallas_call | solution.py:550
  366.5 96.4 %back.1 = (f32[1024,1536]{1,0:T(8,128)}, bf16[1024,1536]{1,0:T(8,128)(2,1)}, f32[1,1536]{1,0:T(1,128)}, bf16[3,12,1024,128]{3,2,1,0:T(8,128)(2,1)}, f32[48,2048]...) custom-call(bf16[1024,6144]{1,0:T(8,128)(2,1)} %get-tuple-element.49.ref, ...), custom_call_target="tpu_custom_call" | custom-call | flops 17179869184 | bytes 33554432 | tf_op jit(solution)/shard_map/back/pallas_call | solution.py:550
  462.9 117.4 %last.1 = (bf16[1024,1536]{1,0:T(8,128)(2,1)}, f32[1,1536]{1,0:T(1,128)}, f32[48,2048]{1,0:T(8,128)}, f32[48,1536]{1,0:T(8,128)}, f32[36,48,128]{2,1,0:T(8,128)}...) custom-call(bf16[1024,1536]{1,0:T(8,128)(2,1)} %get-tuple-element.48.refs_7_.r, ...), custom_call_target="tpu_custom_call" | custom-call | flops 17179869184 | bytes 33554432 | tf_op jit(solution)/shard_map/last/pallas_call | solution.py:550
  580.3 1.3 slice_bitcast_fusion
  581.6 2.8 pad_maximum_fusion
  584.4 0.8 reshape.62
  585.2 1.4 copy.17
  586.6 0.0 copy-start
  586.6 3.9 copy.22
  590.5 0.0 copy-done
  590.5 0.0 copy-start.1
  590.5 0.0 copy-start.2
  590.5 1.7 copy.23
  592.2 0.1 copy-done.1
  592.3 0.9 copy.24
  593.2 0.0 copy-done.2
  593.2 0.7 copy.25
Async XLA Ops:
  586.6 3.9 copy-start
  590.5 1.8 copy-start.1
  590.5 2.7 copy-start.2

commit v10 on v9

--- a/solution.py
+++ b/solution.py
@@ -12,11 +12,13 @@
 LOG2E = math.log2(math.e)
 SUB = 512
 WIDE = 768
+NARROW = 256
 HALF = SUB // 2
 LAG = 2
 GLAG = 1
 CARRY = 2 * LAG
 LEAD = 3
+FRONT = 0.92
 SIDE = -4
 RB = 48
 F32, BF16 = jnp.float32, jnp.bfloat16
@@ -100,46 +102,44 @@
 
 
 class Unit:
-    def __init__(self, rows, cols, width=SUB):
-        self.width, self.nc, self.nr = width, cols // width, rows // RB
-        self.count = self.nc * self.nr
+    def __init__(self, rows, cols, wide=SUB, high=RB):
+        self.wide, self.high, self.nr = wide, high, rows // high
+        self.count = cols // wide * self.nr
 
     def at(self, u, half=None):
-        lanes, col = self.width, rest(u, self.nc) * self.width
+        lanes, col = self.wide, quot(u, self.nr) * self.wide
         if half is not None:
             lanes //= 2
             col = col + half * lanes
-        rows = slice(None) if self.nr == 1 else pl.ds(pl.multiple_of(quot(u, self.nc) * RB, 16), RB)
+        rows = slice(None) if self.nr == 1 else pl.ds(pl.multiple_of(rest(u, self.nr) * self.high, 16), self.high)
         return rows, pl.ds(pl.multiple_of(col, 128), lanes)
 
 
-class Gather:
-    def __init__(self, weights, k0, k1):
-        self.k0, self.k1 = k0, k1
-        self.k, self.tail = k1 - k0 + 1, 0
-        self.z0 = k0 + LEAD if k0 else 0
-        self.z1 = k1 + LEAD
-        self.w, self.ins, self.outs, self.alias = [], [], [], []
-        for shard, full, first in weights:
+class Moves:
+    tail, k, alias = 0, 1, ()
+
+
+class Gather(Moves):
+    def __init__(self, weights):
+        self.w, self.ins, self.outs, n = [], [], [], 0
+        for shard, size in weights:
             heads, rows = shard.shape[:2] if shard.ndim == 3 else (0, shard.shape[0])
             shape = (rows, shard.size // rows)
-            unit = Unit(*shape, WIDE)
-            self.w.append((SIDE if heads else len(self.ins), unit, first, first + unit.count, full is None))
+            unit = Unit(*shape, *size)
+            self.w.append((SIDE if heads else len(self.ins), unit, n, n + unit.count))
+            n += unit.count
+            if heads:
+                self.heads, side = (len(self.ins), heads), pltpu.VMEM(shape, BF16)
             self.ins.append((shard, pl.BlockSpec(memory_space=pltpu.VMEM)))
-            if heads:
-                self.heads, side = (len(self.ins) - 1, heads), pltpu.VMEM(shape, BF16)
-            if full is not None:
-                self.alias.append((len(self.ins), len(self.outs)))
-                self.ins.append((full, pl.BlockSpec(memory_space=HBM)))
             self.outs.append((sds(CHIPS + (2,) + shape, BF16), pl.BlockSpec(memory_space=HBM)))
-        self.base = max(k0 - 2 * GLAG, 0)
-        n = self.z1 - self.base
+        self.n, self.k1 = n, n + 2 * GLAG
+        self.k = self.k1 + 1
         self.scratch = [side, pltpu.SemaphoreType.DMA((n, 8)), pltpu.SemaphoreType.DMA((n, 8)), pltpu.SemaphoreType.DMA((len(weights),))]
 
     def copies(self, stage, w, u, refs):
-        i, unit, first, _, _ = self.w[w]
+        i, unit, first, _ = self.w[w]
         shard, full = refs[i], refs[len(self.ins) + w]
-        sems = lambda i: (refs[-3].at[u - self.base, i], refs[-2].at[u - self.base, i])
+        sems = lambda i: (refs[-3].at[u, i], refs[-2].at[u, i])
         me, z, y, x, c = coords()
         zs, yp, xp, cp = peers()
         r, q = unit.at(u - first)
@@ -160,7 +160,7 @@
         return out
 
     def each(self, lo, hi, u, fn):
-        for w, (_, _, first, last, _) in enumerate(self.w):
+        for w, (_, _, first, last) in enumerate(self.w):
             a, b = max(lo, first), min(hi, last)
             if a < b:
                 if u is None:
@@ -182,42 +182,37 @@
 
     def step(self, k, fire, begin, refs):
         me, z, y, x, c = coords()
-        k0, k1, k = self.k0, self.k1, k + self.k0
-        span = [(self.z0, self.z1)] + [(max(k0 - i * GLAG, 0), k1 - i * GLAG) for i in range(3)]
-
-        @pl.when(fire & (k == k0))
+        n, k1 = self.n, self.k1
+
+        @pl.when(begin)
         def _():
             i, heads = self.heads
             for h in range(heads):
                 refs[SIDE][:, h * 128:(h + 1) * 128] = refs[i][h]
-            own = [pltpu.make_async_copy(refs[i], refs[len(self.ins) + w].at[z, y, x, c], refs[-1].at[w])
-                   for w, (i, _, _, _, fresh) in enumerate(self.w) if fresh]
+            own = [pltpu.make_async_copy(refs[i], refs[len(self.ins) + w].at[z, y, x, c], refs[-1].at[w]) for w, (i, *_) in enumerate(self.w)]
             for cp in own:
                 cp.start()
-            if k0 == 0:
-                self.each(0, LEAD, None, lambda w, u: self.go(0, w, u, refs))
+            self.each(0, LEAD, None, lambda w, u: self.go(0, w, u, refs))
             for cp in own:
                 cp.wait()
 
         @pl.when(fire & (k < k1))
         def _():
-            self.each(*span[0], k + LEAD, lambda w, u: self.go(0, w, u, refs))
+            self.each(0, n, k + LEAD, lambda w, u: self.go(0, w, u, refs))
             for stage in (1, 2, 3):
                 u = k + GLAG * (1 - stage)
-                lo, hi = span[stage - 1]
-                self.each(lo, hi, u, lambda w, u: self.arrive(stage - 1, w, u, refs))
-                self.each(*span[stage], u, lambda w, u: self.go(stage, w, u, refs))
-            self.each(*span[3], k - 3 * GLAG, lambda w, u: self.arrive(3, w, u, refs))
+                self.each(0, n, u, lambda w, u: self.arrive(stage - 1, w, u, refs))
+                self.each(0, n, u, lambda w, u: self.go(stage, w, u, refs))
+            self.each(0, n, k - 3 * GLAG, lambda w, u: self.arrive(3, w, u, refs))
 
         @pl.when(fire & (k == k1))
         def _():
+            self.each(k1 - 3 * GLAG, n, None, lambda w, u: self.arrive(3, w, u, refs))
             for stage in range(4):
-                lo, hi = span[stage]
-                self.each(max(lo, k1 - stage * GLAG), hi, None, lambda w, u: self.arrive(stage, w, u, refs))
-                self.each(lo, hi, None, lambda w, u: self.left(stage, w, u, refs))
-
-
-class Scatter:
+                self.each(0, n, None, lambda w, u: self.left(stage, w, u, refs))
+
+
+class Scatter(Moves):
     def __init__(self, grads, layout, carry=None, last=False):
         self.last, self.carried = last, carry is not None
         self.parts, self.ins, n = [], [], 0
@@ -235,7 +230,8 @@
         self.end = n + CARRY
         self.done = self.end if last else n
         self.k = n + (3 * LAG if last else 1)
-        self.tail = 3 * LAG - 1 if last else 0
+        if last:
+            self.tail = 3 * LAG - 1
         self.two_shape, self.three_shape = (2, 4, 2, RB, HALF), (4, RB, SUB)
         if self.carried:
             self.ins += [(a, pl.BlockSpec(memory_space=pltpu.VMEM)) for a in carry]
@@ -247,7 +243,7 @@
             pltpu.VMEM((self.end, 3, RB, SUB), BF16),
             pltpu.SemaphoreType.DMA((self.end, 8)), pltpu.SemaphoreType.DMA((self.end, 8)), pltpu.SemaphoreType.DMA((2,))]
         self.layout = layout
-        outs = [sds((RB, n * SUB) if n > 0 else (-n * SUB // 128, RB, 128), F32) for n in layout]
+        outs = [sds((nr * RB, m // nr * SUB) if nr else (m * SUB // 128, RB, 128), F32) for nr, m in layout]
         if not last:
             outs += [sds((LAG, *shape), BF16) for shape in (self.two_shape, self.three_shape)]
         self.outs = [(o, pl.BlockSpec(memory_space=pltpu.VMEM)) for o in outs]
@@ -267,7 +263,7 @@
         return self.refs[len(self.ins) + len(self.outs) + i]
 
     def ship(self, u):
-        self.swap(CARRY + u, self.refs, lambda cp: cp.start())
+        self.swap(CARRY + self.known + u, self.refs, lambda cp: cp.start())
 
     def bufs(self, refs):
         return refs[len(self.ins) + len(self.outs):]
@@ -323,16 +319,18 @@
             for d in range(3):
                 total += four[j, d].astype(F32)
             a = self.first
-            for i, n in enumerate(self.layout):
-                b, out = a + abs(n), refs[len(self.ins) + i]
+            for i, (nr, m) in enumerate(self.layout):
+                b, out = a + m, refs[len(self.ins) + i]
 
                 @pl.when((j >= a) & (j < b))
-                def _(out=out, a=a, n=n):
-                    if n > 0:
-                        out[:, pl.ds(pl.multiple_of((j - a) * SUB, SUB), SUB)] = total
+                def _(out=out, nr=nr, u=j - a):
+                    if nr:
+                        rows, cols = pl.ds(pl.multiple_of(rest(u, nr) * RB, RB), RB), pl.ds(pl.multiple_of(quot(u, nr) * SUB, SUB), SUB)
+                        out[rows, cols] = total
                     else:
-                        for h in range(SUB // 128):
-                            out[(j - a) * (SUB // 128) + h] = total[:, h * 128:(h + 1) * 128]
+                        lane = out.shape[-1]
+                        for h in range(SUB // lane):
+                            out[u * (SUB // lane) + h] = total[:, h * lane:(h + 1) * lane]
 
                 a = b
 
@@ -365,9 +363,9 @@
         @pl.when(fire & (k < n))
         def _():
             j = k + CARRY
-            if not self.known:
-                pl.when(j == CARRY)(lambda: self.local(j, refs, start))
-            pl.when(j + 1 < end)(lambda: self.local(j + 1, refs, start))
+            late = CARRY + self.known
+            pl.when(j == late)(lambda: self.local(j, refs, start))
+            pl.when((j + 1 < end) & (j + 1 != late))(lambda: self.local(j + 1, refs, start))
             self.swap(j, refs, lambda cp: cp.wait_recv())
             self.local(j, refs, lambda cp: cp.wait())
             self.add(1, j, refs)
@@ -405,10 +403,10 @@
                     refs[len(self.ins) + len(self.layout) + 1][i] = three[n + i]
 
 
-class SmallSum:
+class SmallSum(Moves):
     def __init__(self, rows, t0, at=None):
         d = rows.shape[1]
-        self.at, self.t0, self.k, self.tail = at, t0, 1, 0
+        self.at, self.t0 = at, t0
         self.ins = [(rows, pl.BlockSpec(memory_space=pltpu.VMEM))]
         self.outs = [(sds((8, d if at is None else 128), F32), pl.BlockSpec(memory_space=pltpu.VMEM))]
         self.alias = []
@@ -464,8 +462,9 @@
         for t in range(at):
             clock.append(clock[-1] + sum(p.cost for p in phases if p.at <= t < p.at + p.n))
         for k in range(1, k_all):
-            t = at if k >= spread else min(t for t in range(at + 1) if clock[t] * spread >= clock[at] * k)
+            t = at if k >= spread else min(t for t in range(at + 1) if clock[t] * spread >= FRONT * clock[at] * k)
             fires.append(max(t, fires[-1] + 1))
+    assert len(fires) == k_all
     total = max([at, fires[-1] + 1] + [c.t0 + 5 for c in small])
     ins, in_specs, outs, out_specs, scratch, alias, resident = [], [], [], [], [], {}, []
     for p in phases:
@@ -687,17 +686,16 @@
     band = lambda i, n=tm: pl.ds(pl.multiple_of(i * n, n), n)
     ts = tm // 2
     ns = seq // ts
-    order = [n // (WIDE * d) for n in (d * nq, d * d, d * ff, d * ff)]
-    qs, os, us, ds = (sum(order[:i]) for i in range(4))
+    qs, os, us, ds = (n // WIDE for n in (0, nq, nq + d, nq + d + ff))
     nu = nq // SUB
     packs = [sds((*CHIPS, 2, RB, n), BF16) for n in (d, nq)]
 
     def S(parts, *args, **kw):
-        return [Scatter([(a.reshape(*CHIPS, 2, -1, a.shape[-1]) if isinstance(a, jax.Array) else a, 0, n) for a, n in parts], *args, **kw)] if comm else []
+        return [Scatter([(a.reshape(*CHIPS, 2, -1, a.shape[-1]) if isinstance(a, jax.Array) else a, u0, n) for a, u0, n in parts], *args, **kw)] if comm else []
 
     blocks = lambda w: w.reshape(*CHIPS, 2, -1, w.shape[-1])
     if comm:
-        gather = Gather([(wq, None, qs), (wo, None, os), (wu, None, us), (wd, None, ds)], 0, sum(order) + 2 * GLAG)
+        gather = Gather([(w, (WIDE,)) for w in (wq, wo, wu)] + [(wd, (NARROW, wd.shape[0]))])
         lnsum = SmallSum(lns, 0)
     held = {}
 
@@ -711,6 +709,10 @@
                 out.append(pltpu.make_async_copy(full.at[:, :, :, :, r, q], ext[3].at[slot], ext[4].at[slot]))
         return out[0]
 
+    def load_down(i, ext):
+        full = gather.refs[len(gather.ins) + 3] if comm else held['weights'][3]
+        return pltpu.make_async_copy(full.at[:, :, :, :, :, pl.ds(pl.multiple_of(i * NARROW, NARROW), NARROW)], ext[5], ext[4].at[0])
+
     def weight(u, ext):
         return ext[3][rest(u, 2)].reshape(d, WIDE)
 
@@ -730,20 +732,23 @@
         h[band(i, ts)] = h1
         ht[:] = h1.T
 
+    def head_of(qkv, h):
+        return qkv.at[:, pl.ds(pl.multiple_of(h * hd, hd), hd)]
+
     def qkv_body(i, ins, outs, ext):
         (o,), (qkv, h, *_) = outs, ext
         load((qs, i), ext).wait()
         r = dot(h[:], weight(i, ext)).astype(BF16)
         for j in range(wide):
             head = r[:, j * hd:(j + 1) * hd]
-            qkv[i * wide + j] = head
+            head_of(qkv, i * wide + j)[:] = head
             o[j] = head
         pl.when(i + 2 < os)(lambda: load((qs, i + 2), ext).start())
         pl.when(i + 2 >= os)(lambda: load((os, i + 2), ext).start())
 
     def attn_body(i, ins, outs, ext):
         (sl,), (o, l), (qkv, _, a, *_) = ins, outs, ext
-        attn_fwd(qkv.at[i], qkv.at[heads + i], qkv.at[2 * heads + i], o, l.at[0], sl[i], scale, tq)
+        attn_fwd(*(head_of(qkv, j * heads + i) for j in range(3)), o, l.at[0], sl[i], scale, tq)
         a[:, pl.ds(pl.multiple_of(i * hd, hd), hd)] = o[:]
 
     def out_body(i, ins, outs, ext):
@@ -758,6 +763,7 @@
         r = jnp.concatenate([dot(ar, weight(u, ext)) for u in range(os, us)], axis=1)
         x1 = (xs[:].astype(F32) + r).astype(BF16)
         o[:] = x1
+        a[band(i, ts)] = x1
         xhat, _ = norm_parts(x1.astype(F32))
         h2 = (xhat * gain(1)).astype(BF16)
         h[band(i, ts)] = h2
@@ -769,49 +775,51 @@
                 load((us, u), ext).start()
 
     def up_body(i, ins, outs, ext):
-        (dyr,), (go, gpo, gd), h = ins, outs, ext[1]
+        (dyr,), (gpo, gd), (go, h, *_) = ins, outs, ext
         load((us, us + i), ext).wait()
         u = dot(h[:], weight(us + i, ext))
         cdf = 0.5 * (1.0 + lax.erf(u * math.sqrt(0.5)))
         g = (u * cdf).astype(BF16)
-        go[:] = g
+        go[:, pl.ds(pl.multiple_of(i * WIDE, WIDE), WIDE)] = g
         gpo[:] = cdf + u * (jnp.exp(-0.5 * u * u) * math.sqrt(0.5 / math.pi))
         gd[:] = t_dot(g, dyr[:]).astype(BF16)
         pl.when(us + i + 2 < ds)(lambda: load((us, us + i + 2), ext).start())
 
+    def y_body(i, ins, outs, ext):
+        (o,), (gr, _, x1r, *_) = outs, ext
+        load_down(i, ext).start()
+        load_down(i, ext).wait()
+        cols = pl.ds(pl.multiple_of(i * NARROW, NARROW), NARROW)
+        o[:] = (x1r[:, cols].astype(F32) + dot(gr[:], ext[5][:].reshape(ff, NARROW))).astype(BF16)
+
     wide = WIDE // hd
-    more = [] if comm else [(lns, pltpu.VMEM, None)] + [(blocks(w), HBM, None) for w in (wq, wo, wu)]
+    more = [] if comm else [(lns, pltpu.VMEM, None)] + [(blocks(w), HBM, None) for w in (wq, wo, wu, wd)]
     pa = [Phase(ns, 1, [rows_of(x, ts), *more], [cols_of(b16(d, seq), ts)], ln1_body, 5),
           Phase(1, 0, [], [], start_body, 4),
           Phase(nq // WIDE, 3, [], [heads_of(b16(3 * heads, seq, hd), wide)], qkv_body, 5 + ns),
           Phase(heads, 2.7, [slopes], [cols_of(act, hd), heads_of(f32(heads, seq, 1), 1)], attn_body, 5 + ns + nq // WIDE),
           Phase(ns, 2, [rows_of(x, ts)], [rows_of(act, ts), cols_of(b16(d, seq), ts)], out_body, 5 + ns + nq // WIDE + heads),
-          Phase(ff // WIDE, 6, [whole(dy)], [cols_of(wide_act, WIDE), cols_of(f32(seq, ff), WIDE), rows_of(b16(ff, d), WIDE)], up_body, 5 + 2 * ns + nq // WIDE + heads)]
-    shared = [vm16(3 * heads, seq, hd), vm16(seq, d), vm16(seq, d), vm16(2, *CHIPS, 2, RB, WIDE), pltpu.SemaphoreType.DMA((2,))]
-    t_qkv, t_attn, t_out, t_up = (p.at for p in pa[2:])
-    fires = [*range(6), t_qkv - 4, t_qkv, t_qkv + 2, t_qkv + 4, t_attn - 1, *range(t_attn, t_up, 4), *range(t_up, t_up + ff // WIDE + 3)]
+          Phase(ff // WIDE, 6, [whole(dy)], [cols_of(f32(seq, ff), WIDE), rows_of(b16(ff, d), WIDE)], up_body, 5 + 2 * ns + nq // WIDE + heads),
+          Phase(d // NARROW, 4, [], [cols_of(act, NARROW)], y_body, 4 + 2 * ns + nq // WIDE + heads + ff // WIDE)]
+    shared = [vm16(seq, ff), vm16(seq, d), vm16(seq, d), vm16(2, *CHIPS, 2, RB, WIDE), pltpu.SemaphoreType.DMA((2,)), vm16(*CHIPS, 2, ff // 32, NARROW)]
+    t_qkv, t_attn, t_out, t_up, t_y = (p.at for p in pa[2:])
+    fires = [*range(6), t_qkv - 4, t_qkv, t_qkv + 2, t_qkv + 4, t_attn - 1, *range(t_attn, t_up, 4), *range(t_up, t_y, 2), *range(t_y + 1, t_y + d // NARROW)]
     got = host('forward', pa, [gather, lnsum] if comm else [], shared=shared, fires=fires if comm else None)
-    h1t, qkv, attn, lse, x1, h2t, g, gp, g_down, *full = got
+    h1t, qkv, attn, lse, x1, h2t, gp, g_down, y, *full = got
     fq, fo, fu, fd = wq, wo, wu, wd
     if comm:
         fq, fo, fu, fd = (f.reshape(-1, f.shape[-1]) for f in full[:4])
         lns = full[4]
 
     def dup_body(i, ins, outs, ext):
-        (dyr, w, gr, gpr, ht), (duo, gu), (acc,) = ins, outs, ext
+        (dyr, w, gpr, ht), (duo, gu) = ins, outs
         du = (dot_t(dyr[:], w[:]) * gpr[:]).astype(BF16)
         duo[:] = du
         gu[:] = dot(ht[:], du).astype(BF16)
-        put(acc, i, lambda: dot(gr[:], w[:]))
-
-    def y_body(i, ins, outs, ext):
-        (xr,), (o,), (acc,) = ins, outs, ext
-        o[:] = (xr[:].astype(F32) + acc[band(i)]).astype(BF16)
-
-    pd = [Phase(nf, 6, [whole(dy), rows_of(fd, ft), cols_of(g, ft), cols_of(gp, ft), whole(h2t)], [cols_of(wide_act, ft), cols_of(b16(d, ff), ft)], dup_body),
-          Phase(nm, 1, [rows_of(x1, tm)], [rows_of(act, tm)], y_body)]
+
+    pd = [Phase(nf, 4.6, [whole(dy), rows_of(fd, ft), cols_of(gp, ft), whole(h2t)], [cols_of(wide_act, ft), cols_of(b16(d, ff), ft)], dup_body)]
     n_down = Unit(ff // 32, d).count
-    d_up, g_up, y, *r1 = host('down', pd, S([(g_down, n_down)], [n_down - CARRY]), shared=[vm32(seq, d)])
+    d_up, g_up, *r1 = host('down', pd, S([(g_down, 0, n_down)], [(4, n_down - CARRY)]))
 
     def dh2_body(i, ins, outs, ext):
         (du, w), acc = ins, ext[0]
@@ -831,21 +839,28 @@
 
     def battn_body(i, ins, outs, ext):
         (qkv, a, l, sl), (o,), (acc, _, dk, dv) = ins, outs, ext
-        da = acc.at[:, pl.ds(pl.multiple_of(i * hd, hd), hd)]
-        attn_bwd(*(qkv.at[j, 0] for j in range(3)), a, da, l.at[0], *(o.at[j, 0] for j in range(3)), dk, dv, sl[i], scale, tq)
-
-    triple = lambda a: (a, (3, 1, seq, hd), lambda i: (0, i, 0, 0))
+
+        @pl.loop(0, pair)
+        def _(j):
+            h = i * pair + j
+            own, here = (pl.ds(pl.multiple_of(n * hd, hd), hd) for n in (h, j))
+            attn_bwd(*(qkv.at[n, j] for n in range(3)), a.at[:, here], acc.at[:, own], l.at[j], *(o.at[n, j] for n in range(3)),
+                     dk, dv, sl[h], scale, tq)
+
+    pair = 2
+    triple = lambda a: (a, (3, pair, seq, hd), lambda i: (0, i, 0, 0))
     pe = [Phase(nf, 2.4, [cols_of(d_up, ft), cols_of(fu, ft)], [], dh2_body),
           Phase(nm, 2, [rows_of(x1, tm), rows_of(dy, tm), whole(lns)], [rows_of(f32(seq, d), tm), rows_of(act, tm), one_vec], ln2b_body),
           Phase(d // ft, 1.9, [rows_of(fo, ft)], [], dattn_body),
-          Phase(heads, 3.5, [triple(qkv.reshape(3, heads, seq, hd)), cols_of(attn, hd), heads_of(lse, 1), slopes],
+          Phase(heads // pair, 6, [triple(qkv.reshape(3, heads, seq, hd)), cols_of(attn, pair * hd), heads_of(lse, pair), slopes],
                 [triple(b16(3, heads, seq, hd))], battn_body)]
-    d_mid, d_mid_bf, g_ln2, d_qkv, *r2 = host('back', pe, S([(g_up, n_down)], [CARRY, n_down - CARRY], carry=r1[1:]),
+    early = n_down - 2
+    d_mid, d_mid_bf, g_ln2, d_qkv, *r2 = host('back', pe, S([(g_up, 0, early)], [(4, CARRY), (1, early - CARRY)], carry=r1[1:]),
                                           shared=[vm32(seq, d), vm16(seq, d), vm32(seq, hd), vm32(seq, hd)])
     d_qkv = d_qkv.reshape(3 * heads, seq, hd)
 
     no = d // SUB
-    scat = S([*zip(packs, (no, nu))], [CARRY, no, -nu], carry=r2[2:], last=True)
+    scat = S([(g_up, early, 2), (packs[0], 0, no), (packs[1], 0, nu)], [(1, CARRY + 2), (1, no), (0, nu)], carry=r2[2:], last=True)
 
     def tile_copy(i, ext):
         r, q = Unit(RB, nq).at(i)
@@ -899,14 +914,14 @@
         pf += [Phase(1, 0, [], [], ship_out_body, 4), Phase(nu, 0, [], [], ship_body, 5)]
         scat.append(SmallSum(g_ln2, 4 + nu + nm, 1))
     shared = [vm32(seq, d), vm16(2, *CHIPS, 2, RB, SUB), pltpu.SemaphoreType.DMA((4,)), vm16(2, *CHIPS[1:], 2, RB, d)]
-    got = host('last', pf, scat, shared=shared, fires=range(5, 5 + no + nu + 3 * LAG) if comm else None)
+    got = host('last', pf, scat, shared=shared, fires=[0, 2, *range(5, 5 + no + nu + 3 * LAG)] if comm else None)
     if not comm:
         g_out, g_qkv, dx, g_ln1 = got
         return y, dx, g_ln1, g_qkv, g_out, g_ln2, g_up, g_down
     dx, _, up_b, g_out, g_qkv, _, _, sums = got
     down_a, (down_b, up_a) = r1[0], r2[:2]
-    g_down = jnp.concatenate([down_a, down_b], axis=1).reshape(RB, -1, d).transpose(1, 0, 2).reshape(-1, d)
-    return y, dx, sums, g_qkv, g_out, None, jnp.concatenate([up_a, up_b], axis=1), g_down
+    g_up, g_down = (jnp.concatenate(p, axis=1) for p in ((up_a, up_b), (down_a, down_b)))
+    return y, dx, sums, g_qkv, g_out, g_up, g_down
 
 
 def solution(mesh):
@@ -917,7 +932,7 @@
         d = x_in.shape[-1]
         lns = jnp.pad(jnp.stack([ln1_w, ln2_w]), ((0, 6), (0, d - rows)))
         wq = w_qkv.transpose(1, 2, 0, 3).reshape(-1, rows, hd)
-        y, dx, sums, g_qkv, g_out, _, g_up, g_down = local_step(x_in[0], lns, wq, w_out, w_up, w_down, dy_out[0])
+        y, dx, sums, g_qkv, g_out, g_up, g_down = local_step(x_in[0], lns, wq, w_out, w_up, w_down, dy_out[0])
         g_qkv = g_qkv.reshape(3, heads, rows, hd).transpose(2, 0, 1, 3)
         return y[None], dx[None], sums[1, :rows], g_qkv, g_out, sums[0, :rows], g_up, g_down
 

time: 594 us -> 610 us (1.027)
  Pallas kernels: 578 us -> 595 us
    pallas_call x4, Pallas kernels: 578 us -> 595 us  [host(): pl.pallas_call(kernel, grid=(total,), in_specs=in_specs, out_specs=out_sp...]
where the time goes in v10:
time: 610 us; the launch traced here: 609 us
  Pallas kernels  595 us (98%)
  local copies, waits for them, and re-layouts  7.78 us (1%)
    pallas_call x4, Pallas kernels, host(): pl.pallas_call(kernel, grid=(total,), in_specs=in_specs, out_specs=out_sp...  595 us

profile of v10, /device:TPU:0, one launch (start us, length us, event | category | flops | bytes accessed | tf_op | source)
XLA Modules:
  0.0 609.0 jit_solution(15692230091884376910)
XLA Ops:
  0.6 1.3 select_maximum_fusion.refs_8_
  1.9 285.0 %forward.1 = (bf16[1536,1024]{1,0:T(8,128)(2,1)}, bf16[36,1024,128]{2,1,0:T(8,128)(2,1)}, bf16[1024,1536]{1,0:T(8,128)(2,1)}, f32[12,1024,1]{2,1,0:T(8,128)}, bf...) custom-call(bf16[1024,1536]{1,0:T(8,128)(2,1)} %bitcast.40, ...), custom_call_target="tpu_custom_call" | custom-call | flops 17179869184 | bytes 33554432 | tf_op jit(solution)/shard_map/forward/pallas_call | solution.py:549
  287.0 92.3 %down.1 = (bf16[1024,6144]{1,0:T(8,128)(2,1)}, bf16[1536,6144]{1,0:T(8,128)(2,1)}, f32[192,1024]{1,0:T(8,128)}, bf16[2,2,4,2,48,256]{5,4,3,2,1,0:T(8,128)(2,1)}, bf16[2,4,48,512]{3,2,1,0:T(8,128)(2,1)}) custom-call(bf16[1024,1536]{1,0:T(8,128)(2,1)} %bitcast.30, bf16[6144,1536]{1,0:T(8,128)(2,1)} %bitcast.28, f32[1024,6144]{1,0:T(8,128)} %get-tuple-element.43.refs_2_, ...), custom_call_target="tpu_custom_call" | custom-call | flops 17179869184 | bytes 33554432 | tf_op jit(solution)/shard_map/down/pallas_call | solution.py:549
  379.2 93.8 %back.1 = (f32[1024,1536]{1,0:T(8,128)}, bf16[1024,1536]{1,0:T(8,128)(2,1)}, f32[1,1536]{1,0:T(1,128)}, bf16[3,12,1024,128]{3,2,1,0:T(8,128)(2,1)}, f32[192,512]...) custom-call(bf16[1024,6144]{1,0:T(8,128)(2,1)} %get-tuple-element.46.ref, ...), custom_call_target="tpu_custom_call" | custom-call | flops 17179869184 | bytes 33554432 | tf_op jit(solution)/shard_map/back/pallas_call | solution.py:549
  473.0 123.5 %last.1 = (bf16[1024,1536]{1,0:T(8,128)(2,1)}, f32[1,1536]{1,0:T(1,128)}, f32[48,3072]{1,0:T(8,128)}, f32[48,1536]{1,0:T(8,128)}, f32[36,48,128]{2,1,0:T(8,128)}...) custom-call(bf16[1024,1536]{1,0:T(8,128)(2,1)} %get-tuple-element.41.refs_7_.r, ...), custom_call_target="tpu_custom_call" | custom-call | flops 17179869184 | bytes 33554432 | tf_op jit(solution)/shard_map/last/pallas_call | solution.py:549
  596.6 0.0 copy-start
  596.6 1.3 slice_bitcast_fusion
  597.9 2.4 pad_maximum_fusion.1
  600.3 2.3 pad_maximum_fusion
  602.6 0.0 copy-done
  602.6 0.0 copy-start.1
  602.6 1.7 copy.21
  604.3 1.4 copy-done.1
  605.6 0.0 copy-start.2
  605.6 0.0 copy-start.3
  605.6 1.7 copy.22
  607.3 0.1 copy-done.2
  607.4 0.9 copy.23
  608.3 0.0 copy-done.3
  608.3 0.7 copy.24
Async XLA Ops:
  596.6 6.1 copy-start
  602.6 3.0 copy-start.1
  605.6 1.8 copy-start.2
  605.6 2.7 copy-start.3

commit v11 on v9

--- a/solution.py
+++ b/solution.py
@@ -120,10 +120,10 @@
         self.z0 = k0 + LEAD if k0 else 0
         self.z1 = k1 + LEAD
         self.w, self.ins, self.outs, self.alias = [], [], [], []
-        for shard, full, first in weights:
+        for shard, full, first, wide in weights:
             heads, rows = shard.shape[:2] if shard.ndim == 3 else (0, shard.shape[0])
             shape = (rows, shard.size // rows)
-            unit = Unit(*shape, WIDE)
+            unit = Unit(*shape, wide)
             self.w.append((SIDE if heads else len(self.ins), unit, first, first + unit.count, full is None))
             self.ins.append((shard, pl.BlockSpec(memory_space=pltpu.VMEM)))
             if heads:
@@ -672,7 +672,7 @@
 def local_step(x, lns, wq, wo, wu, wd, dy, comm=True):
     seq, d = x.shape
     heads, hd, ft = 12, 128, 512
-    ff, nq, per, slab = wu.shape[1], 3 * d, SUB // hd, d // 4
+    ff, nq, per, slab = wu.shape[1], 3 * d, SUB // hd, 3 * hd
     scale = 1 / math.sqrt(hd)
     tq = min(256, seq)
     tm = tq
@@ -687,17 +687,17 @@
     band = lambda i, n=tm: pl.ds(pl.multiple_of(i * n, n), n)
     ts = tm // 2
     ns = seq // ts
-    order = [n // (WIDE * d) for n in (d * nq, d * d, d * ff, d * ff)]
-    qs, os, us, ds = (sum(order[:i]) for i in range(4))
+    qs, os, us, ds = (n // WIDE for n in (0, nq, nq + d, nq + d + ff))
     nu = nq // SUB
-    packs = [sds((*CHIPS, 2, RB, n), BF16) for n in (d, nq)]
+    pack = sds((*CHIPS, 2, RB, nq), BF16)
 
     def S(parts, *args, **kw):
         return [Scatter([(a.reshape(*CHIPS, 2, -1, a.shape[-1]) if isinstance(a, jax.Array) else a, 0, n) for a, n in parts], *args, **kw)] if comm else []
 
     blocks = lambda w: w.reshape(*CHIPS, 2, -1, w.shape[-1])
     if comm:
-        gather = Gather([(wq, None, qs), (wo, None, os), (wu, None, us), (wd, None, ds)], 0, sum(order) + 2 * GLAG)
+        half = (ds - us) // 2
+        gather = Gather([(wq, None, qs, WIDE), (wo, None, os, WIDE), (wu, None, us, d), (wd, None, us + half, d)], qs, ds + 2 * GLAG)
         lnsum = SmallSum(lns, 0)
     held = {}
 
@@ -739,12 +739,16 @@
             qkv[i * wide + j] = head
             o[j] = head
         pl.when(i + 2 < os)(lambda: load((qs, i + 2), ext).start())
-        pl.when(i + 2 >= os)(lambda: load((os, i + 2), ext).start())
 
     def attn_body(i, ins, outs, ext):
         (sl,), (o, l), (qkv, _, a, *_) = ins, outs, ext
         attn_fwd(qkv.at[i], qkv.at[heads + i], qkv.at[2 * heads + i], o, l.at[0], sl[i], scale, tq)
         a[:, pl.ds(pl.multiple_of(i * hd, hd), hd)] = o[:]
+
+        @pl.when(i == heads // 2)
+        def _():
+            for u in range(os, us):
+                load((os, u), ext).start()
 
     def out_body(i, ins, outs, ext):
         (xs,), (o, ht), (_, h, a, *_) = ins, outs, ext
@@ -789,7 +793,8 @@
           Phase(ff // WIDE, 6, [whole(dy)], [cols_of(wide_act, WIDE), cols_of(f32(seq, ff), WIDE), rows_of(b16(ff, d), WIDE)], up_body, 5 + 2 * ns + nq // WIDE + heads)]
     shared = [vm16(3 * heads, seq, hd), vm16(seq, d), vm16(seq, d), vm16(2, *CHIPS, 2, RB, WIDE), pltpu.SemaphoreType.DMA((2,))]
     t_qkv, t_attn, t_out, t_up = (p.at for p in pa[2:])
-    fires = [*range(6), t_qkv - 4, t_qkv, t_qkv + 2, t_qkv + 4, t_attn - 1, *range(t_attn, t_up, 4), *range(t_up, t_up + ff // WIDE + 3)]
+    fires = [*range(6), t_qkv - 4, t_qkv, t_qkv + 2, t_attn, t_attn + heads // 2, t_out, *range(t_up, t_up + ff // WIDE, 2)]
+    fires += [fires[-1] + i for i in (2, 3, 4)]
     got = host('forward', pa, [gather, lnsum] if comm else [], shared=shared, fires=fires if comm else None)
     h1t, qkv, attn, lse, x1, h2t, g, gp, g_down, *full = got
     fq, fo, fu, fd = wq, wo, wu, wd
@@ -818,57 +823,49 @@
         put(acc, i, lambda: dot_t(du[:], w[:]))
 
     def ln2b_body(i, ins, outs, ext):
-        (xr, dyr, lw), (dmo, dmbo, gwo), (acc, dmb, *_) = ins, outs, ext
+        (xr, dyr, lw), (dmo, gwo), (acc, dmb, *_) = ins, outs, ext
         dx, gw = norm_back(acc[band(i)], xr[:].astype(F32), lw[pl.ds(1, 1)])
         dm = dyr[:].astype(F32) + dx
         dmo[:] = dm
-        dmb[band(i)] = dmbo[:] = dm.astype(BF16)
+        dmb[band(i)] = dm.astype(BF16)
         put(gwo, i, lambda: gw)
 
     def dattn_body(i, ins, outs, ext):
         (w,), (acc, dmb, *_) = ins, ext
-        acc[:, pl.ds(pl.multiple_of(i * ft, ft), ft)] = dot_t(dmb[:], w[:])
+        acc[:, pl.ds(pl.multiple_of(i * slab, slab), slab)] = dot_t(dmb[:], w[:])
 
     def battn_body(i, ins, outs, ext):
         (qkv, a, l, sl), (o,), (acc, _, dk, dv) = ins, outs, ext
-        da = acc.at[:, pl.ds(pl.multiple_of(i * hd, hd), hd)]
-        attn_bwd(*(qkv.at[j, 0] for j in range(3)), a, da, l.at[0], *(o.at[j, 0] for j in range(3)), dk, dv, sl[i], scale, tq)
-
-    triple = lambda a: (a, (3, 1, seq, hd), lambda i: (0, i, 0, 0))
+
+        @pl.loop(0, pair)
+        def _(j):
+            h = i * pair + j
+            own, here = (pl.ds(pl.multiple_of(n * hd, hd), hd) for n in (h, j))
+            attn_bwd(*(qkv.at[n, j] for n in range(3)), a.at[:, here], acc.at[:, own], l.at[j], *(o.at[n, j] for n in range(3)),
+                     dk, dv, sl[h], scale, tq)
+
+    def gout_body(i, ins, outs, ext):
+        (a,), (o,), (_, dmb, *_) = ins, outs, ext
+        o[:] = t_dot(a[:], dmb[:]).astype(BF16)
+
+    pair = 2
+    triple = lambda a: (a, (3, pair, seq, hd), lambda i: (0, i, 0, 0))
     pe = [Phase(nf, 2.4, [cols_of(d_up, ft), cols_of(fu, ft)], [], dh2_body),
-          Phase(nm, 2, [rows_of(x1, tm), rows_of(dy, tm), whole(lns)], [rows_of(f32(seq, d), tm), rows_of(act, tm), one_vec], ln2b_body),
-          Phase(d // ft, 1.9, [rows_of(fo, ft)], [], dattn_body),
-          Phase(heads, 3.5, [triple(qkv.reshape(3, heads, seq, hd)), cols_of(attn, hd), heads_of(lse, 1), slopes],
-                [triple(b16(3, heads, seq, hd))], battn_body)]
-    d_mid, d_mid_bf, g_ln2, d_qkv, *r2 = host('back', pe, S([(g_up, n_down)], [CARRY, n_down - CARRY], carry=r1[1:]),
+          Phase(nm, 2, [rows_of(x1, tm), rows_of(dy, tm), whole(lns)], [rows_of(f32(seq, d), tm), one_vec], ln2b_body),
+          Phase(d // slab, 1.9, [rows_of(fo, slab)], [], dattn_body),
+          Phase(heads // pair, 6, [triple(qkv.reshape(3, heads, seq, hd)), cols_of(attn, pair * hd), heads_of(lse, pair), slopes],
+                [triple(b16(3, heads, seq, hd))], battn_body),
+          Phase(d // slab, 2, [cols_of(attn, slab)], [rows_of(b16(d, d), slab)], gout_body)]
+    d_mid, g_ln2, d_qkv, g_out, *r2 = host('back', pe, S([(g_up, n_down)], [CARRY, n_down - CARRY], carry=r1[1:]),
                                           shared=[vm32(seq, d), vm16(seq, d), vm32(seq, hd), vm32(seq, hd)])
     d_qkv = d_qkv.reshape(3 * heads, seq, hd)
 
     no = d // SUB
-    scat = S([*zip(packs, (no, nu))], [CARRY, no, -nu], carry=r2[2:], last=True)
+    scat = S([(g_out, no), (pack, nu)], [CARRY, no, -nu], carry=r2[2:], last=True)
 
     def tile_copy(i, ext):
         r, q = Unit(RB, nq).at(i)
         return pltpu.make_async_copy(ext[1].at[rest(i, 2)], scat[0].written(-1).at[:, :, :, :, r, q], ext[2].at[rest(i, 2)])
-
-    def slab_copy(i, ext):
-        return pltpu.make_async_copy(ext[3].at[rest(i, 2)], scat[0].written(-2).at[i], ext[2].at[2 + rest(i, 2)])
-
-    def gout_body(i, ins, outs, ext):
-        a, dm = ins
-        r = t_dot(a[:], dm[:]).astype(BF16)
-        if comm:
-            pl.when(i > 1)(lambda: slab_copy(i - 2, ext).wait())
-            ext[3][rest(i, 2)] = r.reshape(*CHIPS[1:], 2, RB, d)
-            slab_copy(i, ext).start()
-        else:
-            outs[0][:] = r
-
-    def ship_out_body(i, ins, outs, ext):
-        for j in (2, 3):
-            slab_copy(j, ext).wait()
-        for u in range(no):
-            scat[0].ship(u)
 
     def macro_body(i, ins, outs, ext):
         (ht, dq, w), acc = ins, ext[0]
@@ -891,19 +888,18 @@
         o[:] = (dm[:] + dx).astype(BF16)
         put(gwo, i, lambda: gw)
 
-    firsts = ([], []) if comm else ([rows_of(b16(d, d), slab)], [cols_of(b16(d, nq), SUB)])
-    pf = [Phase(4, 2, [cols_of(attn, slab), whole(d_mid_bf)], firsts[0], gout_body),
-          Phase(nu, 3.9, [whole(h1t), heads_of(d_qkv, per), cols_of(fq, SUB)], firsts[1], macro_body),
+    first = [] if comm else [cols_of(b16(d, nq), SUB)]
+    pf = [Phase(nu, 3.9, [whole(h1t), heads_of(d_qkv, per), cols_of(fq, SUB)], first, macro_body),
           Phase(nm, 2, [rows_of(x, tm), rows_of(d_mid, tm), whole(lns)], [rows_of(act, tm), one_vec], ln1b_body)]
     if comm:
-        pf += [Phase(1, 0, [], [], ship_out_body, 4), Phase(nu, 0, [], [], ship_body, 5)]
-        scat.append(SmallSum(g_ln2, 4 + nu + nm, 1))
-    shared = [vm32(seq, d), vm16(2, *CHIPS, 2, RB, SUB), pltpu.SemaphoreType.DMA((4,)), vm16(2, *CHIPS[1:], 2, RB, d)]
-    got = host('last', pf, scat, shared=shared, fires=range(5, 5 + no + nu + 3 * LAG) if comm else None)
+        pf.append(Phase(nu, 0, [], [], ship_body, 1))
+        scat.append(SmallSum(g_ln2, nu + nm, 1))
+    shared = [vm32(seq, d), vm16(2, *CHIPS, 2, RB, SUB), pltpu.SemaphoreType.DMA((2,))]
+    got = host('last', pf, scat, shared=shared, fires=range(no + nu + 3 * LAG) if comm else None)
     if not comm:
-        g_out, g_qkv, dx, g_ln1 = got
+        g_qkv, dx, g_ln1 = got
         return y, dx, g_ln1, g_qkv, g_out, g_ln2, g_up, g_down
-    dx, _, up_b, g_out, g_qkv, _, _, sums = got
+    dx, _, up_b, g_out, g_qkv, _, sums = got
     down_a, (down_b, up_a) = r1[0], r2[:2]
     g_down = jnp.concatenate([down_a, down_b], axis=1).reshape(RB, -1, d).transpose(1, 0, 2).reshape(-1, d)
     return y, dx, sums, g_qkv, g_out, None, jnp.concatenate([up_a, up_b], axis=1), g_down

time: 594 us -> 590 us (level)
  no operation moved by 1% of the time
where the time goes in v11:
time: 590 us
  Pallas kernels  574 us (97%)
  local copies, waits for them, and re-layouts  10.8 us (2%)
    pallas_call x4, Pallas kernels, host(): pl.pallas_call(kernel, grid=(total,), in_specs=in_specs, out_specs=out_sp...  574 us

profile of v11, /device:TPU:0, one launch (start us, length us, event | category | flops | bytes accessed | tf_op | source)
XLA Modules:
  0.0 589.7 jit_solution(12276769790933550122)
XLA Ops:
  0.6 1.3 select_maximum_fusion.refs_8_
  1.9 260.8 %forward.1 = (bf16[1536,1024]{1,0:T(8,128)(2,1)}, bf16[36,1024,128]{2,1,0:T(8,128)(2,1)}, bf16[1024,1536]{1,0:T(8,128)(2,1)}, f32[12,1024,1]{2,1,0:T(8,128)}, bf...) custom-call(bf16[1024,1536]{1,0:T(8,128)(2,1)} %bitcast.45, ...), custom_call_target="tpu_custom_call" | custom-call | flops 17179869184 | bytes 33554432 | tf_op jit(solution)/shard_map/forward/pallas_call | solution.py:550
  262.7 101.1 %down.1 = (bf16[1024,6144]{1,0:T(8,128)(2,1)}, bf16[1536,6144]{1,0:T(8,128)(2,1)}, bf16[1024,1536]{1,0:T(8,128)(2,1)}, f32[48,4096]{1,0:T(8,128)}, bf16[2,2,4,2,...) custom-call(bf16[1024,1536]{1,0:T(8,128)(2,1)} %bitcast.32, bf16[6144,1536]{1,0:T(8,128)(2,1)} %bitcast.30, ...), custom_call_target="tpu_custom_call" | custom-call | flops 17179869184 | bytes 33554432 | tf_op jit(solution)/shard_map/down/pallas_call | solution.py:550
  363.8 106.0 %back.1 = (f32[1024,1536]{1,0:T(8,128)}, f32[1,1536]{1,0:T(1,128)}, bf16[3,12,1024,128]{3,2,1,0:T(8,128)(2,1)}, bf16[1536,1536]{1,0:T(8,128)(2,1)}, f32[48,2048]...) custom-call(bf16[1024,6144]{1,0:T(8,128)(2,1)} %get-tuple-element.49.ref, ...), custom_call_target="tpu_custom_call" | custom-call | flops 17179869184 | bytes 33554432 | tf_op jit(solution)/shard_map/back/pallas_call | solution.py:550
  469.8 106.3 %last.1 = (bf16[1024,1536]{1,0:T(8,128)(2,1)}, f32[1,1536]{1,0:T(1,128)}, f32[48,2048]{1,0:T(8,128)}, f32[48,1536]{1,0:T(8,128)}, f32[36,48,128]{2,1,0:T(8,128)}...) custom-call(bf16[1536,1024]{1,0:T(8,128)(2,1)} %get-tuple-element.48.refs_0_, ...), custom_call_target="tpu_custom_call" | custom-call | flops 17179869184 | bytes 33554432 | tf_op jit(solution)/shard_map/last/pallas_call | solution.py:550
  576.1 1.3 slice_bitcast_fusion
  577.4 2.8 pad_maximum_fusion
  580.2 0.8 reshape.66
  581.0 1.4 copy.17
  582.4 0.0 copy-start
  582.4 3.9 copy.22
  586.3 0.0 copy-done
  586.3 0.0 copy-start.1
  586.3 0.0 copy-start.2
  586.3 1.7 copy.23
  588.0 0.1 copy-done.1
  588.1 0.9 copy.24
  589.0 0.0 copy-done.2
  589.0 0.7 copy.25
Async XLA Ops:
  582.4 3.9 copy-start
  586.3 1.8 copy-start.1
  586.3 2.7 copy-start.2

commit v12 on v11

--- a/solution.py
+++ b/solution.py
@@ -607,30 +607,28 @@
         l_ref[rows] = m + jnp.log2(l)
 
 
-def attn_bwd(q_ref, k_ref, v_ref, a_ref, da_ref, l_ref, dq_ref, dk_ref, dv_ref, dk_s, dv_s, slope, scale, tq):
+def attn_bwd(q_ref, k_ref, v_ref, a_ref, da_ref, l_ref, dq_ref, dk_ref, dv_ref, dq_s, slope, scale, tq):
     slope2, scale2 = slope * LOG2E, scale * LOG2E
-    dk_s[:] = jnp.zeros_like(dk_s)
-    dv_s[:] = jnp.zeros_like(dv_s)
-    for i in range(q_ref.shape[0] // tq):
-        rows, before = pl.ds(i * tq, tq), pl.ds(0, i * tq)
-        q, da = q_ref[rows], da_ref[rows].astype(BF16)
-        lse = l_ref[rows]
-        delta = row_sum(da.astype(F32) * a_ref[rows].astype(F32))
-        near, far, keep = bias(i, tq, slope2)
-        dq = None
-        for keys, ahead in ((rows, near), (before, far))[:2 if i else 1]:
-            kk, vv = k_ref[keys], v_ref[keys]
-            p = jnp.exp2(dot_t(q, kk) * scale2 + ahead - lse)
-            if keys is rows:
-                p = jnp.where(keep, p, 0)
-            ds = (p * (dot_t(da, vv) - delta)).astype(BF16)
-            dv_s[keys] += t_dot(p.astype(BF16), da)
-            dk_s[keys] += t_dot(ds, q)
-            part = dot(ds, kk)
-            dq = part if dq is None else dq + part
-        dq_ref[rows] = (dq * scale).astype(BF16)
-    dk_ref[:] = (dk_s[:] * scale).astype(BF16)
-    dv_ref[:] = dv_s[:].astype(BF16)
+    seq = q_ref.shape[0]
+    da_all = da_ref[:].astype(BF16)
+    delta = row_sum(da_all.astype(F32) * a_ref[:].astype(F32))
+    near, _, keep = bias(0, tq, slope2)
+    for j in range(seq // tq):
+        keys, rows = pl.ds(j * tq, tq), pl.ds(j * tq, seq - j * tq)
+        kk, q, da = k_ref[keys], q_ref[rows], da_all[j * tq:]
+        l = jnp.concatenate([l_ref[pl.ds(i * tq, tq)] + slope2 * float((i - j) * tq) for i in range(j, seq // tq)], axis=0)
+        p = jnp.exp2(dot_t(q, kk) * scale2 + near - l)
+        own = jnp.where(keep, p[:tq], 0)
+        p = own if j == seq // tq - 1 else jnp.concatenate([own, p[tq:]], axis=0)
+        ds = (p * (dot_t(da, v_ref[keys]) - delta[j * tq:])).astype(BF16)
+        dv_ref[keys] = t_dot(p.astype(BF16), da).astype(BF16)
+        dk_ref[keys] = (t_dot(ds, q) * scale).astype(BF16)
+        part = dot(ds, kk)
+        if j:
+            dq_s[rows] += part
+        else:
+            dq_s[:] = part
+    dq_ref[:] = (dq_s[:] * scale).astype(BF16)
 
 
 def row_map(i):
@@ -835,14 +833,14 @@
         acc[:, pl.ds(pl.multiple_of(i * slab, slab), slab)] = dot_t(dmb[:], w[:])
 
     def battn_body(i, ins, outs, ext):
-        (qkv, a, l, sl), (o,), (acc, _, dk, dv) = ins, outs, ext
+        (qkv, a, l, sl), (o,), (acc, _, dq) = ins, outs, ext
 
         @pl.loop(0, pair)
         def _(j):
             h = i * pair + j
             own, here = (pl.ds(pl.multiple_of(n * hd, hd), hd) for n in (h, j))
             attn_bwd(*(qkv.at[n, j] for n in range(3)), a.at[:, here], acc.at[:, own], l.at[j], *(o.at[n, j] for n in range(3)),
-                     dk, dv, sl[h], scale, tq)
+                     dq, sl[h], scale, tq)
 
     def gout_body(i, ins, outs, ext):
         (a,), (o,), (_, dmb, *_) = ins, outs, ext
@@ -857,7 +855,7 @@
                 [triple(b16(3, heads, seq, hd))], battn_body),
           Phase(d // slab, 2, [cols_of(attn, slab)], [rows_of(b16(d, d), slab)], gout_body)]
     d_mid, g_ln2, d_qkv, g_out, *r2 = host('back', pe, S([(g_up, n_down)], [CARRY, n_down - CARRY], carry=r1[1:]),
-                                          shared=[vm32(seq, d), vm16(seq, d), vm32(seq, hd), vm32(seq, hd)])
+                                          shared=[vm32(seq, d), vm16(seq, d), vm32(seq, hd)])
     d_qkv = d_qkv.reshape(3 * heads, seq, hd)
 
     no = d // SUB

time: 590 us -> 584 us (0.990)
  Pallas kernels: 574 us -> 568 us
    pallas_call x4, Pallas kernels: 574 us -> 568 us  [host(): pl.pallas_call(kernel, grid=(total,), in_specs=in_specs, out_specs=out_sp...]
where the time goes in v12:
time: 584 us; the launch traced here: 583 us
  Pallas kernels  568 us (97%)
  local copies, waits for them, and re-layouts  10.8 us (2%)
    pallas_call x4, Pallas kernels, host(): pl.pallas_call(kernel, grid=(total,), in_specs=in_specs, out_specs=out_sp...  568 us

profile of v12, /device:TPU:0, one launch (start us, length us, event | category | flops | bytes accessed | tf_op | source)
XLA Modules:
  0.0 583.4 jit_solution(13825582627004168480)
XLA Ops:
  0.6 1.3 select_maximum_fusion.refs_8_
  1.9 260.8 %forward.1 = (bf16[1536,1024]{1,0:T(8,128)(2,1)}, bf16[36,1024,128]{2,1,0:T(8,128)(2,1)}, bf16[1024,1536]{1,0:T(8,128)(2,1)}, f32[12,1024,1]{2,1,0:T(8,128)}, bf...) custom-call(bf16[1024,1536]{1,0:T(8,128)(2,1)} %bitcast.45, ...), custom_call_target="tpu_custom_call" | custom-call | flops 17179869184 | bytes 33554432 | tf_op jit(solution)/shard_map/forward/pallas_call | solution.py:550
  262.7 101.1 %down.1 = (bf16[1024,6144]{1,0:T(8,128)(2,1)}, bf16[1536,6144]{1,0:T(8,128)(2,1)}, bf16[1024,1536]{1,0:T(8,128)(2,1)}, f32[48,4096]{1,0:T(8,128)}, bf16[2,2,4,2,...) custom-call(bf16[1024,1536]{1,0:T(8,128)(2,1)} %bitcast.32, bf16[6144,1536]{1,0:T(8,128)(2,1)} %bitcast.30, ...), custom_call_target="tpu_custom_call" | custom-call | flops 17179869184 | bytes 33554432 | tf_op jit(solution)/shard_map/down/pallas_call | solution.py:550
  363.8 99.7 %back.1 = (f32[1024,1536]{1,0:T(8,128)}, f32[1,1536]{1,0:T(1,128)}, bf16[3,12,1024,128]{3,2,1,0:T(8,128)(2,1)}, bf16[1536,1536]{1,0:T(8,128)(2,1)}, f32[48,2048]...) custom-call(bf16[1024,6144]{1,0:T(8,128)(2,1)} %get-tuple-element.49.ref, ...), custom_call_target="tpu_custom_call" | custom-call | flops 17179869184 | bytes 33554432 | tf_op jit(solution)/shard_map/back/pallas_call | solution.py:550
  463.5 106.3 %last.1 = (bf16[1024,1536]{1,0:T(8,128)(2,1)}, f32[1,1536]{1,0:T(1,128)}, f32[48,2048]{1,0:T(8,128)}, f32[48,1536]{1,0:T(8,128)}, f32[36,48,128]{2,1,0:T(8,128)}...) custom-call(bf16[1536,1024]{1,0:T(8,128)(2,1)} %get-tuple-element.48.refs_0_, ...), custom_call_target="tpu_custom_call" | custom-call | flops 17179869184 | bytes 33554432 | tf_op jit(solution)/shard_map/last/pallas_call | solution.py:550
  569.8 1.3 slice_bitcast_fusion
  571.1 2.8 pad_maximum_fusion
  573.9 0.8 reshape.66
  574.7 1.4 copy.17
  576.1 0.0 copy-start
  576.1 3.9 copy.22
  580.0 0.0 copy-done
  580.0 0.0 copy-start.1
  580.0 0.0 copy-start.2
  580.0 1.7 copy.23
  581.7 0.1 copy-done.1
  581.8 0.9 copy.24
  582.7 0.0 copy-done.2
  582.7 0.7 copy.25
Async XLA Ops:
  576.1 3.9 copy-start
  580.0 1.8 copy-start.1
  580.0 2.7 copy-start.2

commit v13 on v12

--- a/solution.py
+++ b/solution.py
@@ -406,16 +406,17 @@
 
 
 class SmallSum:
-    def __init__(self, rows, t0, at=None):
-        d = rows.shape[1]
+    def __init__(self, rows, d, t0, at=None):
         self.at, self.t0, self.k, self.tail = at, t0, 1, 0
-        self.ins = [(rows, pl.BlockSpec(memory_space=pltpu.VMEM))]
+        self.ins = [(row, pl.BlockSpec(memory_space=pltpu.VMEM)) for row in rows]
         self.outs = [(sds((8, d if at is None else 128), F32), pl.BlockSpec(memory_space=pltpu.VMEM))]
         self.alias = []
         self.scratch = [pltpu.VMEM((4, 8, d), F32), pltpu.VMEM((6, 8, d), F32), pltpu.SemaphoreType.DMA((6,)), pltpu.SemaphoreType.DMA((6,))]
 
     def run(self, t, outs):
-        rows, out, acc, got, ss, rs = self.refs
+        *rows, out, acc, got, ss, rs = self.refs
+        if self.at is not None:
+            rows.append(outs[self.at])
         me = coords()[0]
         zs, yp, xp, cp = peers()
         near = (cp, xp, yp, *zs)
@@ -426,12 +427,11 @@
             @pl.when(t == self.t0 + i)
             def _(i=i):
                 if not i:
+                    acc[i] = jnp.zeros_like(acc[i])
+                    for j, row in enumerate(rows):
+                        acc[i, pl.ds(j, 1), pl.ds(0, row.shape[1])] = row[:]
                     if self.at is None:
-                        acc[i] = pltpu.roll(rows[:], RB * me, 1)
-                    else:
-                        acc[i] = jnp.zeros_like(acc[i])
-                        acc[i, pl.ds(0, 1)] = rows[:]
-                        acc[i, pl.ds(self.at, 1)] = outs[self.at][:]
+                        acc[i] = pltpu.roll(acc[i], RB * me, 1)
                 elif i <= n:
                     copies[i - 1].wait_recv()
                     acc[i] = acc[i - 1] + got[i - 1]
@@ -696,7 +696,7 @@
     if comm:
         half = (ds - us) // 2
         gather = Gather([(wq, None, qs, WIDE), (wo, None, os, WIDE), (wu, None, us, d), (wd, None, us + half, d)], qs, ds + 2 * GLAG)
-        lnsum = SmallSum(lns, 0)
+        lnsum = SmallSum(lns, d, 0)
     held = {}
 
     def load(u, ext):
@@ -713,7 +713,7 @@
         return ext[3][rest(u, 2)].reshape(d, WIDE)
 
     def gain(row):
-        return (lnsum.refs[1] if comm else held['lns'])[pl.ds(row, 1)]
+        return (lnsum.refs[len(lnsum.ins)] if comm else held['lns'])[pl.ds(row, 1)]
 
     def start_body(i, ins, outs, ext):
         load((qs, qs), ext).start()
@@ -886,21 +886,31 @@
         o[:] = (dm[:] + dx).astype(BF16)
         put(gwo, i, lambda: gw)
 
+    def join_body(i, ins, outs, ext):
+        (low, high, up), (down_o, up_o) = ins, outs
+        wide = up.shape[1]
+        up_o[:, :wide] = up[:]
+        up_o[:, wide:] = scat[0].refs[len(scat[0].ins)][:]
+        for u in range(n_down):
+            part, v = (low, u) if u * SUB < wide else (high, u - wide // SUB)
+            down_o[pl.ds(u // no * RB, RB), pl.ds(u % no * SUB, SUB)] = part[:, pl.ds(v * SUB, SUB)]
+
     first = [] if comm else [cols_of(b16(d, nq), SUB)]
     pf = [Phase(nu, 3.9, [whole(h1t), heads_of(d_qkv, per), cols_of(fq, SUB)], first, macro_body),
           Phase(nm, 2, [rows_of(x, tm), rows_of(d_mid, tm), whole(lns)], [rows_of(act, tm), one_vec], ln1b_body)]
     if comm:
+        pieces = r1[0], *r2[:2]
         pf.append(Phase(nu, 0, [], [], ship_body, 1))
-        scat.append(SmallSum(g_ln2, nu + nm, 1))
+        pf.append(Phase(1, 0, [(p, pltpu.VMEM, None) for p in pieces], [(o, o.shape, lambda i: (0, 0)) for o in (f32(ff // 32, d), f32(RB, ff))],
+                        join_body, nu + nm))
+        scat.append(SmallSum([g_ln2], d, nu + nm, 1))
     shared = [vm32(seq, d), vm16(2, *CHIPS, 2, RB, SUB), pltpu.SemaphoreType.DMA((2,))]
     got = host('last', pf, scat, shared=shared, fires=range(no + nu + 3 * LAG) if comm else None)
     if not comm:
         g_qkv, dx, g_ln1 = got
         return y, dx, g_ln1, g_qkv, g_out, g_ln2, g_up, g_down
-    dx, _, up_b, g_out, g_qkv, _, sums = got
-    down_a, (down_b, up_a) = r1[0], r2[:2]
-    g_down = jnp.concatenate([down_a, down_b], axis=1).reshape(RB, -1, d).transpose(1, 0, 2).reshape(-1, d)
-    return y, dx, sums, g_qkv, g_out, None, jnp.concatenate([up_a, up_b], axis=1), g_down
+    dx, _, g_down, g_up, _, g_out, g_qkv, _, sums = got
+    return y, dx, sums, g_qkv, g_out, g_up, g_down
 
 
 def solution(mesh):
@@ -909,9 +919,9 @@
     def step(x_in, ln1_w, w_qkv, w_out, ln2_w, w_up, w_down, dy_out):
         rows, _, heads, hd = w_qkv.shape
         d = x_in.shape[-1]
-        lns = jnp.pad(jnp.stack([ln1_w, ln2_w]), ((0, 6), (0, d - rows)))
+        lns = [w.reshape(1, rows) for w in (ln1_w, ln2_w)]
         wq = w_qkv.transpose(1, 2, 0, 3).reshape(-1, rows, hd)
-        y, dx, sums, g_qkv, g_out, _, g_up, g_down = local_step(x_in[0], lns, wq, w_out, w_up, w_down, dy_out[0])
+        y, dx, sums, g_qkv, g_out, g_up, g_down = local_step(x_in[0], lns, wq, w_out, w_up, w_down, dy_out[0])
         g_qkv = g_qkv.reshape(3, heads, rows, hd).transpose(2, 0, 1, 3)
         return y[None], dx[None], sums[1, :rows], g_qkv, g_out, sums[0, :rows], g_up, g_down
 

time: 584 us -> 581 us (level)
  no operation moved by 1% of the time
where the time goes in v13:
time: 581 us; the launch traced here: 580 us
  Pallas kernels  569 us (98%)
  local copies, waits for them, and re-layouts  10.5 us (2%)
    pallas_call x4, Pallas kernels, host(): pl.pallas_call(kernel, grid=(total,), in_specs=in_specs, out_specs=out_sp...  569 us

profile of v13, /device:TPU:0, one launch (start us, length us, event | category | flops | bytes accessed | tf_op | source)
XLA Modules:
  0.0 580.3 jit_solution(1884387120651587320)
XLA Ops:
  0.6 260.7 %forward.1 = (bf16[1536,1024]{1,0:T(8,128)(2,1)}, bf16[36,1024,128]{2,1,0:T(8,128)(2,1)}, bf16[1024,1536]{1,0:T(8,128)(2,1)}, f32[12,1024,1]{2,1,0:T(8,128)}, bf...) custom-call(bf16[1024,1536]{1,0:T(8,128)(2,1)} %bitcast.39, ...), custom_call_target="tpu_custom_call" | custom-call | flops 17179869184 | bytes 33554432 | tf_op jit(solution)/shard_map/forward/pallas_call | solution.py:550
  261.4 101.0 %down.1 = (bf16[1024,6144]{1,0:T(8,128)(2,1)}, bf16[1536,6144]{1,0:T(8,128)(2,1)}, bf16[1024,1536]{1,0:T(8,128)(2,1)}, f32[48,4096]{1,0:T(8,128)}, bf16[2,2,4,2,...) custom-call(bf16[1024,1536]{1,0:T(8,128)(2,1)} %bitcast.30, bf16[6144,1536]{1,0:T(8,128)(2,1)} %bitcast.28, ...), custom_call_target="tpu_custom_call" | custom-call | flops 17179869184 | bytes 33554432 | tf_op jit(solution)/shard_map/down/pallas_call | solution.py:550
  362.4 99.7 %back.1 = (f32[1024,1536]{1,0:T(8,128)}, f32[1,1536]{1,0:T(1,128)}, bf16[3,12,1024,128]{3,2,1,0:T(8,128)(2,1)}, bf16[1536,1536]{1,0:T(8,128)(2,1)}, f32[48,2048]...) custom-call(bf16[1024,6144]{1,0:T(8,128)(2,1)} %get-tuple-element.50.ref, ...), custom_call_target="tpu_custom_call" | custom-call | flops 17179869184 | bytes 33554432 | tf_op jit(solution)/shard_map/back/pallas_call | solution.py:550
  462.1 107.6 %last.1 = (bf16[1024,1536]{1,0:T(8,128)(2,1)}, f32[1,1536]{1,0:T(1,128)}, f32[192,1536]{1,0:T(8,128)}, f32[48,6144]{1,0:T(8,128)}, f32[48,2048]{1,0:T(8,128)}, /...) custom-call(bf16[1536,1024]{1,0:T(8,128)(2,1)} %get-tuple-element.49.re, ...), custom_call_target="tpu_custom_call" | custom-call | flops 17179869184 | bytes 33554432 | tf_op jit(solution)/shard_map/last/pallas_call | solution.py:550
  569.8 0.0 copy-start
  569.8 1.3 slice_bitcast_fusion
  571.1 3.8 copy.23
  574.9 0.0 copy-done
  574.9 0.0 copy-start.3
  574.9 0.0 copy-start.4
  574.9 0.0 copy-start.2
  574.9 0.0 copy-start.1
  574.9 1.7 copy.24
  576.6 0.0 copy-done.3
  576.6 0.9 copy.25
  577.5 0.0 copy-done.4
  577.5 0.7 copy.26
  578.2 0.0 copy-done.2
  578.2 1.0 copy.27
  579.3 0.0 copy-done.1
  579.3 1.0 copy.28
Async XLA Ops:
  569.8 5.1 copy-start
  574.9 1.7 copy-start.3
  574.9 2.6 copy-start.4
  574.9 3.4 copy-start.2
  574.9 4.4 copy-start.1

commit v14 on v13

--- a/solution.py
+++ b/solution.py
@@ -17,6 +17,7 @@
 GLAG = 1
 CARRY = 2 * LAG
 LEAD = 3
+FRONT = 0.92
 SIDE = -4
 RB = 48
 F32, BF16 = jnp.float32, jnp.bfloat16
@@ -464,7 +465,7 @@
         for t in range(at):
             clock.append(clock[-1] + sum(p.cost for p in phases if p.at <= t < p.at + p.n))
         for k in range(1, k_all):
-            t = at if k >= spread else min(t for t in range(at + 1) if clock[t] * spread >= clock[at] * k)
+            t = at if k >= spread else min(t for t in range(at + 1) if clock[t] * spread >= FRONT * clock[at] * k)
             fires.append(max(t, fires[-1] + 1))
     total = max([at, fires[-1] + 1] + [c.t0 + 5 for c in small])
     ins, in_specs, outs, out_specs, scratch, alias, resident = [], [], [], [], [], {}, []

time: 581 us -> 571 us (0.983)
  Pallas kernels: 569 us -> 559 us
    pallas_call x4, Pallas kernels: 569 us -> 559 us  [host(): pl.pallas_call(kernel, grid=(total,), in_specs=in_specs, out_specs=out_sp...]
where the time goes in v14:
time: 571 us; the launch traced here: 570 us
  Pallas kernels  559 us (98%)
  local copies, waits for them, and re-layouts  10.5 us (2%)
    pallas_call x4, Pallas kernels, host(): pl.pallas_call(kernel, grid=(total,), in_specs=in_specs, out_specs=out_sp...  559 us

profile of v14, /device:TPU:0, one launch (start us, length us, event | category | flops | bytes accessed | tf_op | source)
XLA Modules:
  0.0 570.4 jit_solution(4266265287509523412)
XLA Ops:
  0.6 260.7 %forward.1 = (bf16[1536,1024]{1,0:T(8,128)(2,1)}, bf16[36,1024,128]{2,1,0:T(8,128)(2,1)}, bf16[1024,1536]{1,0:T(8,128)(2,1)}, f32[12,1024,1]{2,1,0:T(8,128)}, bf...) custom-call(bf16[1024,1536]{1,0:T(8,128)(2,1)} %bitcast.39, ...), custom_call_target="tpu_custom_call" | custom-call | flops 17179869184 | bytes 33554432 | tf_op jit(solution)/shard_map/forward/pallas_call | solution.py:551
  261.4 95.6 %down.1 = (bf16[1024,6144]{1,0:T(8,128)(2,1)}, bf16[1536,6144]{1,0:T(8,128)(2,1)}, bf16[1024,1536]{1,0:T(8,128)(2,1)}, f32[48,4096]{1,0:T(8,128)}, bf16[2,2,4,2,...) custom-call(bf16[1024,1536]{1,0:T(8,128)(2,1)} %bitcast.30, bf16[6144,1536]{1,0:T(8,128)(2,1)} %bitcast.28, ...), custom_call_target="tpu_custom_call" | custom-call | flops 17179869184 | bytes 33554432 | tf_op jit(solution)/shard_map/down/pallas_call | solution.py:551
  356.9 95.3 %back.1 = (f32[1024,1536]{1,0:T(8,128)}, f32[1,1536]{1,0:T(1,128)}, bf16[3,12,1024,128]{3,2,1,0:T(8,128)(2,1)}, bf16[1536,1536]{1,0:T(8,128)(2,1)}, f32[48,2048]...) custom-call(bf16[1024,6144]{1,0:T(8,128)(2,1)} %get-tuple-element.50.ref, ...), custom_call_target="tpu_custom_call" | custom-call | flops 17179869184 | bytes 33554432 | tf_op jit(solution)/shard_map/back/pallas_call | solution.py:551
  452.2 107.7 %last.1 = (bf16[1024,1536]{1,0:T(8,128)(2,1)}, f32[1,1536]{1,0:T(1,128)}, f32[192,1536]{1,0:T(8,128)}, f32[48,6144]{1,0:T(8,128)}, f32[48,2048]{1,0:T(8,128)}, /...) custom-call(bf16[1536,1024]{1,0:T(8,128)(2,1)} %get-tuple-element.49.re, ...), custom_call_target="tpu_custom_call" | custom-call | flops 17179869184 | bytes 33554432 | tf_op jit(solution)/shard_map/last/pallas_call | solution.py:551
  559.9 0.0 copy-start
  559.9 1.3 slice_bitcast_fusion
  561.3 3.8 copy.23
  565.0 0.0 copy-done
  565.0 0.0 copy-start.3
  565.0 0.0 copy-start.4
  565.0 0.0 copy-start.2
  565.0 0.0 copy-start.1
  565.0 1.7 copy.24
  566.7 0.0 copy-done.3
  566.8 0.9 copy.25
  567.7 0.0 copy-done.4
  567.7 0.7 copy.26
  568.4 0.0 copy-done.2
  568.4 1.0 copy.27
  569.4 0.0 copy-done.1
  569.4 1.0 copy.28
Async XLA Ops:
  559.9 5.1 copy-start
  565.0 1.7 copy-start.3
  565.0 2.6 copy-start.4
  565.0 3.4 copy-start.2
  565.0 4.4 copy-start.1
